TPU v7x, 32 devices: a whole 2x2x4 slice. The times are simulated.
32 devices in a mesh: param: 8 (over z, y), sensor: 4 (over x, core).
Axes of the slice: x: 2, y: 2, z: 4, core: 2. Of those that a mesh axis runs over, the one named last changes fastest.
Arguments:
- blocks: bfloat16 [64, 2, 600, 1024], P(None, None, 'sensor', 'param'), may hold values from -0.1875 to 0.1875
- probes: bfloat16 [64, 2, 4, 1024], P(None, None, None, 'param'), may hold values from -6 to 6
Outputs:
- basis: float32 [64, 2, 4, 600], P(None, None, None, 'sensor')
- coeffs: bfloat16 [64, 2, 4, 1024], P('sensor', None, None, 'param')
All inputs are finite; a program needn't handle non-finite values.
Results may differ from a plain program's by a relative error of at most 0.0049.
Values sent between devices are 32-bit elements; how exact they have to be, the bound alone decides.
No kernel may reach another device: no remote copies, remote signals or barrier semaphores. Data moves between devices by JAX's collectives and lax.ppermute only.
A program may use at most 64 MiB of HBM per device.

v0:
```python
import jax
import jax.numpy as jnp
from jax import lax
from jax.sharding import PartitionSpec as P

SENSORS = 600
FREQ_LINES = 64


def local_gram(values):
    return jnp.einsum("fas,fbs->ab", values, values, precision=lax.Precision.HIGHEST) / (
        2.0 * FREQ_LINES * SENSORS
    )


def inverse_factor(gram):
    lower = jnp.linalg.cholesky(gram)
    return lax.linalg.triangular_solve(
        lower, jnp.eye(gram.shape[0], dtype=gram.dtype), left_side=True, lower=True
    )


def on_device(blocks, probes):
    block_real = blocks[:, 0]
    block_imag = blocks[:, 1]
    probe_real = probes[:, 0]
    probe_imag = probes[:, 1]
    lines = blocks.shape[0]
    group = blocks.shape[2]
    count = probes.shape[2]
    real_part = jnp.einsum(
        "fsn,fan->fas", block_real, probe_real, preferred_element_type=jnp.float32
    ) - jnp.einsum("fsn,fan->fas", block_imag, probe_imag, preferred_element_type=jnp.float32)
    imag_part = jnp.einsum(
        "fsn,fan->fas", block_real, probe_imag, preferred_element_type=jnp.float32
    ) + jnp.einsum("fsn,fan->fas", block_imag, probe_real, preferred_element_type=jnp.float32)
    partial_sketch = jnp.stack([real_part, imag_part], axis=1).reshape(2 * lines, count, group)
    sketch = lax.psum(partial_sketch, "param")
    gram = lax.psum(local_gram(sketch), "sensor")
    inverse = inverse_factor(gram)
    flat_basis = jnp.einsum("ab,fbs->fas", inverse, sketch, precision=lax.Precision.HIGHEST)
    basis = flat_basis.reshape(lines, 2, count, group)
    rounded = basis.astype(jnp.bfloat16)
    vector_real = rounded[:, 0]
    vector_imag = rounded[:, 1]
    adjoint_real = jnp.einsum(
        "fsn,fas->fan", block_real, vector_real, preferred_element_type=jnp.float32
    ) + jnp.einsum("fsn,fas->fan", block_imag, vector_imag, preferred_element_type=jnp.float32)
    adjoint_imag = jnp.einsum(
        "fsn,fas->fan", block_real, vector_imag, preferred_element_type=jnp.float32
    ) - jnp.einsum("fsn,fas->fan", block_imag, vector_real, preferred_element_type=jnp.float32)
    terms = jnp.stack([adjoint_real, adjoint_imag], axis=1)
    coeffs = lax.psum_scatter(terms, "sensor", scatter_dimension=0, tiled=True).astype(jnp.bfloat16)
    return (basis, coeffs)


def solution(mesh):
    placed = (P(None, None, "sensor", "param"), P(None, None, None, "param"))
    return jax.shard_map(
        on_device,
        mesh=mesh,
        in_specs=placed,
        out_specs=(P(None, None, None, "sensor"), P("sensor", None, None, "param")),
        check_vma=False,
    )
```

profile of v0, /device:TPU:0, one launch (start us, length us, event | category | flops | bytes accessed | tf_op | source)
XLA Modules:
  0.0 145.6 jit_solution(4940544736051843440)
XLA Ops:
  7.2 10.0 %fusion.20 = (bf16[64,1,150,128]{3,1,2,0:T(2,128)(2,1)S(1)}, bf16[64,1,150,128]{3,1,2,0:T(2,128)(2,1)S(1)}) fusion(bf16[64,2,150,128]{3,1,2,0:T(2,128)(2,1)} %param.2), kind=kLoop, calls=%fused_computation.41 | loop fusion | bytes 9830400 | tf_op jit(solution)/shard_map/slice | solution.py:25
  17.3 0.7 copy_bitcast_fusion
  18.2 1.4 fusion.7
  19.5 1.4 fusion.11
  20.9 1.4 fusion
  22.3 1.4 fusion.1
  23.9 1.0 copy.31
  25.0 74.1 %all-reduce.2.cloned.1.call-done = f32[128,4,150]{0,1,2:T(4,128)} async-done(((f32[128,4,150]{0,1,2:T(4,128)}), f32[128,4,150]{0,1,2:T(4,128)}) %all-reduce.2.cloned.1.call-update) | async-done | bytes 307216 | tf_op jit(solution)/shard_map/psum | solution.py:38
  99.1 2.5 %fusion.4 = f32[4,4]{0,1:T(4,128)S(1)} fusion(f32[128,4,150]{0,1,2:T(4,128)} %all-reduce.2.cloned.1.call-done), kind=kOutput, calls=%fused_computation.12 | convolution fusion | flops 3686416 | bytes 307264 | tf_op jit(solution)/shard_map/fas,fbs->ab/dot_general | solution.py:11
  101.6 5.6 %psum.15 = f32[4,4]{0,1:T(4,128)S(1)} all-reduce(f32[4,4]{0,1:T(4,128)S(1)} %fusion.4), channel_id=1, replica_groups=mesh['param'=8,'sensor'=4] {'sensor'}, use_global_device_ids=true, to_apply=%region_1.0 | all-reduce | flops 16 | bytes 128 | tf_op jit(solution)/shard_map/psum | solution.py:39
  107.3 0.4 cholesky.17
  107.7 0.6 compare_reduce_fusion
  108.4 0.6 fusion.17
  109.0 0.3 custom-call.6
  109.6 1.6 %convolution_bitcast_fusion = f32[128,4,150]{0,1,2:T(4,128)S(1)} fusion(f32[128,4,150]{0,1,2:T(4,128)} %all-reduce.2.cloned.1.call-done, f32[4,4,1]{1,0,2:T(4,128)S(1)} %convolution_bitcast_fusion.2), kind=kOutput, calls=%fused_computation.2 | convolution fusion | flops 3686400 | bytes 614464 | tf_op jit(solution)/shard_map/ab,fbs->fas/dot_general | solution.py:41
  111.2 0.3 copy.35
  111.6 2.7 %fusion.6 = f32[64,4,128]{2,1,0:T(4,128)S(1)} fusion(bf16[64,150,128]{2,1,0:T(8,128)(2,1)} %copy-done, bf16[64,2,4,150]{3,2,0,1:T(4,128)(2,1)S(1)} %copy.50), kind=kOutput, calls=%fused_computation.20 | convolution fusion | flops 9830400 | bytes 2719744 | tf_op jit(solution)/shard_map/fsn,fas->fan/dot_general | solution.py:49
  114.3 0.8 fusion.5
  115.1 0.8 fusion.3
  115.9 0.8 fusion.2
  116.8 0.8 reshape.23
  117.6 19.7 %reduce-scatter.5.cloned.1.call-done = f32[16,1024]{1,0:T(8,128)} async-done(((f32[64,1024]{1,0:T(8,128)}), f32[16,1024]{1,0:T(8,128)}) %reduce-scatter.5.cloned.1.call-update) | async-done | bytes 65552
  137.3 0.9 reshape.24
  138.2 0.6 copy.37
  (22 shorter events, 1.1 us)
Async XLA Ops:
  7.2 91.9 %all-reduce.2.cloned.1.call-start = ((), (), s32[]{:S(2)}) async-start(), calls=%async_computation.1 | async-start | bytes 614400 | tf_op jit(solution)/shard_map/psum | solution.py:38
  17.3 0.9 copy-start.3
  17.9 3.0 %copy-start = (bf16[64,150,128]{2,1,0:T(8,128)(2,1)}, bf16[64,150,128]{2,1,0:T(8,128)(2,1)S(1)}, u32[]{:S(2)}) copy-start(bf16[64,150,128]{2,1,0:T(8,128)(2,1)S(1)} %get-tuple-element.11) | copy-start | bytes 7372804
  24.9 112.4 %reduce-scatter.5.cloned.1.call-start = ((), (), s32[]{:S(2)}) async-start(), calls=%async_computation.2 | async-start | bytes 327680
  111.5 3.6 %copy-start.2 = (f32[128,4,150]{2,1,0:T(4,128)}, f32[128,4,150]{2,1,0:T(4,128)S(1)}, u32[]{:S(2)}) copy-start(f32[128,4,150]{2,1,0:T(4,128)S(1)} %copy.35) | copy-start | bytes 921604
  111.5 2.8 %copy-start.1 = (bf16[64,150,128]{2,1,0:T(8,128)(2,1)S(1)}, bf16[64,150,128]{2,1,0:T(8,128)(2,1)}, u32[]{:S(2)}) copy-start(bf16[64,150,128]{2,1,0:T(8,128)(2,1)} %copy-done) | copy-start | bytes 7372804
Sparse Core Ops, SparseCore 0:
  25.0 74.0 all-reduce.1
  117.7 19.5 reduce-scatter.4
where the time goes:
time: 146 us
  waiting for transfers between devices  93.8 us (64%)
  matrix products  15 us (10%)
  local copies, waits for them, and re-layouts  14.7 us (10%)
  between operations  14.2 us (10%)
  blocking collectives  5.65 us (4%)
  other arithmetic  2.23 us (2%)
    psum x1, waiting for transfers between devices, on_device(): sketch = lax.psum(partial_sketch, 'param')  74.1 us
    unnamed x3, waiting for transfers between devices  19.7 us
    slice x1, local copies, waits for them, and re-layouts, on_device(): block_imag = blocks[:, 1]  10 us
    psum x1, blocking collectives, on_device(): gram = lax.psum(local_gram(sketch), 'sensor')  5.65 us
  transfers between devices with their start and end apart: 2, of which 2 were waited for; matrix products, arithmetic and copies ran while one was open for 0% of the time, Pallas kernels for 0%

commit v1 on v0

v1 whole, which is shorter than its diff:
```python
import functools

import jax
import jax.numpy as jnp
from jax import lax
from jax.experimental import pallas as pl
from jax.experimental.pallas import tpu as pltpu
from jax.sharding import PartitionSpec as P

LANES = 128
STEP = 2 * LANES
QUAD = 4
PROBES = 4
SPLITS = 3


def roll(x, shift, axis):
    return pltpu.roll(x, shift % x.shape[axis], axis)


def row_of(shape=(8, LANES)):
    return lax.broadcasted_iota(jnp.int32, shape, 0)


def lane_of(shape=(8, LANES)):
    return lax.broadcasted_iota(jnp.int32, shape, 1)


class Plan:
    def __init__(self, lines, parts, group, nodes, shards):
        self.lines, self.parts, self.group, self.nodes = lines, parts, group, nodes
        self.per_line = parts * group
        self.rows = lines * self.per_line
        self.steps = self.rows // STEP
        self.quarter = -(-self.steps // QUAD)
        self.shards = shards
        self.shard_lines = lines // shards
        self.total = parts * lines * group * shards
        assert parts == 2 and nodes == LANES and self.rows % STEP == 0 and self.per_line >= STEP
        assert lines % shards == 0 and self.steps > (QUAD - 1) * self.quarter


def first_line(plan, step):
    return (step * STEP) // plan.per_line


def sketch_kernel(plan, me_ref, blocks_ref, probes_ref, *rest):
    outs, kept_ref, lhs_ref, sems = rest[:QUAD], rest[QUAD], rest[QUAD + 1], rest[QUAD + 2]
    me = me_ref[0]
    main = plan.quarter - 1
    order = [k for k in range(1, QUAD)] + [0]

    def copies(k):
        first = (me ^ k) * plan.quarter
        tail = jnp.minimum(first + main, plan.steps - 1)
        return (
            pltpu.make_async_copy(
                blocks_ref.at[pl.ds(pl.multiple_of(first * STEP, STEP), main * STEP)],
                kept_ref.at[k, pl.ds(0, main * STEP)],
                sems.at[k, 0],
            ),
            pltpu.make_async_copy(
                blocks_ref.at[pl.ds(pl.multiple_of(tail * STEP, STEP), STEP)],
                kept_ref.at[k, pl.ds(main * STEP, STEP)],
                sems.at[k, 1],
            ),
        )

    for k in order:
        for copy in copies(k):
            copy.start()
    held = plan.lines * 2 * PROBES
    lhs_ref[pl.ds(0, held)] = probes_ref[...].astype(jnp.float32)
    lhs_ref[pl.ds(held, 8)] = jnp.zeros((8, LANES), jnp.float32)
    low = row_of() < 4
    even = lane_of() % 2 == 0
    column = lane_of((8, STEP))
    for k in order:
        for copy in copies(k):
            copy.wait()
        first = (me ^ k) * plan.quarter

        def body(t, _, k=k, first=first):
            step = first + t
            line = first_line(plan, jnp.minimum(step, plan.steps - 1))
            probe = lhs_ref[pl.ds(pl.multiple_of(line * 8, 8), 16)].astype(jnp.bfloat16)
            block = kept_ref[k, pl.ds(pl.multiple_of(t * STEP, STEP), STEP)]
            both = lax.dot_general(probe, block, (((1,), (1,)), ((), ())), preferred_element_type=jnp.float32)
            place = column + step * STEP
            own = jnp.where(place < (line + 1) * plan.per_line, both[:8], both[8:])
            own = jnp.where(place < plan.rows, own, 0.0)
            left, right = own[:, :LANES], own[:, LANES:]
            direct = jnp.where(low, left, roll(right, 4, 0))
            crossed = jnp.where(low, roll(left, 4, 0), right)
            outs[k][t] = direct + jnp.where(even, -roll(crossed, -1, 1), roll(crossed, 1, 1))
            return 0

        lax.fori_loop(0, plan.quarter, body, 0, unroll=True)


def sketch_terms(plan, me, blocks, probes):
    piece = jax.ShapeDtypeStruct((plan.quarter, 8, LANES), jnp.float32)
    kept = jax.ShapeDtypeStruct((QUAD, plan.quarter * STEP, LANES), jnp.bfloat16)
    vmem = pl.BlockSpec(memory_space=pltpu.VMEM)
    out = pl.pallas_call(
        functools.partial(sketch_kernel, plan),
        out_shape=[piece] * QUAD + [kept],
        in_specs=[pl.BlockSpec(memory_space=pltpu.SMEM), pl.BlockSpec(memory_space=pl.ANY), vmem],
        out_specs=[vmem] * (QUAD + 1),
        scratch_shapes=[
            pltpu.VMEM((plan.lines * 8 + 8, LANES), jnp.float32),
            pltpu.SemaphoreType.DMA((QUAD, 2)),
        ],
        name="sketch_terms",
    )(me, blocks, probes)
    return out[:QUAD], out[QUAD]


def gram_kernel(plan, *refs):
    ins, out_ref = refs[:-1], refs[-1]
    row = row_of()
    lane = lane_of()
    sums = [jnp.zeros((8, LANES), jnp.float32) for _ in range(3)]
    for t in range(plan.quarter):
        x = ins[0][t]
        for other in ins[1:]:
            x = x + other[t]
        out_ref[t] = x
        for d in range(3):
            y = x if d == 0 else jnp.where(row % 4 + d < 4, roll(x, -d, 0), roll(x, 4 - d, 0))
            sums[d] = sums[d] + x * y
    packed = jnp.zeros((8, LANES), jnp.float32)
    for d in range(3):
        packed = jnp.where(lane == d, jnp.sum(sums[d], axis=1, keepdims=True), packed)
    out_ref[plan.quarter] = packed


def add_with_gram(plan, *pieces):
    vmem = pl.BlockSpec(memory_space=pltpu.VMEM)
    return pl.pallas_call(
        functools.partial(gram_kernel, plan),
        out_shape=jax.ShapeDtypeStruct((plan.quarter + 1, 8, LANES), jnp.float32),
        in_specs=[vmem] * len(pieces),
        out_specs=vmem,
        name="add_with_gram",
    )(*pieces)


def adjoint_kernel(plan, me_ref, spot_ref, kept_ref, *rest):
    ins, outs, acc_ref = rest[:QUAD], rest[QUAD : QUAD + plan.shards], rest[QUAD + plan.shards]
    me = me_ref[0]
    spot = spot_ref[0]
    low = row_of() < 4
    even = lane_of() % 2 == 0
    column = lane_of((8, STEP))
    acc_ref[...] = jnp.zeros(acc_ref.shape, jnp.float32)
    for k in range(QUAD):
        first = (me ^ k) * plan.quarter

        def body(t, _, k=k, first=first):
            step = jnp.minimum(first + t, plan.steps - 1)
            line = first_line(plan, step)
            x = ins[k][t]
            y = jnp.where(even, roll(x, -1, 1), -roll(x, 1, 1))
            left = jnp.where(low, x, roll(y, 4, 0))
            right = jnp.where(low, roll(x, 4, 0), y)
            value = jnp.concatenate([left, right], axis=1)
            mine = column + step * STEP < (line + 1) * plan.per_line
            terms = []
            for _ in range(SPLITS):
                term = value.astype(jnp.bfloat16).astype(jnp.float32)
                terms.append(jnp.where(mine, term, 0.0))
                terms.append(jnp.where(mine, 0.0, term))
                value = value - term
            lhs = jnp.concatenate(terms, axis=0).astype(jnp.bfloat16)
            block = kept_ref[k, pl.ds(pl.multiple_of(t * STEP, STEP), STEP)]
            got = jnp.dot(lhs, block, preferred_element_type=jnp.float32)
            here = sum(got[16 * i : 16 * i + 8] for i in range(SPLITS))
            after = sum(got[16 * i + 8 : 16 * i + 16] for i in range(SPLITS))
            acc_ref[line] = acc_ref[line] + here
            acc_ref[line + 1] = acc_ref[line + 1] + after
            return 0

        lax.fori_loop(0, plan.quarter, body, 0, unroll=True)
    packed = sum(ref[plan.quarter] for ref in ins)
    for k in range(plan.shards):
        start = (spot ^ k) * plan.shard_lines
        outs[k][pl.ds(0, plan.shard_lines)] = acc_ref[pl.ds(start, plan.shard_lines)]
        outs[k][plan.shard_lines] = packed


def adjoint_terms(plan, me, spot, kept, pieces):
    vmem = pl.BlockSpec(memory_space=pltpu.VMEM)
    smem = pl.BlockSpec(memory_space=pltpu.SMEM)
    return pl.pallas_call(
        functools.partial(adjoint_kernel, plan),
        out_shape=[jax.ShapeDtypeStruct((plan.shard_lines + 1, 8, LANES), jnp.float32)] * plan.shards,
        in_specs=[smem, smem] + [vmem] * (1 + QUAD),
        out_specs=[vmem] * plan.shards,
        scratch_shapes=[pltpu.VMEM((plan.lines + 1, 8, LANES), jnp.float32)],
        name="adjoint_terms",
    )(me, spot, kept, *pieces)


def by_line_kernel(plan, me_ref, *rest):
    ins, out_ref, flat_ref = rest[:QUAD], rest[QUAD], rest[QUAD + 1]
    me = me_ref[0]
    lane = lane_of()
    half = LANES // 2
    stay = (row_of() < 4) == (lane < half)
    source = jnp.where(lane < half, 2 * lane, 2 * lane - (LANES - 1))
    for k in range(QUAD):
        first = (me ^ k) * plan.quarter
        for t in range(plan.quarter):
            split = jnp.take_along_axis(ins[k][t], source, axis=1)
            flat_ref[first + t] = jnp.where(stay, split, roll(roll(split, 4, 0), half, 1))
    tiles = -(-plan.group // LANES)
    for line in range(plan.lines):
        tile, shift = divmod(line * plan.group, LANES)
        turned = [roll(flat_ref[tile + i], -shift, 1) for i in range(tiles + 1)]
        for i in range(tiles):
            width = min(LANES, plan.group - i * LANES)
            part = jnp.where(lane < LANES - shift, turned[i], turned[i + 1])
            out_ref[line, :, pl.ds(i * LANES, width)] = part[:, :width]


def sketch_by_line(plan, me, pieces):
    vmem = pl.BlockSpec(memory_space=pltpu.VMEM)
    return pl.pallas_call(
        functools.partial(by_line_kernel, plan),
        out_shape=jax.ShapeDtypeStruct((plan.lines, 8, plan.group), jnp.float32),
        in_specs=[pl.BlockSpec(memory_space=pltpu.SMEM)] + [vmem] * QUAD,
        out_specs=vmem,
        scratch_shapes=[pltpu.VMEM((QUAD * plan.quarter + 2, 8, LANES), jnp.float32)],
        name="sketch_by_line",
    )(me, *pieces)


def inverse_rows(plan, packed):
    row = row_of()
    lane = lane_of()
    packed = packed + roll(packed, 4, 0)
    entry = {}
    for d in range(3):
        for a in range(PROBES):
            b = (a + d) % PROBES
            if (max(a, b), min(a, b)) not in entry:
                chosen = jnp.where((row == a) & (lane == d), packed, 0.0)
                whole = jnp.sum(jnp.sum(chosen, axis=1, keepdims=True), axis=0, keepdims=True)
                entry[max(a, b), min(a, b)] = jnp.broadcast_to(whole, (8, LANES)) / plan.total
    low = {}
    inv = {}
    for j in range(PROBES):
        rest = entry[j, j]
        for m in range(j):
            rest = rest - low[j, m] * low[j, m]
        low[j, j] = jnp.sqrt(rest)
        inv[j, j] = 1.0 / low[j, j]
        for i in range(j + 1, PROBES):
            rest = entry[i, j]
            for m in range(j):
                rest = rest - low[i, m] * low[j, m]
            low[i, j] = rest * inv[j, j]
    for i in range(PROBES):
        for j in range(i):
            total = sum(low[i, m] * inv[m, j] for m in range(j, i))
            inv[i, j] = -total * inv[i, i]
    rows = []
    for d in range(PROBES):
        value = jnp.zeros((8, LANES), jnp.float32)
        for a in range(d, PROBES):
            value = jnp.where(row % 4 == a, inv[a, a - d], value)
        rows.append(value)
    return rows


def final_kernel(plan, sketch_ref, *rest):
    ins, basis_ref, coeffs_ref = rest[: plan.shards], rest[plan.shards], rest[plan.shards + 1]
    packed = sum(ref[plan.shard_lines] for ref in ins)
    rows = inverse_rows(plan, packed)

    def scaled(x):
        width = x.shape[1]
        return sum((rows[d][:, :width] * (roll(x, d, 0) if d else x)) for d in range(PROBES))

    for pair in range(plan.shard_lines // 2):
        two = [scaled(sum(ref[2 * pair + i] for ref in ins)) for i in range(2)]
        coeffs_ref[pl.ds(16 * pair, 16)] = jnp.concatenate(two, axis=0).astype(jnp.bfloat16)
    for line in range(plan.lines):
        for start in range(0, plan.group, LANES):
            width = min(LANES, plan.group - start)
            value = scaled(sketch_ref[line, :, pl.ds(start, width)])
            for part in range(2):
                basis_ref[line, part, :, pl.ds(start, width)] = value[4 * part : 4 * part + 4]


def finish(plan, sketch, pieces):
    vmem = pl.BlockSpec(memory_space=pltpu.VMEM)
    return pl.pallas_call(
        functools.partial(final_kernel, plan),
        out_shape=[
            jax.ShapeDtypeStruct((plan.lines, 2, PROBES, plan.group), jnp.float32),
            jax.ShapeDtypeStruct((plan.shard_lines * 8, LANES), jnp.bfloat16),
        ],
        in_specs=[vmem] * (1 + plan.shards),
        out_specs=[vmem] * 2,
        name="finish",
    )(sketch, *pieces)


def trade(x, axis, size, k):
    return lax.ppermute(x, axis, [(i, i ^ k) for i in range(size)])


def on_device(param, sensor, blocks, probes):
    lines, parts, group, nodes = blocks.shape
    plan = Plan(lines, parts, group, nodes, sensor)
    rank = lax.axis_index("param")
    me = (rank % QUAD).astype(jnp.int32).reshape(1)
    spot = lax.axis_index("sensor").astype(jnp.int32).reshape(1)
    flat_blocks = blocks.transpose(0, 2, 1, 3).reshape(plan.rows, nodes)
    flat_probes = probes.reshape(lines * parts * PROBES, nodes)
    terms, kept = sketch_terms(plan, me, flat_blocks, flat_probes)
    total = terms[0] + sum(trade(terms[k], "param", param, k) for k in range(1, QUAD))
    span = QUAD
    while span * 2 < param:
        total = total + trade(total, "param", param, span)
        span *= 2
    sums = [total] + ([trade(total, "param", param, span)] if span < param else [])
    own = add_with_gram(plan, *sums)
    pieces = [own] + [trade(own, "param", param, k) for k in range(1, QUAD)]
    adjoint = adjoint_terms(plan, me, spot, kept, pieces)
    gathered = [adjoint[0]] + [trade(adjoint[k], "sensor", sensor, k) for k in range(1, sensor)]
    sketch = sketch_by_line(plan, me, pieces)
    basis, coeffs = finish(plan, sketch, gathered)
    return basis, coeffs.reshape(plan.shard_lines, parts, PROBES, nodes)


def solution(mesh):
    param, sensor = mesh.shape["param"], mesh.shape["sensor"]
    assert param % QUAD == 0 and param & (param - 1) == 0 and sensor & (sensor - 1) == 0
    placed = (P(None, None, "sensor", "param"), P(None, None, None, "param"))
    return jax.shard_map(
        functools.partial(on_device, param, sensor),
        mesh=mesh,
        in_specs=placed,
        out_specs=(P(None, None, None, "sensor"), P("sensor", None, None, "param")),
        check_vma=False,
    )
```

time: 146 us -> 47.5 us (0.33)
  waiting for transfers between devices: 93.8 us -> 13.9 us
  Pallas kernels: 0 us -> 17.2 us
  matrix products: 15 us -> 0 us
  between operations: 14.2 us -> 0.68 us
  local copies, waits for them, and re-layouts: 14.7 us -> 1.89 us
  starting transfers between devices: 0.08 us -> 12.6 us
  blocking collectives: 5.65 us -> 0 us
    psum x1 -> x0, waiting for transfers between devices: 74.1 us -> none  [on_device(): sketch = lax.psum(partial_sketch, 'param')]
    unnamed x3 -> x0, waiting for transfers between devices: 19.7 us -> none
    pallas_call x0 -> x5, Pallas kernels: none -> 17.2 us  [the longest x1 6.59 us: sketch_terms(): pl.pallas_call(functools.partial(sketch_kernel, plan), out_shape=[piece]...]
    dot_general x10 -> x0, matrix products: 14.8 us -> none  [the longest x1 2.72 us: on_device(): jnp.einsum('fsn,fas->fan', block_real, vector_imag, preferred_element_typ...]
    ppermute x0 -> x10, waiting for transfers between devices: none -> 13.9 us  [trade(): return lax.ppermute(x, axis, [(i, i ^ k) for i in range(size)])]
    ppermute x0 -> x10, starting transfers between devices: none -> 12.6 us  [trade(): return lax.ppermute(x, axis, [(i, i ^ k) for i in range(size)])]
    slice x1 -> x0, local copies, waits for them, and re-layouts: 10 us -> none  [on_device(): block_imag = blocks[:, 1]]
    psum x1 -> x0, blocking collectives: 5.65 us -> none  [on_device(): gram = lax.psum(local_gram(sketch), 'sensor')]
  transfers between devices with their start and end apart: 2 -> 10, of which waited for: 2 -> 8; matrix products, arithmetic and copies ran while one was open for 0% -> 0% of each run, Pallas kernels for 0% -> 5%
where the time goes in v1:
time: 47.5 us; the launch traced here: 47.2 us
  Pallas kernels  17.2 us (36%)
  waiting for transfers between devices  13.9 us (29%)
  starting transfers between devices  12.6 us (27%)
  local copies, waits for them, and re-layouts  1.89 us (4%)
  other arithmetic  0.91 us (2%)
  between operations  0.68 us (1%)
    ppermute x10, waiting for transfers between devices, trade(): return lax.ppermute(x, axis, [(i, i ^ k) for i in range(size)])  13.9 us
    ppermute x10, starting transfers between devices, trade(): return lax.ppermute(x, axis, [(i, i ^ k) for i in range(size)])  12.6 us
    pallas_call x1, Pallas kernels, sketch_terms(): pl.pallas_call(functools.partial(sketch_kernel, plan), out_shape=[piece]...  6.59 us
    pallas_call x1, Pallas kernels, adjoint_terms(): pl.pallas_call(functools.partial(adjoint_kernel, plan), out_shape=[jax.Sh...  4.25 us
    pallas_call x1, Pallas kernels, sketch_by_line(): pl.pallas_call(functools.partial(by_line_kernel, plan), out_shape=jax.Sha...  2.37 us
    pallas_call x1, Pallas kernels, finish(): pl.pallas_call(functools.partial(final_kernel, plan), out_shape=[jax.Shap...  2.29 us
    unnamed x16, local copies, waits for them, and re-layouts  1.89 us
    pallas_call x1, Pallas kernels, add_with_gram(): pl.pallas_call(functools.partial(gram_kernel, plan), out_shape=jax.ShapeD...  1.68 us
  transfers between devices with their start and end apart: 10, of which 8 were waited for; matrix products, arithmetic and copies ran while one was open for 0% of the time, Pallas kernels for 5%

profile of v1, /device:TPU:0, one launch (start us, length us, event | category | flops | bytes accessed | tf_op | source)
XLA Modules:
  0.0 47.2 jit_solution(15120315372038728908)
XLA Ops:
  0.6 6.6 %sketch_terms.1 = (f32[19,8,128]{2,1,0:T(8,128)}, f32[19,8,128]{2,1,0:T(8,128)}, f32[19,8,128]{2,1,0:T(8,128)}, f32[19,8,128]{2,1,0:T(8,128)}, bf16[4,4864,128]{2,1,0:T(8,128)(2,1)}) custom-call(s32[1]{0:T(128)} %bitcast.me_ref, bf16[19200,128]{1,0:T(8,128)(2,1)} %bitcast.7, bf16[512,128]{1,0:T(8,128)(2,1)} %bitcast.8), custom_call_target="tpu_custom_call" | custom-call | tf_op jit(solution)/shard_map/sketch_terms/pallas_call | solution.py:105
  7.2 3.1 %collective-permute-start = (f32[19,8,128]{2,1,0:T(8,128)}, f32[19,8,128]{2,1,0:T(8,128)S(1)}, u32[]{:S(2)}, u32[]{:S(2)}) collective-permute-start(f32[19,8,128]{2,1,0:T(8,128)} %get-tuple-element.14), channel_id=1, source_target_pairs={{0,4},{4,0},{8,12},{12,8},{16,20},{20,16},{24,28},{28,24},{1,5},{5... | collective-permute-start | bytes 233480 | tf_op jit(solution)/shard_map/ppermute | solution.py:312
  10.3 1.6 %collective-permute-start.1 = (f32[19,8,128]{2,1,0:T(8,128)}, f32[19,8,128]{2,1,0:T(8,128)S(1)}, u32[]{:S(2)}, u32[]{:S(2)}) collective-permute-start(f32[19,8,128]{2,1,0:T(8,128)} %get-tuple-element.15), channel_id=1, source_target_pairs={{0,8},{4,12},{8,0},{12,4},{16,24},{20,28},{24,16},{28,20},{1,9},{5... | collective-permute-start | bytes 233480 | tf_op jit(solution)/shard_map/ppermute | solution.py:312
  11.9 1.0 %collective-permute-done = f32[19,8,128]{2,1,0:T(8,128)S(1)} collective-permute-done((f32[19,8,128]{2,1,0:T(8,128)}, f32[19,8,128]{2,1,0:T(8,128)S(1)}, u32[]{:S(2)}, u32[]{:S(2)}) %collective-permute-start) | collective-permute-done | bytes 77856 | tf_op jit(solution)/shard_map/ppermute | solution.py:312
  12.9 2.7 %collective-permute-done.1 = f32[19,8,128]{2,1,0:T(8,128)S(1)} collective-permute-done((f32[19,8,128]{2,1,0:T(8,128)}, f32[19,8,128]{2,1,0:T(8,128)S(1)}, u32[]{:S(2)}, u32[]{:S(2)}) %collective-permute-start.1) | collective-permute-done | bytes 77856 | tf_op jit(solution)/shard_map/ppermute | solution.py:312
  15.6 1.8 %collective-permute-done.2 = f32[19,8,128]{2,1,0:T(8,128)S(1)} collective-permute-done((f32[19,8,128]{2,1,0:T(8,128)}, f32[19,8,128]{2,1,0:T(8,128)S(1)}, u32[]{:S(2)}, u32[]{:S(2)}) %collective-permute-start.2) | collective-permute-done | bytes 77856 | tf_op jit(solution)/shard_map/ppermute | solution.py:312
  17.4 0.9 %add_add_fusion.refs_0_ = f32[19,8,128]{2,1,0:T(8,128)S(1)} fusion(f32[19,8,128]{2,1,0:T(8,128)} %get-tuple-element.13, f32[19,8,128]{2,1,0:T(8,128)S(1)} %collective-permute-done.2, f32[19,8,128]{2,1,0:T(8,128)S(1)} %collective-permute-done, f32[19,8,128]{2,1,0:T(8,128)S(1)} %collective-permute-done.1), kind=kLoop, calls=%fused_computation | loop fusion | flops 58368 | bytes 389120 | tf_op jit(solution)/shard_map/add | solution.py:324
  18.3 2.7 %collective-permute-start.3 = (f32[19,8,128]{2,1,0:T(8,128)S(1)}, f32[19,8,128]{2,1,0:T(8,128)S(1)}, u32[]{:S(2)}, u32[]{:S(2)}) collective-permute-start(f32[19,8,128]{2,1,0:T(8,128)S(1)} %add_add_fusion.refs_0_), channel_id=1, source_target_pairs={{0,16},{4,20},{8,24},{12,28},{16,0},{20,4},{24,8},{28,12},{1,17},{... | collective-permute-start | bytes 233480 | tf_op jit(solution)/shard_map/ppermute | solution.py:312
  21.0 3.4 %collective-permute-done.3.refs_1_ = f32[19,8,128]{2,1,0:T(8,128)S(1)} collective-permute-done((f32[19,8,128]{2,1,0:T(8,128)S(1)}, f32[19,8,128]{2,1,0:T(8,128)S(1)}, u32[]{:S(2)}, u32[]{:S(2)}) %collective-permute-start.3) | collective-permute-done | bytes 77856 | tf_op jit(solution)/shard_map/ppermute | solution.py:312
  24.4 0.6 %copy-done.4 = f32[19,8,128]{2,1,0:T(8,128)} copy-done((f32[19,8,128]{2,1,0:T(8,128)}, f32[19,8,128]{2,1,0:T(8,128)S(1)}, u32[]{:S(2)}) %copy-start.4) | copy-done | bytes 77848
  25.0 1.7 %add_with_gram.1.rest_0_ = f32[20,8,128]{2,1,0:T(8,128)} custom-call(f32[19,8,128]{2,1,0:T(8,128)} %copy-done.3, f32[19,8,128]{2,1,0:T(8,128)} %copy-done.4), custom_call_target="tpu_custom_call" | custom-call | tf_op jit(solution)/shard_map/add_with_gram/pallas_call | solution.py:140
  26.7 0.5 collective-permute-start.6
  27.2 1.6 %collective-permute-start.5 = (f32[20,8,128]{2,1,0:T(8,128)}, f32[20,8,128]{2,1,0:T(8,128)S(1)}, u32[]{:S(2)}, u32[]{:S(2)}) collective-permute-start(f32[20,8,128]{2,1,0:T(8,128)} %add_with_gram.1.rest_0_), channel_id=1, source_target_pairs={{0,8},{4,12},{8,0},{12,4},{16,24},{20,28},{24,16},{28,20},{1,9},{5... | collective-permute-start | bytes 245768 | tf_op jit(solution)/shard_map/ppermute | solution.py:312
  28.8 1.4 %collective-permute-start.4 = (f32[20,8,128]{2,1,0:T(8,128)}, f32[20,8,128]{2,1,0:T(8,128)S(1)}, u32[]{:S(2)}, u32[]{:S(2)}) collective-permute-start(f32[20,8,128]{2,1,0:T(8,128)} %add_with_gram.1.rest_0_), channel_id=1, source_target_pairs={{0,4},{4,0},{8,12},{12,8},{16,20},{20,16},{24,28},{28,24},{1,5},{5... | collective-permute-start | bytes 245768 | tf_op jit(solution)/shard_map/ppermute | solution.py:312
  30.2 2.1 %collective-permute-done.6.rest_3_ = f32[20,8,128]{2,1,0:T(8,128)S(1)} collective-permute-done((f32[20,8,128]{2,1,0:T(8,128)}, f32[20,8,128]{2,1,0:T(8,128)S(1)}, u32[]{:S(2)}, u32[]{:S(2)}) %collective-permute-start.6) | collective-permute-done | bytes 81952 | tf_op jit(solution)/shard_map/ppermute | solution.py:312
  32.3 1.1 %collective-permute-done.4.rest_1_ = f32[20,8,128]{2,1,0:T(8,128)S(1)} collective-permute-done((f32[20,8,128]{2,1,0:T(8,128)}, f32[20,8,128]{2,1,0:T(8,128)S(1)}, u32[]{:S(2)}, u32[]{:S(2)}) %collective-permute-start.4) | collective-permute-done | bytes 81952 | tf_op jit(solution)/shard_map/ppermute | solution.py:312
  33.4 0.6 %copy-done.2 = f32[20,8,128]{2,1,0:T(8,128)} copy-done((f32[20,8,128]{2,1,0:T(8,128)}, f32[20,8,128]{2,1,0:T(8,128)S(1)}, u32[]{:S(2)}) %copy-start.2) | copy-done | bytes 81944
  34.1 4.2 %adjoint_terms.1 = (f32[17,8,128]{2,1,0:T(8,128)}, f32[17,8,128]{2,1,0:T(8,128)}, f32[17,8,128]{2,1,0:T(8,128)}, f32[17,8,128]{2,1,0:T(8,128)}) custom-call(s32[1]{0:T(128)} %bitcast.me_ref, s32[1]{0:T(128)} %bitcast.4.spot_ref, bf16[4,4864,128]{2,1,0:T(8,128)(2,1)} %get-tuple-element.17.kept_ref, f32[20,8,128]{2,1,0:T(8,128)} %add_with_gram.1.rest_0_, ...), custom_call_target="tpu_custom_call" | custom-call | tf_op jit(solution)/shard_map/adjoint_terms/pallas_call | solution.py:195
  38.3 1.5 %collective-permute-start.8 = (f32[17,8,128]{2,1,0:T(8,128)}, f32[17,8,128]{2,1,0:T(8,128)S(1)}, u32[]{:S(2)}, u32[]{:S(2)}) collective-permute-start(f32[17,8,128]{2,1,0:T(8,128)} %get-tuple-element.20), channel_id=1, source_target_pairs={{0,2},{1,3},{2,0},{3,1},{4,6},{5,7},{6,4},{7,5},{8,10},{9,11},{10,... | collective-permute-start | bytes 208904 | tf_op jit(solution)/shard_map/ppermute | solution.py:312
  40.2 2.4 %sketch_by_line.1.sketch_ref = f32[64,8,150]{2,1,0:T(8,128)} custom-call(s32[1]{0:T(128)} %bitcast.me_ref, f32[20,8,128]{2,1,0:T(8,128)} %add_with_gram.1.rest_0_, f32[20,8,128]{2,1,0:T(8,128)} %copy-done.2, f32[20,8,128]{2,1,0:T(8,128)} %copy-done.1, f32[20,8,128]{2,1,0:T(8,128)} %copy-done), custom_call_target="tpu_custom_call" | custom-call | tf_op jit(solution)/shard_map/sketch_by_line/pallas_call | solution.py:229
  42.5 0.7 %collective-permute-done.8.rest_2_ = f32[17,8,128]{2,1,0:T(8,128)S(1)} collective-permute-done((f32[17,8,128]{2,1,0:T(8,128)}, f32[17,8,128]{2,1,0:T(8,128)S(1)}, u32[]{:S(2)}, u32[]{:S(2)}) %collective-permute-start.8) | collective-permute-done | bytes 69664 | tf_op jit(solution)/shard_map/ppermute | solution.py:312
  43.2 1.1 %collective-permute-done.9.rest_3_ = f32[17,8,128]{2,1,0:T(8,128)S(1)} collective-permute-done((f32[17,8,128]{2,1,0:T(8,128)}, f32[17,8,128]{2,1,0:T(8,128)S(1)}, u32[]{:S(2)}, u32[]{:S(2)}) %collective-permute-start.9) | collective-permute-done | bytes 69664 | tf_op jit(solution)/shard_map/ppermute | solution.py:312
  44.3 0.6 %copy-done.7 = f32[17,8,128]{2,1,0:T(8,128)} copy-done((f32[17,8,128]{2,1,0:T(8,128)}, f32[17,8,128]{2,1,0:T(8,128)S(1)}, u32[]{:S(2)}) %copy-start.7) | copy-done | bytes 69656
  44.9 2.3 %finish.1 = (f32[64,2,4,150]{3,2,1,0:T(4,128)}, bf16[128,128]{1,0:T(8,128)(2,1)}) custom-call(f32[64,8,150]{2,1,0:T(8,128)} %sketch_by_line.1.sketch_ref, f32[17,8,128]{2,1,0:T(8,128)} %get-tuple-element.18.rest_0_, f32[17,8,128]{2,1,0:T(8,128)} %copy-done.5, f32[17,8,128]{2,1,0:T(8,128)} %copy-done.6, f32[17,8,128]{2,1,0:T(8,128)} %copy-done.7), custom_call_target="tpu_custom_call" | custom-call | tf_op jit(solution)/shard_map/finish/pallas_call | solution.py:299
  (18 shorter events, 0.4 us)
Async XLA Ops:
  7.2 5.6 %collective-permute-start = (f32[19,8,128]{2,1,0:T(8,128)}, f32[19,8,128]{2,1,0:T(8,128)S(1)}, u32[]{:S(2)}, u32[]{:S(2)}) collective-permute-start(f32[19,8,128]{2,1,0:T(8,128)} %get-tuple-element.14), channel_id=1, source_target_pairs={{0,4},{4,0},{8,12},{12,8},{16,20},{20,16},{24,28},{28,24},{1,5},{5... | collective-permute-start | bytes 233480 | tf_op jit(solution)/shard_map/ppermute | solution.py:312
  10.3 5.3 %collective-permute-start.1 = (f32[19,8,128]{2,1,0:T(8,128)}, f32[19,8,128]{2,1,0:T(8,128)S(1)}, u32[]{:S(2)}, u32[]{:S(2)}) collective-permute-start(f32[19,8,128]{2,1,0:T(8,128)} %get-tuple-element.15), channel_id=1, source_target_pairs={{0,8},{4,12},{8,0},{12,4},{16,24},{20,28},{24,16},{28,20},{1,9},{5... | collective-permute-start | bytes 233480 | tf_op jit(solution)/shard_map/ppermute | solution.py:312
  11.9 5.5 %collective-permute-start.2 = (f32[19,8,128]{2,1,0:T(8,128)}, f32[19,8,128]{2,1,0:T(8,128)S(1)}, u32[]{:S(2)}, u32[]{:S(2)}) collective-permute-start(f32[19,8,128]{2,1,0:T(8,128)} %get-tuple-element.16), channel_id=1, source_target_pairs={{0,12},{4,8},{8,4},{12,0},{16,28},{20,24},{24,20},{28,16},{1,13},{... | collective-permute-start | bytes 233480 | tf_op jit(solution)/shard_map/ppermute | solution.py:312
  18.3 6.1 %copy-start.3 = (f32[19,8,128]{2,1,0:T(8,128)}, f32[19,8,128]{2,1,0:T(8,128)S(1)}, u32[]{:S(2)}) copy-start(f32[19,8,128]{2,1,0:T(8,128)S(1)} %add_add_fusion.refs_0_) | copy-start | bytes 233476
  18.3 6.1 %collective-permute-start.3 = (f32[19,8,128]{2,1,0:T(8,128)S(1)}, f32[19,8,128]{2,1,0:T(8,128)S(1)}, u32[]{:S(2)}, u32[]{:S(2)}) collective-permute-start(f32[19,8,128]{2,1,0:T(8,128)S(1)} %add_add_fusion.refs_0_), channel_id=1, source_target_pairs={{0,16},{4,20},{8,24},{12,28},{16,0},{20,4},{24,8},{28,12},{1,17},{... | collective-permute-start | bytes 233480 | tf_op jit(solution)/shard_map/ppermute | solution.py:312
  24.4 0.6 %copy-start.4 = (f32[19,8,128]{2,1,0:T(8,128)}, f32[19,8,128]{2,1,0:T(8,128)S(1)}, u32[]{:S(2)}) copy-start(f32[19,8,128]{2,1,0:T(8,128)S(1)} %collective-permute-done.3.refs_1_) | copy-start | bytes 233476
  26.7 5.6 %collective-permute-start.6 = (f32[20,8,128]{2,1,0:T(8,128)}, f32[20,8,128]{2,1,0:T(8,128)S(1)}, u32[]{:S(2)}, u32[]{:S(2)}) collective-permute-start(f32[20,8,128]{2,1,0:T(8,128)} %add_with_gram.1.rest_0_), channel_id=1, source_target_pairs={{0,12},{4,8},{8,4},{12,0},{16,28},{20,24},{24,20},{28,16},{1,13},{... | collective-permute-start | bytes 245768 | tf_op jit(solution)/shard_map/ppermute | solution.py:312
  27.2 5.1 %collective-permute-start.5 = (f32[20,8,128]{2,1,0:T(8,128)}, f32[20,8,128]{2,1,0:T(8,128)S(1)}, u32[]{:S(2)}, u32[]{:S(2)}) collective-permute-start(f32[20,8,128]{2,1,0:T(8,128)} %add_with_gram.1.rest_0_), channel_id=1, source_target_pairs={{0,8},{4,12},{8,0},{12,4},{16,24},{20,28},{24,16},{28,20},{1,9},{5... | collective-permute-start | bytes 245768 | tf_op jit(solution)/shard_map/ppermute | solution.py:312
  28.8 4.7 %collective-permute-start.4 = (f32[20,8,128]{2,1,0:T(8,128)}, f32[20,8,128]{2,1,0:T(8,128)S(1)}, u32[]{:S(2)}, u32[]{:S(2)}) collective-permute-start(f32[20,8,128]{2,1,0:T(8,128)} %add_with_gram.1.rest_0_), channel_id=1, source_target_pairs={{0,4},{4,0},{8,12},{12,8},{16,20},{20,16},{24,28},{28,24},{1,5},{5... | collective-permute-start | bytes 245768 | tf_op jit(solution)/shard_map/ppermute | solution.py:312
  32.2 1.2 %copy-start = (f32[20,8,128]{2,1,0:T(8,128)}, f32[20,8,128]{2,1,0:T(8,128)S(1)}, u32[]{:S(2)}) copy-start(f32[20,8,128]{2,1,0:T(8,128)S(1)} %collective-permute-done.6.rest_3_) | copy-start | bytes 245764
  32.3 1.2 %copy-start.1 = (f32[20,8,128]{2,1,0:T(8,128)}, f32[20,8,128]{2,1,0:T(8,128)S(1)}, u32[]{:S(2)}) copy-start(f32[20,8,128]{2,1,0:T(8,128)S(1)} %collective-permute-done.5.rest_2_) | copy-start | bytes 245764
  33.4 0.6 %copy-start.2 = (f32[20,8,128]{2,1,0:T(8,128)}, f32[20,8,128]{2,1,0:T(8,128)S(1)}, u32[]{:S(2)}) copy-start(f32[20,8,128]{2,1,0:T(8,128)S(1)} %collective-permute-done.4.rest_1_) | copy-start | bytes 245764
  38.3 4.2 %collective-permute-start.7 = (f32[17,8,128]{2,1,0:T(8,128)}, f32[17,8,128]{2,1,0:T(8,128)S(1)}, u32[]{:S(2)}, u32[]{:S(2)}) collective-permute-start(f32[17,8,128]{2,1,0:T(8,128)} %get-tuple-element.19), channel_id=1, source_target_pairs={{0,1},{1,0},{2,3},{3,2},{4,5},{5,4},{6,7},{7,6},{8,9},{9,8},{10,11... | collective-permute-start | bytes 208904 | tf_op jit(solution)/shard_map/ppermute | solution.py:312
  38.3 4.9 %collective-permute-start.8 = (f32[17,8,128]{2,1,0:T(8,128)}, f32[17,8,128]{2,1,0:T(8,128)S(1)}, u32[]{:S(2)}, u32[]{:S(2)}) collective-permute-start(f32[17,8,128]{2,1,0:T(8,128)} %get-tuple-element.20), channel_id=1, source_target_pairs={{0,2},{1,3},{2,0},{3,1},{4,6},{5,7},{6,4},{7,5},{8,10},{9,11},{10,... | collective-permute-start | bytes 208904 | tf_op jit(solution)/shard_map/ppermute | solution.py:312
  39.8 4.5 %collective-permute-start.9 = (f32[17,8,128]{2,1,0:T(8,128)}, f32[17,8,128]{2,1,0:T(8,128)S(1)}, u32[]{:S(2)}, u32[]{:S(2)}) collective-permute-start(f32[17,8,128]{2,1,0:T(8,128)} %get-tuple-element.21), channel_id=1, source_target_pairs={{0,3},{1,2},{2,1},{3,0},{4,7},{5,6},{6,5},{7,4},{8,11},{9,10},{10,... | collective-permute-start | bytes 208904 | tf_op jit(solution)/shard_map/ppermute | solution.py:312
  42.5 1.8 %copy-start.5 = (f32[17,8,128]{2,1,0:T(8,128)}, f32[17,8,128]{2,1,0:T(8,128)S(1)}, u32[]{:S(2)}) copy-start(f32[17,8,128]{2,1,0:T(8,128)S(1)} %collective-permute-done.7.rest_1_) | copy-start | bytes 208900
  43.2 1.1 %copy-start.6 = (f32[17,8,128]{2,1,0:T(8,128)}, f32[17,8,128]{2,1,0:T(8,128)S(1)}, u32[]{:S(2)}) copy-start(f32[17,8,128]{2,1,0:T(8,128)S(1)} %collective-permute-done.8.rest_2_) | copy-start | bytes 208900
  44.3 0.6 %copy-start.7 = (f32[17,8,128]{2,1,0:T(8,128)}, f32[17,8,128]{2,1,0:T(8,128)S(1)}, u32[]{:S(2)}) copy-start(f32[17,8,128]{2,1,0:T(8,128)S(1)} %collective-permute-done.9.rest_3_) | copy-start | bytes 208900

commit v2 on v1

--- a/solution.py
+++ b/solution.py
@@ -12,6 +12,21 @@
 QUAD = 4
 PROBES = 4
 SPLITS = 3
+
+
+MIB = 1 << 20
+
+
+def in_vmem(shape, dtype):
+    return pltpu.VMEM(shape, dtype)
+
+
+def from_vmem(*arrays):
+    return [pltpu.with_memory_space_constraint(x, pltpu.VMEM) for x in arrays]
+
+
+def params(limit):
+    return pltpu.CompilerParams(vmem_limit_bytes=limit * MIB)
 
 
 def roll(x, shift, axis):
@@ -44,9 +59,9 @@
     return (step * STEP) // plan.per_line
 
 
-def sketch_kernel(plan, me_ref, blocks_ref, probes_ref, *rest):
-    outs, kept_ref, lhs_ref, sems = rest[:QUAD], rest[QUAD], rest[QUAD + 1], rest[QUAD + 2]
-    me = me_ref[0]
+def sketch_kernel(plan, blocks_ref, probes_ref, *rest):
+    outs, kept_ref, held_ref, lhs_ref, held_sem, sems = rest[:QUAD], *rest[QUAD:]
+    me = lax.axis_index("param") & (QUAD - 1)
     main = plan.quarter - 1
     order = [k for k in range(1, QUAD)] + [0]
 
@@ -66,11 +81,14 @@
             ),
         )
 
+    load = pltpu.make_async_copy(probes_ref, held_ref, held_sem)
+    load.start()
     for k in order:
         for copy in copies(k):
             copy.start()
+    load.wait()
     held = plan.lines * 2 * PROBES
-    lhs_ref[pl.ds(0, held)] = probes_ref[...].astype(jnp.float32)
+    lhs_ref[pl.ds(0, held)] = held_ref[...].astype(jnp.float32)
     lhs_ref[pl.ds(held, 8)] = jnp.zeros((8, LANES), jnp.float32)
     low = row_of() < 4
     even = lane_of() % 2 == 0
@@ -98,22 +116,24 @@
         lax.fori_loop(0, plan.quarter, body, 0, unroll=True)
 
 
-def sketch_terms(plan, me, blocks, probes):
-    piece = jax.ShapeDtypeStruct((plan.quarter, 8, LANES), jnp.float32)
-    kept = jax.ShapeDtypeStruct((QUAD, plan.quarter * STEP, LANES), jnp.bfloat16)
-    vmem = pl.BlockSpec(memory_space=pltpu.VMEM)
-    out = pl.pallas_call(
+def sketch_terms(plan, blocks, probes):
+    piece = in_vmem((plan.quarter, 8, LANES), jnp.float32)
+    kept = in_vmem((QUAD, plan.quarter * STEP, LANES), jnp.bfloat16)
+    vmem = pl.BlockSpec(memory_space=pltpu.VMEM)
+    return pl.pallas_call(
         functools.partial(sketch_kernel, plan),
         out_shape=[piece] * QUAD + [kept],
-        in_specs=[pl.BlockSpec(memory_space=pltpu.SMEM), pl.BlockSpec(memory_space=pl.ANY), vmem],
+        in_specs=[pl.BlockSpec(memory_space=pl.ANY)] * 2,
         out_specs=[vmem] * (QUAD + 1),
         scratch_shapes=[
+            pltpu.VMEM((plan.lines * 8, LANES), jnp.bfloat16),
             pltpu.VMEM((plan.lines * 8 + 8, LANES), jnp.float32),
+            pltpu.SemaphoreType.DMA(()),
             pltpu.SemaphoreType.DMA((QUAD, 2)),
         ],
+        compiler_params=params(16),
         name="sketch_terms",
-    )(me, blocks, probes)
-    return out[:QUAD], out[QUAD]
+    )(*[pltpu.with_memory_space_constraint(x, pltpu.HBM) for x in (blocks, probes)])
 
 
 def gram_kernel(plan, *refs):
@@ -139,17 +159,18 @@
     vmem = pl.BlockSpec(memory_space=pltpu.VMEM)
     return pl.pallas_call(
         functools.partial(gram_kernel, plan),
-        out_shape=jax.ShapeDtypeStruct((plan.quarter + 1, 8, LANES), jnp.float32),
+        out_shape=in_vmem((plan.quarter + 1, 8, LANES), jnp.float32),
         in_specs=[vmem] * len(pieces),
         out_specs=vmem,
+        compiler_params=params(16),
         name="add_with_gram",
-    )(*pieces)
-
-
-def adjoint_kernel(plan, me_ref, spot_ref, kept_ref, *rest):
+    )(*from_vmem(*pieces))
+
+
+def adjoint_kernel(plan, kept_ref, *rest):
     ins, outs, acc_ref = rest[:QUAD], rest[QUAD : QUAD + plan.shards], rest[QUAD + plan.shards]
-    me = me_ref[0]
-    spot = spot_ref[0]
+    me = lax.axis_index("param") & (QUAD - 1)
+    spot = lax.axis_index("sensor")
     low = row_of() < 4
     even = lane_of() % 2 == 0
     column = lane_of((8, STEP))
@@ -189,22 +210,22 @@
         outs[k][plan.shard_lines] = packed
 
 
-def adjoint_terms(plan, me, spot, kept, pieces):
-    vmem = pl.BlockSpec(memory_space=pltpu.VMEM)
-    smem = pl.BlockSpec(memory_space=pltpu.SMEM)
+def adjoint_terms(plan, kept, pieces):
+    vmem = pl.BlockSpec(memory_space=pltpu.VMEM)
     return pl.pallas_call(
         functools.partial(adjoint_kernel, plan),
-        out_shape=[jax.ShapeDtypeStruct((plan.shard_lines + 1, 8, LANES), jnp.float32)] * plan.shards,
-        in_specs=[smem, smem] + [vmem] * (1 + QUAD),
+        out_shape=[in_vmem((plan.shard_lines + 1, 8, LANES), jnp.float32)] * plan.shards,
+        in_specs=[vmem] * (1 + QUAD),
         out_specs=[vmem] * plan.shards,
         scratch_shapes=[pltpu.VMEM((plan.lines + 1, 8, LANES), jnp.float32)],
+        compiler_params=params(16),
         name="adjoint_terms",
-    )(me, spot, kept, *pieces)
-
-
-def by_line_kernel(plan, me_ref, *rest):
+    )(*from_vmem(kept, *pieces))
+
+
+def by_line_kernel(plan, *rest):
     ins, out_ref, flat_ref = rest[:QUAD], rest[QUAD], rest[QUAD + 1]
-    me = me_ref[0]
+    me = lax.axis_index("param") & (QUAD - 1)
     lane = lane_of()
     half = LANES // 2
     stay = (row_of() < 4) == (lane < half)
@@ -224,16 +245,17 @@
             out_ref[line, :, pl.ds(i * LANES, width)] = part[:, :width]
 
 
-def sketch_by_line(plan, me, pieces):
+def sketch_by_line(plan, pieces):
     vmem = pl.BlockSpec(memory_space=pltpu.VMEM)
     return pl.pallas_call(
         functools.partial(by_line_kernel, plan),
-        out_shape=jax.ShapeDtypeStruct((plan.lines, 8, plan.group), jnp.float32),
-        in_specs=[pl.BlockSpec(memory_space=pltpu.SMEM)] + [vmem] * QUAD,
+        out_shape=in_vmem((plan.lines, 8, plan.group), jnp.float32),
+        in_specs=[vmem] * QUAD,
         out_specs=vmem,
         scratch_shapes=[pltpu.VMEM((QUAD * plan.quarter + 2, 8, LANES), jnp.float32)],
+        compiler_params=params(16),
         name="sketch_by_line",
-    )(me, *pieces)
+    )(*from_vmem(*pieces))
 
 
 def inverse_rows(plan, packed):
@@ -304,8 +326,9 @@
         ],
         in_specs=[vmem] * (1 + plan.shards),
         out_specs=[vmem] * 2,
+        compiler_params=params(16),
         name="finish",
-    )(sketch, *pieces)
+    )(*from_vmem(sketch, *pieces))
 
 
 def trade(x, axis, size, k):
@@ -315,12 +338,9 @@
 def on_device(param, sensor, blocks, probes):
     lines, parts, group, nodes = blocks.shape
     plan = Plan(lines, parts, group, nodes, sensor)
-    rank = lax.axis_index("param")
-    me = (rank % QUAD).astype(jnp.int32).reshape(1)
-    spot = lax.axis_index("sensor").astype(jnp.int32).reshape(1)
     flat_blocks = blocks.transpose(0, 2, 1, 3).reshape(plan.rows, nodes)
     flat_probes = probes.reshape(lines * parts * PROBES, nodes)
-    terms, kept = sketch_terms(plan, me, flat_blocks, flat_probes)
+    *terms, kept = sketch_terms(plan, flat_blocks, flat_probes)
     total = terms[0] + sum(trade(terms[k], "param", param, k) for k in range(1, QUAD))
     span = QUAD
     while span * 2 < param:
@@ -329,9 +349,9 @@
     sums = [total] + ([trade(total, "param", param, span)] if span < param else [])
     own = add_with_gram(plan, *sums)
     pieces = [own] + [trade(own, "param", param, k) for k in range(1, QUAD)]
-    adjoint = adjoint_terms(plan, me, spot, kept, pieces)
+    adjoint = adjoint_terms(plan, kept, pieces)
     gathered = [adjoint[0]] + [trade(adjoint[k], "sensor", sensor, k) for k in range(1, sensor)]
-    sketch = sketch_by_line(plan, me, pieces)
+    sketch = sketch_by_line(plan, pieces)
     basis, coeffs = finish(plan, sketch, gathered)
     return basis, coeffs.reshape(plan.shard_lines, parts, PROBES, nodes)
 

time: 47.5 us -> 36.2 us (0.76)
  Pallas kernels: 17.2 us -> 7.51 us
  local copies, waits for them, and re-layouts: 1.89 us -> 0 us
  waiting for transfers between devices: 13.9 us -> 15.1 us
  other arithmetic: 0.91 us -> 0.03 us
    pallas_call x3, Pallas kernels: 8.29 us -> 1.7 us  [the longest x1 1.02 us: adjoint_terms(): pl.pallas_call(functools.partial(adjoint_kernel, plan), out_shape=[in_vme...]
    pallas_call x1, Pallas kernels: 6.59 us -> 4.65 us  [sketch_terms(): pl.pallas_call(functools.partial(sketch_kernel, plan), out_shape=[piece]...]
    unnamed x16 -> x0, local copies, waits for them, and re-layouts: 1.89 us -> none
    ppermute x10, waiting for transfers between devices: 13.9 us -> 15.1 us  [trade(): return lax.ppermute(x, axis, [(i, i ^ k) for i in range(size)])]
    pallas_call x1, Pallas kernels: 2.29 us -> 1.16 us  [finish(): pl.pallas_call(functools.partial(final_kernel, plan), out_shape=[jax.Shap...]
    add x1, other arithmetic: 0.91 us -> 0.03 us  [on_device(): terms[0] + sum((trade(terms[k], 'param', param, k) for k in range(1, QUAD)))]
  transfers between devices with their start and end apart: 10 -> 10, of which waited for: 8 -> 8; matrix products, arithmetic and copies ran while one was open for 0% -> 0% of each run, Pallas kernels for 5% -> 2%
where the time goes in v2:
time: 36.2 us; the launch traced here: 36 us
  waiting for transfers between devices  15.1 us (42%)
  starting transfers between devices  12.7 us (35%)
  Pallas kernels  7.51 us (21%)
  between operations  0.68 us (2%)
    ppermute x10, waiting for transfers between devices, trade(): return lax.ppermute(x, axis, [(i, i ^ k) for i in range(size)])  15.1 us
    ppermute x10, starting transfers between devices, trade(): return lax.ppermute(x, axis, [(i, i ^ k) for i in range(size)])  12.7 us
    pallas_call x1, Pallas kernels, sketch_terms(): pl.pallas_call(functools.partial(sketch_kernel, plan), out_shape=[piece]...  4.65 us
    pallas_call x1, Pallas kernels, finish(): pl.pallas_call(functools.partial(final_kernel, plan), out_shape=[jax.Shap...  1.16 us
    pallas_call x1, Pallas kernels, adjoint_terms(): pl.pallas_call(functools.partial(adjoint_kernel, plan), out_shape=[in_vme...  1.02 us
  transfers between devices with their start and end apart: 10, of which 8 were waited for; matrix products, arithmetic and copies ran while one was open for 0% of the time, Pallas kernels for 2%

profile of v2, /device:TPU:0, one launch (start us, length us, event | category | flops | bytes accessed | tf_op | source)
XLA Modules:
  0.0 36.0 jit_solution(3137424394227143361)
XLA Ops:
  0.6 4.6 %sketch_terms.1 = (f32[19,8,128]{2,1,0:T(8,128)S(1)}, f32[19,8,128]{2,1,0:T(8,128)S(1)}, f32[19,8,128]{2,1,0:T(8,128)S(1)}, f32[19,8,128]{2,1,0:T(8,128)S(1)}, bf16[4,4864,128]{2,1,0:T(8,128)(2,1)S(1)}) custom-call(bf16[19200,128]{1,0:T(8,128)(2,1)} %bitcast.5, bf16[512,128]{1,0:T(8,128)(2,1)} %bitcast.6), custom_call_target="tpu_custom_call" | custom-call | tf_op jit(solution)/shard_map/sketch_terms/pallas_call | solution.py:123
  5.3 3.0 %collective-permute-start = (f32[19,8,128]{2,1,0:T(8,128)S(1)}, f32[19,8,128]{2,1,0:T(8,128)S(1)}, u32[]{:S(2)}, u32[]{:S(2)}) collective-permute-start(f32[19,8,128]{2,1,0:T(8,128)S(1)} %get-tuple-element.14), channel_id=1, source_target_pairs={{0,4},{4,0},{8,12},{12,8},{16,20},{20,16},{24,28},{28,24},{1,5},{5... | collective-permute-start | bytes 233480 | tf_op jit(solution)/shard_map/ppermute | solution.py:335
  8.3 1.6 %collective-permute-start.1 = (f32[19,8,128]{2,1,0:T(8,128)S(1)}, f32[19,8,128]{2,1,0:T(8,128)S(1)}, u32[]{:S(2)}, u32[]{:S(2)}) collective-permute-start(f32[19,8,128]{2,1,0:T(8,128)S(1)} %get-tuple-element.15), channel_id=1, source_target_pairs={{0,8},{4,12},{8,0},{12,4},{16,24},{20,28},{24,16},{28,20},{1,9},{5... | collective-permute-start | bytes 233480 | tf_op jit(solution)/shard_map/ppermute | solution.py:335
  9.9 0.0 collective-permute-start.2
  9.9 0.8 %collective-permute-done = f32[19,8,128]{2,1,0:T(8,128)S(1)} collective-permute-done((f32[19,8,128]{2,1,0:T(8,128)S(1)}, f32[19,8,128]{2,1,0:T(8,128)S(1)}, u32[]{:S(2)}, u32[]{:S(2)}) %collective-permute-start) | collective-permute-done | bytes 77856 | tf_op jit(solution)/shard_map/ppermute | solution.py:335
  10.7 2.7 %collective-permute-done.1 = f32[19,8,128]{2,1,0:T(8,128)S(1)} collective-permute-done((f32[19,8,128]{2,1,0:T(8,128)S(1)}, f32[19,8,128]{2,1,0:T(8,128)S(1)}, u32[]{:S(2)}, u32[]{:S(2)}) %collective-permute-start.1) | collective-permute-done | bytes 77856 | tf_op jit(solution)/shard_map/ppermute | solution.py:335
  13.4 1.8 %collective-permute-done.2 = f32[19,8,128]{2,1,0:T(8,128)S(1)} collective-permute-done((f32[19,8,128]{2,1,0:T(8,128)S(1)}, f32[19,8,128]{2,1,0:T(8,128)S(1)}, u32[]{:S(2)}, u32[]{:S(2)}) %collective-permute-start.2) | collective-permute-done | bytes 77856 | tf_op jit(solution)/shard_map/ppermute | solution.py:335
  15.2 2.7 %collective-permute-start.3 = (f32[19,8,128]{2,1,0:T(8,128)S(1)}, f32[19,8,128]{2,1,0:T(8,128)S(1)}, u32[]{:S(2)}, u32[]{:S(2)}) collective-permute-start(f32[19,8,128]{2,1,0:T(8,128)S(1)} %add_add_fusion.refs_0_), channel_id=1, source_target_pairs={{0,16},{4,20},{8,24},{12,28},{16,0},{20,4},{24,8},{28,12},{1,17},{... | collective-permute-start | bytes 233480 | tf_op jit(solution)/shard_map/ppermute | solution.py:335
  17.9 3.4 %collective-permute-done.3.refs_1_ = f32[19,8,128]{2,1,0:T(8,128)S(1)} collective-permute-done((f32[19,8,128]{2,1,0:T(8,128)S(1)}, f32[19,8,128]{2,1,0:T(8,128)S(1)}, u32[]{:S(2)}, u32[]{:S(2)}) %collective-permute-start.3) | collective-permute-done | bytes 77856 | tf_op jit(solution)/shard_map/ppermute | solution.py:335
  21.3 0.1 add_with_gram.1.rest_0_
  21.4 0.5 %collective-permute-start.6 = (f32[20,8,128]{2,1,0:T(8,128)S(1)}, f32[20,8,128]{2,1,0:T(8,128)S(1)}, u32[]{:S(2)}, u32[]{:S(2)}) collective-permute-start(f32[20,8,128]{2,1,0:T(8,128)S(1)} %add_with_gram.1.rest_0_), channel_id=1, source_target_pairs={{0,12},{4,8},{8,4},{12,0},{16,28},{20,24},{24,20},{28,16},{1,13},{... | collective-permute-start | bytes 245768 | tf_op jit(solution)/shard_map/ppermute | solution.py:335
  21.9 1.6 %collective-permute-start.5 = (f32[20,8,128]{2,1,0:T(8,128)S(1)}, f32[20,8,128]{2,1,0:T(8,128)S(1)}, u32[]{:S(2)}, u32[]{:S(2)}) collective-permute-start(f32[20,8,128]{2,1,0:T(8,128)S(1)} %add_with_gram.1.rest_0_), channel_id=1, source_target_pairs={{0,8},{4,12},{8,0},{12,4},{16,24},{20,28},{24,16},{28,20},{1,9},{5... | collective-permute-start | bytes 245768 | tf_op jit(solution)/shard_map/ppermute | solution.py:335
  23.5 1.4 %collective-permute-start.4 = (f32[20,8,128]{2,1,0:T(8,128)S(1)}, f32[20,8,128]{2,1,0:T(8,128)S(1)}, u32[]{:S(2)}, u32[]{:S(2)}) collective-permute-start(f32[20,8,128]{2,1,0:T(8,128)S(1)} %add_with_gram.1.rest_0_), channel_id=1, source_target_pairs={{0,4},{4,0},{8,12},{12,8},{16,20},{20,16},{24,28},{28,24},{1,5},{5... | collective-permute-start | bytes 245768 | tf_op jit(solution)/shard_map/ppermute | solution.py:335
  24.9 1.9 %collective-permute-done.6.rest_3_ = f32[20,8,128]{2,1,0:T(8,128)S(1)} collective-permute-done((f32[20,8,128]{2,1,0:T(8,128)S(1)}, f32[20,8,128]{2,1,0:T(8,128)S(1)}, u32[]{:S(2)}, u32[]{:S(2)}) %collective-permute-start.6) | collective-permute-done | bytes 81952 | tf_op jit(solution)/shard_map/ppermute | solution.py:335
  26.8 0.0 collective-permute-done.5.rest_2_
  26.8 1.1 %collective-permute-done.4.rest_1_ = f32[20,8,128]{2,1,0:T(8,128)S(1)} collective-permute-done((f32[20,8,128]{2,1,0:T(8,128)S(1)}, f32[20,8,128]{2,1,0:T(8,128)S(1)}, u32[]{:S(2)}, u32[]{:S(2)}) %collective-permute-start.4) | collective-permute-done | bytes 81952 | tf_op jit(solution)/shard_map/ppermute | solution.py:335
  28.0 1.0 %adjoint_terms.1 = (f32[17,8,128]{2,1,0:T(8,128)S(1)}, f32[17,8,128]{2,1,0:T(8,128)S(1)}, f32[17,8,128]{2,1,0:T(8,128)S(1)}, f32[17,8,128]{2,1,0:T(8,128)S(1)}) custom-call(bf16[4,4864,128]{2,1,0:T(8,128)(2,1)S(1)} %get-tuple-element.17.kept_ref, f32[20,8,128]{2,1,0:T(8,128)S(1)} %add_with_gram.1.rest_0_, f32[20,8,128]{2,1,0:T(8,128)S(1)} %collective-permute-done.4.rest_1_, ...), custom_call_target="tpu_custom_call" | custom-call | tf_op jit(solution)/shard_map/adjoint_terms/pallas_call | solution.py:215
  29.0 0.1 collective-permute-start.7
  29.1 1.6 %collective-permute-start.8 = (f32[17,8,128]{2,1,0:T(8,128)S(1)}, f32[17,8,128]{2,1,0:T(8,128)S(1)}, u32[]{:S(2)}, u32[]{:S(2)}) collective-permute-start(f32[17,8,128]{2,1,0:T(8,128)S(1)} %get-tuple-element.20), channel_id=1, source_target_pairs={{0,2},{1,3},{2,0},{3,1},{4,6},{5,7},{6,4},{7,5},{8,10},{9,11},{10,... | collective-permute-start | bytes 208904 | tf_op jit(solution)/shard_map/ppermute | solution.py:335
  30.6 0.3 collective-permute-start.9
  30.9 0.6 %sketch_by_line.1.sketch_ref = f32[64,8,150]{2,1,0:T(8,128)S(1)} custom-call(f32[20,8,128]{2,1,0:T(8,128)S(1)} %add_with_gram.1.rest_0_, f32[20,8,128]{2,1,0:T(8,128)S(1)} %collective-permute-done.4.rest_1_, f32[20,8,128]{2,1,0:T(8,128)S(1)} %collective-permute-done.5.rest_2_, f32[20,8,128]{2,1,0:T(8,128)S(1)} %collective-permute-done.6.rest_3_), custom_call_target="tpu_custom_call" | custom-call | tf_op jit(solution)/shard_map/sketch_by_line/pallas_call | solution.py:250
  31.5 2.2 %collective-permute-done.8.rest_2_ = f32[17,8,128]{2,1,0:T(8,128)S(1)} collective-permute-done((f32[17,8,128]{2,1,0:T(8,128)S(1)}, f32[17,8,128]{2,1,0:T(8,128)S(1)}, u32[]{:S(2)}, u32[]{:S(2)}) %collective-permute-start.8) | collective-permute-done | bytes 69664 | tf_op jit(solution)/shard_map/ppermute | solution.py:335
  33.7 1.2 %collective-permute-done.9.rest_3_ = f32[17,8,128]{2,1,0:T(8,128)S(1)} collective-permute-done((f32[17,8,128]{2,1,0:T(8,128)S(1)}, f32[17,8,128]{2,1,0:T(8,128)S(1)}, u32[]{:S(2)}, u32[]{:S(2)}) %collective-permute-start.9) | collective-permute-done | bytes 69664 | tf_op jit(solution)/shard_map/ppermute | solution.py:335
  34.8 1.2 %finish.1 = (f32[64,2,4,150]{3,2,1,0:T(4,128)}, bf16[128,128]{1,0:T(8,128)(2,1)}) custom-call(f32[64,8,150]{2,1,0:T(8,128)S(1)} %sketch_by_line.1.sketch_ref, f32[17,8,128]{2,1,0:T(8,128)S(1)} %get-tuple-element.18.rest_0_, f32[17,8,128]{2,1,0:T(8,128)S(1)} %collective-permute-done.7.rest_1_, f32[17,8,128]{2,1,0:T(8,128)S(1)} %collective-permute-done.8.rest_2_, ...), custom_call_target="tpu_custom_call" | custom-call | tf_op jit(solution)/shard_map/finish/pallas_call | solution.py:321
  (2 shorter events, 0.0 us)
Async XLA Ops:
  5.3 5.4 %collective-permute-start = (f32[19,8,128]{2,1,0:T(8,128)S(1)}, f32[19,8,128]{2,1,0:T(8,128)S(1)}, u32[]{:S(2)}, u32[]{:S(2)}) collective-permute-start(f32[19,8,128]{2,1,0:T(8,128)S(1)} %get-tuple-element.14), channel_id=1, source_target_pairs={{0,4},{4,0},{8,12},{12,8},{16,20},{20,16},{24,28},{28,24},{1,5},{5... | collective-permute-start | bytes 233480 | tf_op jit(solution)/shard_map/ppermute | solution.py:335
  8.3 5.1 %collective-permute-start.1 = (f32[19,8,128]{2,1,0:T(8,128)S(1)}, f32[19,8,128]{2,1,0:T(8,128)S(1)}, u32[]{:S(2)}, u32[]{:S(2)}) collective-permute-start(f32[19,8,128]{2,1,0:T(8,128)S(1)} %get-tuple-element.15), channel_id=1, source_target_pairs={{0,8},{4,12},{8,0},{12,4},{16,24},{20,28},{24,16},{28,20},{1,9},{5... | collective-permute-start | bytes 233480 | tf_op jit(solution)/shard_map/ppermute | solution.py:335
  9.9 5.3 %collective-permute-start.2 = (f32[19,8,128]{2,1,0:T(8,128)S(1)}, f32[19,8,128]{2,1,0:T(8,128)S(1)}, u32[]{:S(2)}, u32[]{:S(2)}) collective-permute-start(f32[19,8,128]{2,1,0:T(8,128)S(1)} %get-tuple-element.16), channel_id=1, source_target_pairs={{0,12},{4,8},{8,4},{12,0},{16,28},{20,24},{24,20},{28,16},{1,13},{... | collective-permute-start | bytes 233480 | tf_op jit(solution)/shard_map/ppermute | solution.py:335
  15.2 6.1 %collective-permute-start.3 = (f32[19,8,128]{2,1,0:T(8,128)S(1)}, f32[19,8,128]{2,1,0:T(8,128)S(1)}, u32[]{:S(2)}, u32[]{:S(2)}) collective-permute-start(f32[19,8,128]{2,1,0:T(8,128)S(1)} %add_add_fusion.refs_0_), channel_id=1, source_target_pairs={{0,16},{4,20},{8,24},{12,28},{16,0},{20,4},{24,8},{28,12},{1,17},{... | collective-permute-start | bytes 233480 | tf_op jit(solution)/shard_map/ppermute | solution.py:335
  21.4 5.3 %collective-permute-start.6 = (f32[20,8,128]{2,1,0:T(8,128)S(1)}, f32[20,8,128]{2,1,0:T(8,128)S(1)}, u32[]{:S(2)}, u32[]{:S(2)}) collective-permute-start(f32[20,8,128]{2,1,0:T(8,128)S(1)} %add_with_gram.1.rest_0_), channel_id=1, source_target_pairs={{0,12},{4,8},{8,4},{12,0},{16,28},{20,24},{24,20},{28,16},{1,13},{... | collective-permute-start | bytes 245768 | tf_op jit(solution)/shard_map/ppermute | solution.py:335
  21.9 4.9 %collective-permute-start.5 = (f32[20,8,128]{2,1,0:T(8,128)S(1)}, f32[20,8,128]{2,1,0:T(8,128)S(1)}, u32[]{:S(2)}, u32[]{:S(2)}) collective-permute-start(f32[20,8,128]{2,1,0:T(8,128)S(1)} %add_with_gram.1.rest_0_), channel_id=1, source_target_pairs={{0,8},{4,12},{8,0},{12,4},{16,24},{20,28},{24,16},{28,20},{1,9},{5... | collective-permute-start | bytes 245768 | tf_op jit(solution)/shard_map/ppermute | solution.py:335
  23.5 4.4 %collective-permute-start.4 = (f32[20,8,128]{2,1,0:T(8,128)S(1)}, f32[20,8,128]{2,1,0:T(8,128)S(1)}, u32[]{:S(2)}, u32[]{:S(2)}) collective-permute-start(f32[20,8,128]{2,1,0:T(8,128)S(1)} %add_with_gram.1.rest_0_), channel_id=1, source_target_pairs={{0,4},{4,0},{8,12},{12,8},{16,20},{20,16},{24,28},{28,24},{1,5},{5... | collective-permute-start | bytes 245768 | tf_op jit(solution)/shard_map/ppermute | solution.py:335
  29.0 2.5 %collective-permute-start.7 = (f32[17,8,128]{2,1,0:T(8,128)S(1)}, f32[17,8,128]{2,1,0:T(8,128)S(1)}, u32[]{:S(2)}, u32[]{:S(2)}) collective-permute-start(f32[17,8,128]{2,1,0:T(8,128)S(1)} %get-tuple-element.19), channel_id=1, source_target_pairs={{0,1},{1,0},{2,3},{3,2},{4,5},{5,4},{6,7},{7,6},{8,9},{9,8},{10,11... | collective-permute-start | bytes 208904 | tf_op jit(solution)/shard_map/ppermute | solution.py:335
  29.1 4.6 %collective-permute-start.8 = (f32[17,8,128]{2,1,0:T(8,128)S(1)}, f32[17,8,128]{2,1,0:T(8,128)S(1)}, u32[]{:S(2)}, u32[]{:S(2)}) collective-permute-start(f32[17,8,128]{2,1,0:T(8,128)S(1)} %get-tuple-element.20), channel_id=1, source_target_pairs={{0,2},{1,3},{2,0},{3,1},{4,6},{5,7},{6,4},{7,5},{8,10},{9,11},{10,... | collective-permute-start | bytes 208904 | tf_op jit(solution)/shard_map/ppermute | solution.py:335
  30.6 4.2 %collective-permute-start.9 = (f32[17,8,128]{2,1,0:T(8,128)S(1)}, f32[17,8,128]{2,1,0:T(8,128)S(1)}, u32[]{:S(2)}, u32[]{:S(2)}) collective-permute-start(f32[17,8,128]{2,1,0:T(8,128)S(1)} %get-tuple-element.21), channel_id=1, source_target_pairs={{0,3},{1,2},{2,1},{3,0},{4,7},{5,6},{6,5},{7,4},{8,11},{9,10},{10,... | collective-permute-start | bytes 208904 | tf_op jit(solution)/shard_map/ppermute | solution.py:335

commit v3 on v2

--- a/solution.py
+++ b/solution.py
@@ -11,6 +11,8 @@
 STEP = 2 * LANES
 QUAD = 4
 PROBES = 4
+ARRIVALS = ((3, 2), (1, 0))
+URGENCY = (0, 1)
 SPLITS = 3
 
 
@@ -62,58 +64,58 @@
 def sketch_kernel(plan, blocks_ref, probes_ref, *rest):
     outs, kept_ref, held_ref, lhs_ref, held_sem, sems = rest[:QUAD], *rest[QUAD:]
     me = lax.axis_index("param") & (QUAD - 1)
-    main = plan.quarter - 1
-    order = [k for k in range(1, QUAD)] + [0]
+    whole = plan.quarter - 1
 
     def copies(k):
         first = (me ^ k) * plan.quarter
-        tail = jnp.minimum(first + main, plan.steps - 1)
-        return (
-            pltpu.make_async_copy(
-                blocks_ref.at[pl.ds(pl.multiple_of(first * STEP, STEP), main * STEP)],
-                kept_ref.at[k, pl.ds(0, main * STEP)],
-                sems.at[k, 0],
-            ),
-            pltpu.make_async_copy(
-                blocks_ref.at[pl.ds(pl.multiple_of(tail * STEP, STEP), STEP)],
-                kept_ref.at[k, pl.ds(main * STEP, STEP)],
-                sems.at[k, 1],
-            ),
-        )
+        found = []
+        for at, (start, count) in enumerate(((0, whole), (whole, 1))):
+            source = jnp.minimum(first + start, plan.steps - count)
+            found.append(
+                pltpu.make_async_copy(
+                    blocks_ref.at[pl.ds(pl.multiple_of(source * STEP, STEP), count * STEP)],
+                    kept_ref.at[k, pl.ds(start * STEP, count * STEP)],
+                    sems.at[k, at],
+                )
+            )
+        return found
 
     load = pltpu.make_async_copy(probes_ref, held_ref, held_sem)
     load.start()
-    for k in order:
-        for copy in copies(k):
-            copy.start()
+    for order, group in enumerate(ARRIVALS):
+        for k in group:
+            for copy in copies(k):
+                copy.start(priority=URGENCY[order])
     load.wait()
     held = plan.lines * 2 * PROBES
     lhs_ref[pl.ds(0, held)] = held_ref[...].astype(jnp.float32)
     lhs_ref[pl.ds(held, 8)] = jnp.zeros((8, LANES), jnp.float32)
-    low = row_of() < 4
+    low_rows = row_of() < 4
     even = lane_of() % 2 == 0
     column = lane_of((8, STEP))
-    for k in order:
-        for copy in copies(k):
-            copy.wait()
-        first = (me ^ k) * plan.quarter
-
-        def body(t, _, k=k, first=first):
-            step = first + t
-            line = first_line(plan, jnp.minimum(step, plan.steps - 1))
-            probe = lhs_ref[pl.ds(pl.multiple_of(line * 8, 8), 16)].astype(jnp.bfloat16)
-            block = kept_ref[k, pl.ds(pl.multiple_of(t * STEP, STEP), STEP)]
-            both = lax.dot_general(probe, block, (((1,), (1,)), ((), ())), preferred_element_type=jnp.float32)
-            place = column + step * STEP
-            own = jnp.where(place < (line + 1) * plan.per_line, both[:8], both[8:])
-            own = jnp.where(place < plan.rows, own, 0.0)
-            left, right = own[:, :LANES], own[:, LANES:]
-            direct = jnp.where(low, left, roll(right, 4, 0))
-            crossed = jnp.where(low, roll(left, 4, 0), right)
-            outs[k][t] = direct + jnp.where(even, -roll(crossed, -1, 1), roll(crossed, 1, 1))
-            return 0
-
-        lax.fori_loop(0, plan.quarter, body, 0, unroll=True)
+    for group in ARRIVALS:
+        for k in group:
+            for copy in copies(k):
+                copy.wait()
+        for k in group:
+            first = (me ^ k) * plan.quarter
+
+            def body(t, _, k=k, first=first):
+                step = first + t
+                line = first_line(plan, jnp.minimum(step, plan.steps - 1))
+                probe = lhs_ref[pl.ds(pl.multiple_of(line * 8, 8), 16)].astype(jnp.bfloat16)
+                block = kept_ref[k, pl.ds(pl.multiple_of(t * STEP, STEP), STEP)]
+                both = lax.dot_general(probe, block, (((1,), (1,)), ((), ())), preferred_element_type=jnp.float32)
+                place = column + step * STEP
+                own = jnp.where(place < (line + 1) * plan.per_line, both[:8], both[8:])
+                own = jnp.where(place < plan.rows, own, 0.0)
+                left, right = own[:, :LANES], own[:, LANES:]
+                direct = jnp.where(low_rows, left, roll(right, 4, 0))
+                crossed = jnp.where(low_rows, roll(left, 4, 0), right)
+                outs[k][t] = direct + jnp.where(even, -roll(crossed, -1, 1), roll(crossed, 1, 1))
+                return 0
+
+            lax.fori_loop(0, plan.quarter, body, 0, unroll=True)
 
 
 def sketch_terms(plan, blocks, probes):
@@ -341,7 +343,7 @@
     flat_blocks = blocks.transpose(0, 2, 1, 3).reshape(plan.rows, nodes)
     flat_probes = probes.reshape(lines * parts * PROBES, nodes)
     *terms, kept = sketch_terms(plan, flat_blocks, flat_probes)
-    total = terms[0] + sum(trade(terms[k], "param", param, k) for k in range(1, QUAD))
+    total = terms[0] + sum(trade(terms[k], "param", param, k) for k in reversed(range(1, QUAD)))
     span = QUAD
     while span * 2 < param:
         total = total + trade(total, "param", param, span)

time: 36.2 us -> 33.7 us (0.931)
  waiting for transfers between devices: 15.1 us -> 13.7 us
  Pallas kernels: 7.51 us -> 6.33 us
    ppermute x10, waiting for transfers between devices: 15.1 us -> 13.7 us  [trade(): return lax.ppermute(x, axis, [(i, i ^ k) for i in range(size)])]
    pallas_call x1, Pallas kernels: 4.65 us -> 3.46 us  [sketch_terms(): pl.pallas_call(functools.partial(sketch_kernel, plan), out_shape=[piece]...]
  transfers between devices with their start and end apart: 10 -> 10, of which waited for: 8 -> 9; matrix products, arithmetic and copies ran while one was open for 0% -> 0% of each run, Pallas kernels for 2% -> 2%
where the time goes in v3:
time: 33.7 us; the launch traced here: 33.5 us
  waiting for transfers between devices  13.7 us (41%)
  starting transfers between devices  12.8 us (38%)
  Pallas kernels  6.33 us (19%)
  between operations  0.68 us (2%)
    ppermute x10, waiting for transfers between devices, trade(): return lax.ppermute(x, axis, [(i, i ^ k) for i in range(size)])  13.7 us
    ppermute x10, starting transfers between devices, trade(): return lax.ppermute(x, axis, [(i, i ^ k) for i in range(size)])  12.8 us
    pallas_call x1, Pallas kernels, sketch_terms(): pl.pallas_call(functools.partial(sketch_kernel, plan), out_shape=[piece]...  3.46 us
    pallas_call x1, Pallas kernels, finish(): pl.pallas_call(functools.partial(final_kernel, plan), out_shape=[jax.Shap...  1.16 us
    pallas_call x1, Pallas kernels, adjoint_terms(): pl.pallas_call(functools.partial(adjoint_kernel, plan), out_shape=[in_vme...  1.02 us
  transfers between devices with their start and end apart: 10, of which 9 were waited for; matrix products, arithmetic and copies ran while one was open for 0% of the time, Pallas kernels for 2%

profile of v3, /device:TPU:0, one launch (start us, length us, event | category | flops | bytes accessed | tf_op | source)
XLA Modules:
  0.0 33.5 jit_solution(16146780347336161503)
XLA Ops:
  0.6 3.5 %sketch_terms.1 = (f32[19,8,128]{2,1,0:T(8,128)S(1)}, f32[19,8,128]{2,1,0:T(8,128)S(1)}, f32[19,8,128]{2,1,0:T(8,128)S(1)}, f32[19,8,128]{2,1,0:T(8,128)S(1)}, bf16[4,4864,128]{2,1,0:T(8,128)(2,1)S(1)}) custom-call(bf16[19200,128]{1,0:T(8,128)(2,1)} %bitcast.5, bf16[512,128]{1,0:T(8,128)(2,1)} %bitcast.6), custom_call_target="tpu_custom_call" | custom-call | tf_op jit(solution)/shard_map/sketch_terms/pallas_call | solution.py:125
  4.1 4.1 %collective-permute-start = (f32[19,8,128]{2,1,0:T(8,128)S(1)}, f32[19,8,128]{2,1,0:T(8,128)S(1)}, u32[]{:S(2)}, u32[]{:S(2)}) collective-permute-start(f32[19,8,128]{2,1,0:T(8,128)S(1)} %get-tuple-element.14), channel_id=1, source_target_pairs={{0,12},{4,8},{8,4},{12,0},{16,28},{20,24},{24,20},{28,16},{1,13},{... | collective-permute-start | bytes 233480 | tf_op jit(solution)/shard_map/ppermute | solution.py:337
  8.2 0.5 %collective-permute-start.1 = (f32[19,8,128]{2,1,0:T(8,128)S(1)}, f32[19,8,128]{2,1,0:T(8,128)S(1)}, u32[]{:S(2)}, u32[]{:S(2)}) collective-permute-start(f32[19,8,128]{2,1,0:T(8,128)S(1)} %get-tuple-element.15), channel_id=1, source_target_pairs={{0,8},{4,12},{8,0},{12,4},{16,24},{20,28},{24,16},{28,20},{1,9},{5... | collective-permute-start | bytes 233480 | tf_op jit(solution)/shard_map/ppermute | solution.py:337
  8.6 0.2 collective-permute-start.2
  8.8 2.0 %collective-permute-done = f32[19,8,128]{2,1,0:T(8,128)S(1)} collective-permute-done((f32[19,8,128]{2,1,0:T(8,128)S(1)}, f32[19,8,128]{2,1,0:T(8,128)S(1)}, u32[]{:S(2)}, u32[]{:S(2)}) %collective-permute-start) | collective-permute-done | bytes 77856 | tf_op jit(solution)/shard_map/ppermute | solution.py:337
  10.8 1.8 %collective-permute-done.1 = f32[19,8,128]{2,1,0:T(8,128)S(1)} collective-permute-done((f32[19,8,128]{2,1,0:T(8,128)S(1)}, f32[19,8,128]{2,1,0:T(8,128)S(1)}, u32[]{:S(2)}, u32[]{:S(2)}) %collective-permute-start.1) | collective-permute-done | bytes 77856 | tf_op jit(solution)/shard_map/ppermute | solution.py:337
  12.7 0.4 %collective-permute-done.2 = f32[19,8,128]{2,1,0:T(8,128)S(1)} collective-permute-done((f32[19,8,128]{2,1,0:T(8,128)S(1)}, f32[19,8,128]{2,1,0:T(8,128)S(1)}, u32[]{:S(2)}, u32[]{:S(2)}) %collective-permute-start.2) | collective-permute-done | bytes 77856 | tf_op jit(solution)/shard_map/ppermute | solution.py:337
  13.0 2.7 %collective-permute-start.3 = (f32[19,8,128]{2,1,0:T(8,128)S(1)}, f32[19,8,128]{2,1,0:T(8,128)S(1)}, u32[]{:S(2)}, u32[]{:S(2)}) collective-permute-start(f32[19,8,128]{2,1,0:T(8,128)S(1)} %add_add_fusion.refs_0_), channel_id=1, source_target_pairs={{0,16},{4,20},{8,24},{12,28},{16,0},{20,4},{24,8},{28,12},{1,17},{... | collective-permute-start | bytes 233480 | tf_op jit(solution)/shard_map/ppermute | solution.py:337
  15.7 2.7 %collective-permute-done.3.refs_1_ = f32[19,8,128]{2,1,0:T(8,128)S(1)} collective-permute-done((f32[19,8,128]{2,1,0:T(8,128)S(1)}, f32[19,8,128]{2,1,0:T(8,128)S(1)}, u32[]{:S(2)}, u32[]{:S(2)}) %collective-permute-start.3) | collective-permute-done | bytes 77856 | tf_op jit(solution)/shard_map/ppermute | solution.py:337
  18.4 0.1 add_with_gram.1.rest_0_
  18.5 1.9 %collective-permute-start.6 = (f32[20,8,128]{2,1,0:T(8,128)S(1)}, f32[20,8,128]{2,1,0:T(8,128)S(1)}, u32[]{:S(2)}, u32[]{:S(2)}) collective-permute-start(f32[20,8,128]{2,1,0:T(8,128)S(1)} %add_with_gram.1.rest_0_), channel_id=1, source_target_pairs={{0,12},{4,8},{8,4},{12,0},{16,28},{20,24},{24,20},{28,16},{1,13},{... | collective-permute-start | bytes 245768 | tf_op jit(solution)/shard_map/ppermute | solution.py:337
  20.4 0.6 %collective-permute-start.5 = (f32[20,8,128]{2,1,0:T(8,128)S(1)}, f32[20,8,128]{2,1,0:T(8,128)S(1)}, u32[]{:S(2)}, u32[]{:S(2)}) collective-permute-start(f32[20,8,128]{2,1,0:T(8,128)S(1)} %add_with_gram.1.rest_0_), channel_id=1, source_target_pairs={{0,8},{4,12},{8,0},{12,4},{16,24},{20,28},{24,16},{28,20},{1,9},{5... | collective-permute-start | bytes 245768 | tf_op jit(solution)/shard_map/ppermute | solution.py:337
  21.0 1.0 %collective-permute-start.4 = (f32[20,8,128]{2,1,0:T(8,128)S(1)}, f32[20,8,128]{2,1,0:T(8,128)S(1)}, u32[]{:S(2)}, u32[]{:S(2)}) collective-permute-start(f32[20,8,128]{2,1,0:T(8,128)S(1)} %add_with_gram.1.rest_0_), channel_id=1, source_target_pairs={{0,4},{4,0},{8,12},{12,8},{16,20},{20,16},{24,28},{28,24},{1,5},{5... | collective-permute-start | bytes 245768 | tf_op jit(solution)/shard_map/ppermute | solution.py:337
  22.0 2.0 %collective-permute-done.6.rest_3_ = f32[20,8,128]{2,1,0:T(8,128)S(1)} collective-permute-done((f32[20,8,128]{2,1,0:T(8,128)S(1)}, f32[20,8,128]{2,1,0:T(8,128)S(1)}, u32[]{:S(2)}, u32[]{:S(2)}) %collective-permute-start.6) | collective-permute-done | bytes 81952 | tf_op jit(solution)/shard_map/ppermute | solution.py:337
  24.0 0.9 %collective-permute-done.5.rest_2_ = f32[20,8,128]{2,1,0:T(8,128)S(1)} collective-permute-done((f32[20,8,128]{2,1,0:T(8,128)S(1)}, f32[20,8,128]{2,1,0:T(8,128)S(1)}, u32[]{:S(2)}, u32[]{:S(2)}) %collective-permute-start.5) | collective-permute-done | bytes 81952 | tf_op jit(solution)/shard_map/ppermute | solution.py:337
  24.8 0.6 %collective-permute-done.4.rest_1_ = f32[20,8,128]{2,1,0:T(8,128)S(1)} collective-permute-done((f32[20,8,128]{2,1,0:T(8,128)S(1)}, f32[20,8,128]{2,1,0:T(8,128)S(1)}, u32[]{:S(2)}, u32[]{:S(2)}) %collective-permute-start.4) | collective-permute-done | bytes 81952 | tf_op jit(solution)/shard_map/ppermute | solution.py:337
  25.5 1.0 %adjoint_terms.1 = (f32[17,8,128]{2,1,0:T(8,128)S(1)}, f32[17,8,128]{2,1,0:T(8,128)S(1)}, f32[17,8,128]{2,1,0:T(8,128)S(1)}, f32[17,8,128]{2,1,0:T(8,128)S(1)}) custom-call(bf16[4,4864,128]{2,1,0:T(8,128)(2,1)S(1)} %get-tuple-element.17.kept_ref, f32[20,8,128]{2,1,0:T(8,128)S(1)} %add_with_gram.1.rest_0_, f32[20,8,128]{2,1,0:T(8,128)S(1)} %collective-permute-done.4.rest_1_, ...), custom_call_target="tpu_custom_call" | custom-call | tf_op jit(solution)/shard_map/adjoint_terms/pallas_call | solution.py:217
  26.5 0.1 collective-permute-start.7
  26.6 1.3 %collective-permute-start.8 = (f32[17,8,128]{2,1,0:T(8,128)S(1)}, f32[17,8,128]{2,1,0:T(8,128)S(1)}, u32[]{:S(2)}, u32[]{:S(2)}) collective-permute-start(f32[17,8,128]{2,1,0:T(8,128)S(1)} %get-tuple-element.20), channel_id=1, source_target_pairs={{0,2},{1,3},{2,0},{3,1},{4,6},{5,7},{6,4},{7,5},{8,10},{9,11},{10,... | collective-permute-start | bytes 208904 | tf_op jit(solution)/shard_map/ppermute | solution.py:337
  27.9 0.5 %collective-permute-start.9 = (f32[17,8,128]{2,1,0:T(8,128)S(1)}, f32[17,8,128]{2,1,0:T(8,128)S(1)}, u32[]{:S(2)}, u32[]{:S(2)}) collective-permute-start(f32[17,8,128]{2,1,0:T(8,128)S(1)} %get-tuple-element.21), channel_id=1, source_target_pairs={{0,3},{1,2},{2,1},{3,0},{4,7},{5,6},{6,5},{7,4},{8,11},{9,10},{10,... | collective-permute-start | bytes 208904 | tf_op jit(solution)/shard_map/ppermute | solution.py:337
  28.4 0.6 %sketch_by_line.1.sketch_ref = f32[64,8,150]{2,1,0:T(8,128)S(1)} custom-call(f32[20,8,128]{2,1,0:T(8,128)S(1)} %add_with_gram.1.rest_0_, f32[20,8,128]{2,1,0:T(8,128)S(1)} %collective-permute-done.4.rest_1_, f32[20,8,128]{2,1,0:T(8,128)S(1)} %collective-permute-done.5.rest_2_, f32[20,8,128]{2,1,0:T(8,128)S(1)} %collective-permute-done.6.rest_3_), custom_call_target="tpu_custom_call" | custom-call | tf_op jit(solution)/shard_map/sketch_by_line/pallas_call | solution.py:252
  29.0 2.4 %collective-permute-done.8.rest_2_ = f32[17,8,128]{2,1,0:T(8,128)S(1)} collective-permute-done((f32[17,8,128]{2,1,0:T(8,128)S(1)}, f32[17,8,128]{2,1,0:T(8,128)S(1)}, u32[]{:S(2)}, u32[]{:S(2)}) %collective-permute-start.8) | collective-permute-done | bytes 69664 | tf_op jit(solution)/shard_map/ppermute | solution.py:337
  31.4 1.0 %collective-permute-done.9.rest_3_ = f32[17,8,128]{2,1,0:T(8,128)S(1)} collective-permute-done((f32[17,8,128]{2,1,0:T(8,128)S(1)}, f32[17,8,128]{2,1,0:T(8,128)S(1)}, u32[]{:S(2)}, u32[]{:S(2)}) %collective-permute-start.9) | collective-permute-done | bytes 69664 | tf_op jit(solution)/shard_map/ppermute | solution.py:337
  32.4 1.2 %finish.1 = (f32[64,2,4,150]{3,2,1,0:T(4,128)}, bf16[128,128]{1,0:T(8,128)(2,1)}) custom-call(f32[64,8,150]{2,1,0:T(8,128)S(1)} %sketch_by_line.1.sketch_ref, f32[17,8,128]{2,1,0:T(8,128)S(1)} %get-tuple-element.18.rest_0_, f32[17,8,128]{2,1,0:T(8,128)S(1)} %collective-permute-done.7.rest_1_, f32[17,8,128]{2,1,0:T(8,128)S(1)} %collective-permute-done.8.rest_2_, ...), custom_call_target="tpu_custom_call" | custom-call | tf_op jit(solution)/shard_map/finish/pallas_call | solution.py:323
  (2 shorter events, 0.0 us)
Async XLA Ops:
  4.1 6.7 %collective-permute-start = (f32[19,8,128]{2,1,0:T(8,128)S(1)}, f32[19,8,128]{2,1,0:T(8,128)S(1)}, u32[]{:S(2)}, u32[]{:S(2)}) collective-permute-start(f32[19,8,128]{2,1,0:T(8,128)S(1)} %get-tuple-element.14), channel_id=1, source_target_pairs={{0,12},{4,8},{8,4},{12,0},{16,28},{20,24},{24,20},{28,16},{1,13},{... | collective-permute-start | bytes 233480 | tf_op jit(solution)/shard_map/ppermute | solution.py:337
  8.2 4.5 %collective-permute-start.1 = (f32[19,8,128]{2,1,0:T(8,128)S(1)}, f32[19,8,128]{2,1,0:T(8,128)S(1)}, u32[]{:S(2)}, u32[]{:S(2)}) collective-permute-start(f32[19,8,128]{2,1,0:T(8,128)S(1)} %get-tuple-element.15), channel_id=1, source_target_pairs={{0,8},{4,12},{8,0},{12,4},{16,24},{20,28},{24,16},{28,20},{1,9},{5... | collective-permute-start | bytes 233480 | tf_op jit(solution)/shard_map/ppermute | solution.py:337
  8.6 4.4 %collective-permute-start.2 = (f32[19,8,128]{2,1,0:T(8,128)S(1)}, f32[19,8,128]{2,1,0:T(8,128)S(1)}, u32[]{:S(2)}, u32[]{:S(2)}) collective-permute-start(f32[19,8,128]{2,1,0:T(8,128)S(1)} %get-tuple-element.16), channel_id=1, source_target_pairs={{0,4},{4,0},{8,12},{12,8},{16,20},{20,16},{24,28},{28,24},{1,5},{5... | collective-permute-start | bytes 233480 | tf_op jit(solution)/shard_map/ppermute | solution.py:337
  13.0 5.4 %collective-permute-start.3 = (f32[19,8,128]{2,1,0:T(8,128)S(1)}, f32[19,8,128]{2,1,0:T(8,128)S(1)}, u32[]{:S(2)}, u32[]{:S(2)}) collective-permute-start(f32[19,8,128]{2,1,0:T(8,128)S(1)} %add_add_fusion.refs_0_), channel_id=1, source_target_pairs={{0,16},{4,20},{8,24},{12,28},{16,0},{20,4},{24,8},{28,12},{1,17},{... | collective-permute-start | bytes 233480 | tf_op jit(solution)/shard_map/ppermute | solution.py:337
  18.5 5.4 %collective-permute-start.6 = (f32[20,8,128]{2,1,0:T(8,128)S(1)}, f32[20,8,128]{2,1,0:T(8,128)S(1)}, u32[]{:S(2)}, u32[]{:S(2)}) collective-permute-start(f32[20,8,128]{2,1,0:T(8,128)S(1)} %add_with_gram.1.rest_0_), channel_id=1, source_target_pairs={{0,12},{4,8},{8,4},{12,0},{16,28},{20,24},{24,20},{28,16},{1,13},{... | collective-permute-start | bytes 245768 | tf_op jit(solution)/shard_map/ppermute | solution.py:337
  20.4 4.4 %collective-permute-start.5 = (f32[20,8,128]{2,1,0:T(8,128)S(1)}, f32[20,8,128]{2,1,0:T(8,128)S(1)}, u32[]{:S(2)}, u32[]{:S(2)}) collective-permute-start(f32[20,8,128]{2,1,0:T(8,128)S(1)} %add_with_gram.1.rest_0_), channel_id=1, source_target_pairs={{0,8},{4,12},{8,0},{12,4},{16,24},{20,28},{24,16},{28,20},{1,9},{5... | collective-permute-start | bytes 245768 | tf_op jit(solution)/shard_map/ppermute | solution.py:337
  21.0 4.4 %collective-permute-start.4 = (f32[20,8,128]{2,1,0:T(8,128)S(1)}, f32[20,8,128]{2,1,0:T(8,128)S(1)}, u32[]{:S(2)}, u32[]{:S(2)}) collective-permute-start(f32[20,8,128]{2,1,0:T(8,128)S(1)} %add_with_gram.1.rest_0_), channel_id=1, source_target_pairs={{0,4},{4,0},{8,12},{12,8},{16,20},{20,16},{24,28},{28,24},{1,5},{5... | collective-permute-start | bytes 245768 | tf_op jit(solution)/shard_map/ppermute | solution.py:337
  26.5 2.5 %collective-permute-start.7 = (f32[17,8,128]{2,1,0:T(8,128)S(1)}, f32[17,8,128]{2,1,0:T(8,128)S(1)}, u32[]{:S(2)}, u32[]{:S(2)}) collective-permute-start(f32[17,8,128]{2,1,0:T(8,128)S(1)} %get-tuple-element.19), channel_id=1, source_target_pairs={{0,1},{1,0},{2,3},{3,2},{4,5},{5,4},{6,7},{7,6},{8,9},{9,8},{10,11... | collective-permute-start | bytes 208904 | tf_op jit(solution)/shard_map/ppermute | solution.py:337
  26.6 4.8 %collective-permute-start.8 = (f32[17,8,128]{2,1,0:T(8,128)S(1)}, f32[17,8,128]{2,1,0:T(8,128)S(1)}, u32[]{:S(2)}, u32[]{:S(2)}) collective-permute-start(f32[17,8,128]{2,1,0:T(8,128)S(1)} %get-tuple-element.20), channel_id=1, source_target_pairs={{0,2},{1,3},{2,0},{3,1},{4,6},{5,7},{6,4},{7,5},{8,10},{9,11},{10,... | collective-permute-start | bytes 208904 | tf_op jit(solution)/shard_map/ppermute | solution.py:337
  27.9 4.5 %collective-permute-start.9 = (f32[17,8,128]{2,1,0:T(8,128)S(1)}, f32[17,8,128]{2,1,0:T(8,128)S(1)}, u32[]{:S(2)}, u32[]{:S(2)}) collective-permute-start(f32[17,8,128]{2,1,0:T(8,128)S(1)} %get-tuple-element.21), channel_id=1, source_target_pairs={{0,3},{1,2},{2,1},{3,0},{4,7},{5,6},{6,5},{7,4},{8,11},{9,10},{10,... | collective-permute-start | bytes 208904 | tf_op jit(solution)/shard_map/ppermute | solution.py:337

commit v4 on v2

--- a/solution.py
+++ b/solution.py
@@ -7,10 +7,12 @@
 from jax.experimental.pallas import tpu as pltpu
 from jax.sharding import PartitionSpec as P
 
+
 LANES = 128
 STEP = 2 * LANES
 QUAD = 4
 PROBES = 4
+FAR, NEAR = 3, (2, 1, 0)
 SPLITS = 3
 
 
@@ -59,81 +61,103 @@
     return (step * STEP) // plan.per_line
 
 
-def sketch_kernel(plan, blocks_ref, probes_ref, *rest):
-    outs, kept_ref, held_ref, lhs_ref, held_sem, sems = rest[:QUAD], *rest[QUAD:]
-    me = lax.axis_index("param") & (QUAD - 1)
-    main = plan.quarter - 1
-    order = [k for k in range(1, QUAD)] + [0]
-
-    def copies(k):
-        first = (me ^ k) * plan.quarter
-        tail = jnp.minimum(first + main, plan.steps - 1)
-        return (
-            pltpu.make_async_copy(
-                blocks_ref.at[pl.ds(pl.multiple_of(first * STEP, STEP), main * STEP)],
-                kept_ref.at[k, pl.ds(0, main * STEP)],
-                sems.at[k, 0],
-            ),
-            pltpu.make_async_copy(
-                blocks_ref.at[pl.ds(pl.multiple_of(tail * STEP, STEP), STEP)],
-                kept_ref.at[k, pl.ds(main * STEP, STEP)],
-                sems.at[k, 1],
-            ),
-        )
-
-    load = pltpu.make_async_copy(probes_ref, held_ref, held_sem)
-    load.start()
-    for k in order:
-        for copy in copies(k):
-            copy.start()
-    load.wait()
-    held = plan.lines * 2 * PROBES
-    lhs_ref[pl.ds(0, held)] = held_ref[...].astype(jnp.float32)
-    lhs_ref[pl.ds(held, 8)] = jnp.zeros((8, LANES), jnp.float32)
+def sketch_steps(plan, k, block_at, lhs_ref, out_ref):
+    first = (lax.axis_index("param") & (QUAD - 1) ^ k) * plan.quarter
     low = row_of() < 4
     even = lane_of() % 2 == 0
     column = lane_of((8, STEP))
-    for k in order:
-        for copy in copies(k):
-            copy.wait()
-        first = (me ^ k) * plan.quarter
-
-        def body(t, _, k=k, first=first):
-            step = first + t
-            line = first_line(plan, jnp.minimum(step, plan.steps - 1))
-            probe = lhs_ref[pl.ds(pl.multiple_of(line * 8, 8), 16)].astype(jnp.bfloat16)
-            block = kept_ref[k, pl.ds(pl.multiple_of(t * STEP, STEP), STEP)]
-            both = lax.dot_general(probe, block, (((1,), (1,)), ((), ())), preferred_element_type=jnp.float32)
-            place = column + step * STEP
-            own = jnp.where(place < (line + 1) * plan.per_line, both[:8], both[8:])
-            own = jnp.where(place < plan.rows, own, 0.0)
-            left, right = own[:, :LANES], own[:, LANES:]
-            direct = jnp.where(low, left, roll(right, 4, 0))
-            crossed = jnp.where(low, roll(left, 4, 0), right)
-            outs[k][t] = direct + jnp.where(even, -roll(crossed, -1, 1), roll(crossed, 1, 1))
-            return 0
-
-        lax.fori_loop(0, plan.quarter, body, 0, unroll=True)
-
-
-def sketch_terms(plan, blocks, probes):
+
+    def body(t, _):
+        step = first + t
+        used = jnp.minimum(step, plan.steps - 1)
+        line = first_line(plan, used)
+        probe = lhs_ref[pl.ds(pl.multiple_of(line * 8, 8), 16)].astype(jnp.bfloat16)
+        both = lax.dot_general(
+            probe, block_at(t, used), (((1,), (1,)), ((), ())), preferred_element_type=jnp.float32
+        )
+        place = column + step * STEP
+        own = jnp.where(place < (line + 1) * plan.per_line, both[:8], both[8:])
+        own = jnp.where(place < plan.rows, own, 0.0)
+        left, right = own[:, :LANES], own[:, LANES:]
+        direct = jnp.where(low, left, roll(right, 4, 0))
+        crossed = jnp.where(low, roll(left, 4, 0), right)
+        out_ref[t] = direct + jnp.where(even, -roll(crossed, -1, 1), roll(crossed, 1, 1))
+        return 0
+
+    lax.fori_loop(0, plan.quarter, body, 0, unroll=True)
+
+
+def spread_probes(plan, probes_ref, lhs_ref):
+    held = plan.lines * 2 * PROBES
+    lhs_ref[pl.ds(0, held)] = probes_ref[...].astype(jnp.float32)
+    lhs_ref[pl.ds(held, 8)] = jnp.zeros((8, LANES), jnp.float32)
+
+
+def far_kernel(plan, blocks_ref, probes_ref, out_ref, lhs_ref, held_ref, here_ref, sems):
+    first = (lax.axis_index("param") & (QUAD - 1) ^ FAR) * plan.quarter
+    whole = plan.quarter - 1
+    copies = []
+    for at, (start, count) in enumerate(((0, whole), (whole, 1))):
+        source = jnp.minimum(first + start, plan.steps - count)
+        copies.append(
+            pltpu.make_async_copy(
+                blocks_ref.at[pl.ds(pl.multiple_of(source * STEP, STEP), count * STEP)],
+                here_ref.at[pl.ds(start * STEP, count * STEP)],
+                sems.at[at],
+            )
+        )
+    copies.append(pltpu.make_async_copy(probes_ref, held_ref, sems.at[2]))
+    for copy in copies:
+        copy.start()
+    copies[2].wait()
+    spread_probes(plan, held_ref, lhs_ref)
+    copies[0].wait()
+    copies[1].wait()
+
+    def block_at(t, used):
+        return here_ref[pl.ds(pl.multiple_of(t * STEP, STEP), STEP)]
+
+    sketch_steps(plan, FAR, block_at, lhs_ref, out_ref)
+
+
+def near_kernel(plan, blocks_ref, lhs_ref, *outs):
+    def block_at(t, used):
+        return blocks_ref[pl.ds(pl.multiple_of(used * STEP, STEP), STEP)]
+
+    for k, out_ref in zip(NEAR, outs):
+        sketch_steps(plan, k, block_at, lhs_ref, out_ref)
+
+
+def far_terms(plan, blocks, probes):
     piece = in_vmem((plan.quarter, 8, LANES), jnp.float32)
-    kept = in_vmem((QUAD, plan.quarter * STEP, LANES), jnp.bfloat16)
-    vmem = pl.BlockSpec(memory_space=pltpu.VMEM)
-    return pl.pallas_call(
-        functools.partial(sketch_kernel, plan),
-        out_shape=[piece] * QUAD + [kept],
+    lhs = in_vmem((plan.lines * 8 + 8, LANES), jnp.float32)
+    vmem = pl.BlockSpec(memory_space=pltpu.VMEM)
+    return pl.pallas_call(
+        functools.partial(far_kernel, plan),
+        out_shape=[piece, lhs],
         in_specs=[pl.BlockSpec(memory_space=pl.ANY)] * 2,
-        out_specs=[vmem] * (QUAD + 1),
+        out_specs=[vmem] * 2,
         scratch_shapes=[
             pltpu.VMEM((plan.lines * 8, LANES), jnp.bfloat16),
-            pltpu.VMEM((plan.lines * 8 + 8, LANES), jnp.float32),
-            pltpu.SemaphoreType.DMA(()),
-            pltpu.SemaphoreType.DMA((QUAD, 2)),
+            pltpu.VMEM((plan.quarter * STEP, LANES), jnp.bfloat16),
+            pltpu.SemaphoreType.DMA((3,)),
         ],
         compiler_params=params(16),
-        name="sketch_terms",
+        name="far_terms",
     )(*[pltpu.with_memory_space_constraint(x, pltpu.HBM) for x in (blocks, probes)])
+
+
+def near_terms(plan, blocks, lhs):
+    piece = in_vmem((plan.quarter, 8, LANES), jnp.float32)
+    vmem = pl.BlockSpec(memory_space=pltpu.VMEM)
+    return pl.pallas_call(
+        functools.partial(near_kernel, plan),
+        out_shape=[piece] * len(NEAR),
+        in_specs=[vmem] * 2,
+        out_specs=[vmem] * len(NEAR),
+        compiler_params=params(16),
+        name="near_terms",
+    )(*from_vmem(blocks, lhs))
 
 
 def gram_kernel(plan, *refs):
@@ -167,7 +191,7 @@
     )(*from_vmem(*pieces))
 
 
-def adjoint_kernel(plan, kept_ref, *rest):
+def adjoint_kernel(plan, blocks_ref, *rest):
     ins, outs, acc_ref = rest[:QUAD], rest[QUAD : QUAD + plan.shards], rest[QUAD + plan.shards]
     me = lax.axis_index("param") & (QUAD - 1)
     spot = lax.axis_index("sensor")
@@ -194,7 +218,7 @@
                 terms.append(jnp.where(mine, 0.0, term))
                 value = value - term
             lhs = jnp.concatenate(terms, axis=0).astype(jnp.bfloat16)
-            block = kept_ref[k, pl.ds(pl.multiple_of(t * STEP, STEP), STEP)]
+            block = blocks_ref[pl.ds(pl.multiple_of(step * STEP, STEP), STEP)]
             got = jnp.dot(lhs, block, preferred_element_type=jnp.float32)
             here = sum(got[16 * i : 16 * i + 8] for i in range(SPLITS))
             after = sum(got[16 * i + 8 : 16 * i + 16] for i in range(SPLITS))
@@ -210,7 +234,7 @@
         outs[k][plan.shard_lines] = packed
 
 
-def adjoint_terms(plan, kept, pieces):
+def adjoint_terms(plan, blocks, pieces):
     vmem = pl.BlockSpec(memory_space=pltpu.VMEM)
     return pl.pallas_call(
         functools.partial(adjoint_kernel, plan),
@@ -220,7 +244,7 @@
         scratch_shapes=[pltpu.VMEM((plan.lines + 1, 8, LANES), jnp.float32)],
         compiler_params=params(16),
         name="adjoint_terms",
-    )(*from_vmem(kept, *pieces))
+    )(*from_vmem(blocks, *pieces))
 
 
 def by_line_kernel(plan, *rest):
@@ -336,12 +360,20 @@
 
 
 def on_device(param, sensor, blocks, probes):
+    return sketch_and_adjoint(param, sensor, blocks, probes)
+
+
+def sketch_and_adjoint(param, sensor, blocks, probes):
     lines, parts, group, nodes = blocks.shape
     plan = Plan(lines, parts, group, nodes, sensor)
     flat_blocks = blocks.transpose(0, 2, 1, 3).reshape(plan.rows, nodes)
     flat_probes = probes.reshape(lines * parts * PROBES, nodes)
-    *terms, kept = sketch_terms(plan, flat_blocks, flat_probes)
-    total = terms[0] + sum(trade(terms[k], "param", param, k) for k in range(1, QUAD))
+    far, lhs = far_terms(plan, flat_blocks, flat_probes)
+    far = trade(far, "param", param, FAR)
+    near = near_terms(plan, flat_blocks, lhs)
+    total = near[-1] + far
+    for k, piece in zip(NEAR[:-1], near):
+        total = total + trade(piece, "param", param, k)
     span = QUAD
     while span * 2 < param:
         total = total + trade(total, "param", param, span)
@@ -349,7 +381,7 @@
     sums = [total] + ([trade(total, "param", param, span)] if span < param else [])
     own = add_with_gram(plan, *sums)
     pieces = [own] + [trade(own, "param", param, k) for k in range(1, QUAD)]
-    adjoint = adjoint_terms(plan, kept, pieces)
+    adjoint = adjoint_terms(plan, flat_blocks, pieces)
     gathered = [adjoint[0]] + [trade(adjoint[k], "sensor", sensor, k) for k in range(1, sensor)]
     sketch = sketch_by_line(plan, pieces)
     basis, coeffs = finish(plan, sketch, gathered)

time: 36.2 us -> 35.4 us (0.978)
  Pallas kernels: 7.51 us -> 6.05 us
  local copies, waits for them, and re-layouts: 0 us -> 0.77 us
    pallas_call x1 -> x2, Pallas kernels: 4.65 us -> 3.18 us  [the longest x1 2.02 us: far_terms(): pl.pallas_call(functools.partial(far_kernel, plan), out_shape=[piece, lhs...]
    unnamed x0 -> x2, local copies, waits for them, and re-layouts: none -> 0.77 us
where the time goes in v4:
time: 35.4 us; the launch traced here: 35.2 us
  waiting for transfers between devices  15 us (42%)
  starting transfers between devices  12.7 us (36%)
  Pallas kernels  6.05 us (17%)
  local copies, waits for them, and re-layouts  0.77 us (2%)
  between operations  0.69 us (2%)
    ppermute x10, waiting for transfers between devices, trade(): return lax.ppermute(x, axis, [(i, i ^ k) for i in range(size)])  15 us
    ppermute x10, starting transfers between devices, trade(): return lax.ppermute(x, axis, [(i, i ^ k) for i in range(size)])  12.7 us
    pallas_call x1, Pallas kernels, far_terms(): pl.pallas_call(functools.partial(far_kernel, plan), out_shape=[piece, lhs...  2.02 us
    pallas_call x1, Pallas kernels, finish(): pl.pallas_call(functools.partial(final_kernel, plan), out_shape=[jax.Shap...  1.16 us
    pallas_call x1, Pallas kernels, near_terms(): pl.pallas_call(functools.partial(near_kernel, plan), out_shape=[piece] *...  1.16 us
    pallas_call x1, Pallas kernels, adjoint_terms(): pl.pallas_call(functools.partial(adjoint_kernel, plan), out_shape=[in_vme...  1.02 us
    unnamed x2, local copies, waits for them, and re-layouts  0.77 us
  transfers between devices with their start and end apart: 10, of which 8 were waited for; matrix products, arithmetic and copies ran while one was open for 0% of the time, Pallas kernels for 2%

profile of v4, /device:TPU:0, one launch (start us, length us, event | category | flops | bytes accessed | tf_op | source)
XLA Modules:
  0.0 35.2 jit_solution(18102182823165762701)
XLA Ops:
  0.6 2.0 %far_terms.1 = (f32[19,8,128]{2,1,0:T(8,128)S(1)}, f32[520,128]{1,0:T(8,128)S(1)}) custom-call(bf16[19200,128]{1,0:T(8,128)(2,1)} %bitcast.5, bf16[512,128]{1,0:T(8,128)(2,1)} %bitcast.8), custom_call_target="tpu_custom_call" | custom-call | tf_op jit(solution)/shard_map/far_terms/pallas_call | solution.py:135
  2.7 0.8 %copy-done = bf16[64,2,150,128]{3,1,2,0:T(2,128)(2,1)S(1)} copy-done((bf16[64,2,150,128]{3,1,2,0:T(2,128)(2,1)S(1)}, bf16[64,2,150,128]{3,1,2,0:T(2,128)(2,1)}, u32[]{:S(2)}) %copy-start) | copy-done | bytes 4915224
  3.4 1.2 %near_terms.1 = (f32[19,8,128]{2,1,0:T(8,128)S(1)}, f32[19,8,128]{2,1,0:T(8,128)S(1)}, f32[19,8,128]{2,1,0:T(8,128)S(1)}) custom-call(bf16[19200,128]{1,0:T(8,128)(2,1)S(1)} %bitcast.6, f32[520,128]{1,0:T(8,128)S(1)} %get-tuple-element.13.lhs_ref), custom_call_target="tpu_custom_call" | custom-call | tf_op jit(solution)/shard_map/near_terms/pallas_call | solution.py:153
  4.6 3.1 %collective-permute-start.1 = (f32[19,8,128]{2,1,0:T(8,128)S(1)}, f32[19,8,128]{2,1,0:T(8,128)S(1)}, u32[]{:S(2)}, u32[]{:S(2)}) collective-permute-start(f32[19,8,128]{2,1,0:T(8,128)S(1)} %get-tuple-element.16), channel_id=1, source_target_pairs={{0,8},{4,12},{8,0},{12,4},{16,24},{20,28},{24,16},{28,20},{1,9},{5... | collective-permute-start | bytes 233480 | tf_op jit(solution)/shard_map/ppermute | solution.py:359
  7.7 1.5 %collective-permute-start.2 = (f32[19,8,128]{2,1,0:T(8,128)S(1)}, f32[19,8,128]{2,1,0:T(8,128)S(1)}, u32[]{:S(2)}, u32[]{:S(2)}) collective-permute-start(f32[19,8,128]{2,1,0:T(8,128)S(1)} %get-tuple-element.17), channel_id=1, source_target_pairs={{0,4},{4,0},{8,12},{12,8},{16,20},{20,16},{24,28},{28,24},{1,5},{5... | collective-permute-start | bytes 233480 | tf_op jit(solution)/shard_map/ppermute | solution.py:359
  9.2 0.0 collective-permute-start
  9.2 1.1 %collective-permute-done.1 = f32[19,8,128]{2,1,0:T(8,128)S(1)} collective-permute-done((f32[19,8,128]{2,1,0:T(8,128)S(1)}, f32[19,8,128]{2,1,0:T(8,128)S(1)}, u32[]{:S(2)}, u32[]{:S(2)}) %collective-permute-start.1) | collective-permute-done | bytes 77856 | tf_op jit(solution)/shard_map/ppermute | solution.py:359
  10.3 2.6 %collective-permute-done.2 = f32[19,8,128]{2,1,0:T(8,128)S(1)} collective-permute-done((f32[19,8,128]{2,1,0:T(8,128)S(1)}, f32[19,8,128]{2,1,0:T(8,128)S(1)}, u32[]{:S(2)}, u32[]{:S(2)}) %collective-permute-start.2) | collective-permute-done | bytes 77856 | tf_op jit(solution)/shard_map/ppermute | solution.py:359
  12.9 1.6 %collective-permute-done = f32[19,8,128]{2,1,0:T(8,128)S(1)} collective-permute-done((f32[19,8,128]{2,1,0:T(8,128)S(1)}, f32[19,8,128]{2,1,0:T(8,128)S(1)}, u32[]{:S(2)}, u32[]{:S(2)}) %collective-permute-start) | collective-permute-done | bytes 77856 | tf_op jit(solution)/shard_map/ppermute | solution.py:359
  14.5 2.7 %collective-permute-start.3 = (f32[19,8,128]{2,1,0:T(8,128)S(1)}, f32[19,8,128]{2,1,0:T(8,128)S(1)}, u32[]{:S(2)}, u32[]{:S(2)}) collective-permute-start(f32[19,8,128]{2,1,0:T(8,128)S(1)} %add_add_fusion.refs_0_), channel_id=1, source_target_pairs={{0,16},{4,20},{8,24},{12,28},{16,0},{20,4},{24,8},{28,12},{1,17},{... | collective-permute-start | bytes 233480 | tf_op jit(solution)/shard_map/ppermute | solution.py:359
  17.2 3.5 %collective-permute-done.3.refs_1_ = f32[19,8,128]{2,1,0:T(8,128)S(1)} collective-permute-done((f32[19,8,128]{2,1,0:T(8,128)S(1)}, f32[19,8,128]{2,1,0:T(8,128)S(1)}, u32[]{:S(2)}, u32[]{:S(2)}) %collective-permute-start.3) | collective-permute-done | bytes 77856 | tf_op jit(solution)/shard_map/ppermute | solution.py:359
  20.7 0.1 add_with_gram.1.rest_0_
  20.8 1.9 %collective-permute-start.5 = (f32[20,8,128]{2,1,0:T(8,128)S(1)}, f32[20,8,128]{2,1,0:T(8,128)S(1)}, u32[]{:S(2)}, u32[]{:S(2)}) collective-permute-start(f32[20,8,128]{2,1,0:T(8,128)S(1)} %add_with_gram.1.rest_0_), channel_id=1, source_target_pairs={{0,8},{4,12},{8,0},{12,4},{16,24},{20,28},{24,16},{28,20},{1,9},{5... | collective-permute-start | bytes 245768 | tf_op jit(solution)/shard_map/ppermute | solution.py:359
  22.8 1.5 %collective-permute-start.4 = (f32[20,8,128]{2,1,0:T(8,128)S(1)}, f32[20,8,128]{2,1,0:T(8,128)S(1)}, u32[]{:S(2)}, u32[]{:S(2)}) collective-permute-start(f32[20,8,128]{2,1,0:T(8,128)S(1)} %add_with_gram.1.rest_0_), channel_id=1, source_target_pairs={{0,4},{4,0},{8,12},{12,8},{16,20},{20,16},{24,28},{28,24},{1,5},{5... | collective-permute-start | bytes 245768 | tf_op jit(solution)/shard_map/ppermute | solution.py:359
  24.3 1.9 %collective-permute-done.6.rest_3_ = f32[20,8,128]{2,1,0:T(8,128)S(1)} collective-permute-done((f32[20,8,128]{2,1,0:T(8,128)S(1)}, f32[20,8,128]{2,1,0:T(8,128)S(1)}, u32[]{:S(2)}, u32[]{:S(2)}) %collective-permute-start.6) | collective-permute-done | bytes 81952 | tf_op jit(solution)/shard_map/ppermute | solution.py:359
  26.2 1.0 %collective-permute-done.4.rest_1_ = f32[20,8,128]{2,1,0:T(8,128)S(1)} collective-permute-done((f32[20,8,128]{2,1,0:T(8,128)S(1)}, f32[20,8,128]{2,1,0:T(8,128)S(1)}, u32[]{:S(2)}, u32[]{:S(2)}) %collective-permute-start.4) | collective-permute-done | bytes 81952 | tf_op jit(solution)/shard_map/ppermute | solution.py:359
  27.2 1.0 %adjoint_terms.1 = (f32[17,8,128]{2,1,0:T(8,128)S(1)}, f32[17,8,128]{2,1,0:T(8,128)S(1)}, f32[17,8,128]{2,1,0:T(8,128)S(1)}, f32[17,8,128]{2,1,0:T(8,128)S(1)}) custom-call(bf16[19200,128]{1,0:T(8,128)(2,1)S(1)} %bitcast.7, f32[20,8,128]{2,1,0:T(8,128)S(1)} %add_with_gram.1.rest_0_, f32[20,8,128]{2,1,0:T(8,128)S(1)} %collective-permute-done.4.rest_1_, ...), custom_call_target="tpu_custom_call" | custom-call | tf_op jit(solution)/shard_map/adjoint_terms/pallas_call | solution.py:239
  28.2 0.1 collective-permute-start.7
  28.3 1.6 %collective-permute-start.8 = (f32[17,8,128]{2,1,0:T(8,128)S(1)}, f32[17,8,128]{2,1,0:T(8,128)S(1)}, u32[]{:S(2)}, u32[]{:S(2)}) collective-permute-start(f32[17,8,128]{2,1,0:T(8,128)S(1)} %get-tuple-element.20), channel_id=1, source_target_pairs={{0,2},{1,3},{2,0},{3,1},{4,6},{5,7},{6,4},{7,5},{8,10},{9,11},{10,... | collective-permute-start | bytes 208904 | tf_op jit(solution)/shard_map/ppermute | solution.py:359
  29.9 0.3 collective-permute-start.9
  30.2 0.6 %sketch_by_line.1.sketch_ref = f32[64,8,150]{2,1,0:T(8,128)S(1)} custom-call(f32[20,8,128]{2,1,0:T(8,128)S(1)} %add_with_gram.1.rest_0_, f32[20,8,128]{2,1,0:T(8,128)S(1)} %collective-permute-done.4.rest_1_, f32[20,8,128]{2,1,0:T(8,128)S(1)} %collective-permute-done.5.rest_2_, f32[20,8,128]{2,1,0:T(8,128)S(1)} %collective-permute-done.6.rest_3_), custom_call_target="tpu_custom_call" | custom-call | tf_op jit(solution)/shard_map/sketch_by_line/pallas_call | solution.py:274
  30.8 2.2 %collective-permute-done.8.rest_2_ = f32[17,8,128]{2,1,0:T(8,128)S(1)} collective-permute-done((f32[17,8,128]{2,1,0:T(8,128)S(1)}, f32[17,8,128]{2,1,0:T(8,128)S(1)}, u32[]{:S(2)}, u32[]{:S(2)}) %collective-permute-start.8) | collective-permute-done | bytes 69664 | tf_op jit(solution)/shard_map/ppermute | solution.py:359
  32.9 1.2 %collective-permute-done.9.rest_3_ = f32[17,8,128]{2,1,0:T(8,128)S(1)} collective-permute-done((f32[17,8,128]{2,1,0:T(8,128)S(1)}, f32[17,8,128]{2,1,0:T(8,128)S(1)}, u32[]{:S(2)}, u32[]{:S(2)}) %collective-permute-start.9) | collective-permute-done | bytes 69664 | tf_op jit(solution)/shard_map/ppermute | solution.py:359
  34.1 1.2 %finish.1 = (f32[64,2,4,150]{3,2,1,0:T(4,128)}, bf16[128,128]{1,0:T(8,128)(2,1)}) custom-call(f32[64,8,150]{2,1,0:T(8,128)S(1)} %sketch_by_line.1.sketch_ref, f32[17,8,128]{2,1,0:T(8,128)S(1)} %get-tuple-element.18.rest_0_, f32[17,8,128]{2,1,0:T(8,128)S(1)} %collective-permute-done.7.rest_1_, f32[17,8,128]{2,1,0:T(8,128)S(1)} %collective-permute-done.8.rest_2_, ...), custom_call_target="tpu_custom_call" | custom-call | tf_op jit(solution)/shard_map/finish/pallas_call | solution.py:345
  (5 shorter events, 0.0 us)
Async XLA Ops:
  0.6 2.8 %copy-start = (bf16[64,2,150,128]{3,1,2,0:T(2,128)(2,1)S(1)}, bf16[64,2,150,128]{3,1,2,0:T(2,128)(2,1)}, u32[]{:S(2)}) copy-start(bf16[64,2,150,128]{3,1,2,0:T(2,128)(2,1)} %param.2) | copy-start | bytes 14745604
  4.6 5.7 %collective-permute-start.1 = (f32[19,8,128]{2,1,0:T(8,128)S(1)}, f32[19,8,128]{2,1,0:T(8,128)S(1)}, u32[]{:S(2)}, u32[]{:S(2)}) collective-permute-start(f32[19,8,128]{2,1,0:T(8,128)S(1)} %get-tuple-element.16), channel_id=1, source_target_pairs={{0,8},{4,12},{8,0},{12,4},{16,24},{20,28},{24,16},{28,20},{1,9},{5... | collective-permute-start | bytes 233480 | tf_op jit(solution)/shard_map/ppermute | solution.py:359
  7.7 5.2 %collective-permute-start.2 = (f32[19,8,128]{2,1,0:T(8,128)S(1)}, f32[19,8,128]{2,1,0:T(8,128)S(1)}, u32[]{:S(2)}, u32[]{:S(2)}) collective-permute-start(f32[19,8,128]{2,1,0:T(8,128)S(1)} %get-tuple-element.17), channel_id=1, source_target_pairs={{0,4},{4,0},{8,12},{12,8},{16,20},{20,16},{24,28},{28,24},{1,5},{5... | collective-permute-start | bytes 233480 | tf_op jit(solution)/shard_map/ppermute | solution.py:359
  9.2 5.3 %collective-permute-start = (f32[19,8,128]{2,1,0:T(8,128)S(1)}, f32[19,8,128]{2,1,0:T(8,128)S(1)}, u32[]{:S(2)}, u32[]{:S(2)}) collective-permute-start(f32[19,8,128]{2,1,0:T(8,128)S(1)} %get-tuple-element.15), channel_id=1, source_target_pairs={{0,12},{4,8},{8,4},{12,0},{16,28},{20,24},{24,20},{28,16},{1,13},{... | collective-permute-start | bytes 233480 | tf_op jit(solution)/shard_map/ppermute | solution.py:359
  14.5 6.2 %collective-permute-start.3 = (f32[19,8,128]{2,1,0:T(8,128)S(1)}, f32[19,8,128]{2,1,0:T(8,128)S(1)}, u32[]{:S(2)}, u32[]{:S(2)}) collective-permute-start(f32[19,8,128]{2,1,0:T(8,128)S(1)} %add_add_fusion.refs_0_), channel_id=1, source_target_pairs={{0,16},{4,20},{8,24},{12,28},{16,0},{20,4},{24,8},{28,12},{1,17},{... | collective-permute-start | bytes 233480 | tf_op jit(solution)/shard_map/ppermute | solution.py:359
  20.8 5.3 %collective-permute-start.6 = (f32[20,8,128]{2,1,0:T(8,128)S(1)}, f32[20,8,128]{2,1,0:T(8,128)S(1)}, u32[]{:S(2)}, u32[]{:S(2)}) collective-permute-start(f32[20,8,128]{2,1,0:T(8,128)S(1)} %add_with_gram.1.rest_0_), channel_id=1, source_target_pairs={{0,12},{4,8},{8,4},{12,0},{16,28},{20,24},{24,20},{28,16},{1,13},{... | collective-permute-start | bytes 245768 | tf_op jit(solution)/shard_map/ppermute | solution.py:359
  20.8 5.3 %collective-permute-start.5 = (f32[20,8,128]{2,1,0:T(8,128)S(1)}, f32[20,8,128]{2,1,0:T(8,128)S(1)}, u32[]{:S(2)}, u32[]{:S(2)}) collective-permute-start(f32[20,8,128]{2,1,0:T(8,128)S(1)} %add_with_gram.1.rest_0_), channel_id=1, source_target_pairs={{0,8},{4,12},{8,0},{12,4},{16,24},{20,28},{24,16},{28,20},{1,9},{5... | collective-permute-start | bytes 245768 | tf_op jit(solution)/shard_map/ppermute | solution.py:359
  22.8 4.4 %collective-permute-start.4 = (f32[20,8,128]{2,1,0:T(8,128)S(1)}, f32[20,8,128]{2,1,0:T(8,128)S(1)}, u32[]{:S(2)}, u32[]{:S(2)}) collective-permute-start(f32[20,8,128]{2,1,0:T(8,128)S(1)} %add_with_gram.1.rest_0_), channel_id=1, source_target_pairs={{0,4},{4,0},{8,12},{12,8},{16,20},{20,16},{24,28},{28,24},{1,5},{5... | collective-permute-start | bytes 245768 | tf_op jit(solution)/shard_map/ppermute | solution.py:359
  28.2 2.5 %collective-permute-start.7 = (f32[17,8,128]{2,1,0:T(8,128)S(1)}, f32[17,8,128]{2,1,0:T(8,128)S(1)}, u32[]{:S(2)}, u32[]{:S(2)}) collective-permute-start(f32[17,8,128]{2,1,0:T(8,128)S(1)} %get-tuple-element.19), channel_id=1, source_target_pairs={{0,1},{1,0},{2,3},{3,2},{4,5},{5,4},{6,7},{7,6},{8,9},{9,8},{10,11... | collective-permute-start | bytes 208904 | tf_op jit(solution)/shard_map/ppermute | solution.py:359
  28.3 4.6 %collective-permute-start.8 = (f32[17,8,128]{2,1,0:T(8,128)S(1)}, f32[17,8,128]{2,1,0:T(8,128)S(1)}, u32[]{:S(2)}, u32[]{:S(2)}) collective-permute-start(f32[17,8,128]{2,1,0:T(8,128)S(1)} %get-tuple-element.20), channel_id=1, source_target_pairs={{0,2},{1,3},{2,0},{3,1},{4,6},{5,7},{6,4},{7,5},{8,10},{9,11},{10,... | collective-permute-start | bytes 208904 | tf_op jit(solution)/shard_map/ppermute | solution.py:359
  29.9 4.2 %collective-permute-start.9 = (f32[17,8,128]{2,1,0:T(8,128)S(1)}, f32[17,8,128]{2,1,0:T(8,128)S(1)}, u32[]{:S(2)}, u32[]{:S(2)}) collective-permute-start(f32[17,8,128]{2,1,0:T(8,128)S(1)} %get-tuple-element.21), channel_id=1, source_target_pairs={{0,3},{1,2},{2,1},{3,0},{4,7},{5,6},{6,5},{7,4},{8,11},{9,10},{10,... | collective-permute-start | bytes 208904 | tf_op jit(solution)/shard_map/ppermute | solution.py:359

commit v5 on v3

--- a/solution.py
+++ b/solution.py
@@ -7,11 +7,13 @@
 from jax.experimental.pallas import tpu as pltpu
 from jax.sharding import PartitionSpec as P
 
+
 LANES = 128
 STEP = 2 * LANES
 QUAD = 4
 PROBES = 4
-ARRIVALS = ((3, 2), (1, 0))
+ARRIVALS = ((3, 2), (1,))
+REDUCE, GATHER = (3, 2, 1), (3, 2, 1)
 URGENCY = (0, 1)
 SPLITS = 3
 
@@ -61,81 +63,114 @@
     return (step * STEP) // plan.per_line
 
 
-def sketch_kernel(plan, blocks_ref, probes_ref, *rest):
-    outs, kept_ref, held_ref, lhs_ref, held_sem, sems = rest[:QUAD], *rest[QUAD:]
-    me = lax.axis_index("param") & (QUAD - 1)
+def quarter_copies(plan, k, blocks_ref, kept_ref, sems):
+    first = (lax.axis_index("param") & (QUAD - 1) ^ k) * plan.quarter
     whole = plan.quarter - 1
-
-    def copies(k):
-        first = (me ^ k) * plan.quarter
-        found = []
-        for at, (start, count) in enumerate(((0, whole), (whole, 1))):
-            source = jnp.minimum(first + start, plan.steps - count)
-            found.append(
-                pltpu.make_async_copy(
-                    blocks_ref.at[pl.ds(pl.multiple_of(source * STEP, STEP), count * STEP)],
-                    kept_ref.at[k, pl.ds(start * STEP, count * STEP)],
-                    sems.at[k, at],
-                )
+    found = []
+    for at, (start, count) in enumerate(((0, whole), (whole, 1))):
+        source = jnp.minimum(first + start, plan.steps - count)
+        found.append(
+            pltpu.make_async_copy(
+                blocks_ref.at[pl.ds(pl.multiple_of(source * STEP, STEP), count * STEP)],
+                kept_ref.at[pl.ds(start * STEP, count * STEP)],
+                sems.at[at],
             )
-        return found
-
+        )
+    return found
+
+
+def quarter_terms(plan, k, kept_ref, lhs_ref, out_ref):
+    first = (lax.axis_index("param") & (QUAD - 1) ^ k) * plan.quarter
+    low = row_of() < 4
+    even = lane_of() % 2 == 0
+    column = lane_of((8, STEP))
+
+    def body(t, _):
+        step = first + t
+        line = first_line(plan, jnp.minimum(step, plan.steps - 1))
+        probe = lhs_ref[pl.ds(pl.multiple_of(line * 8, 8), 16)].astype(jnp.bfloat16)
+        block = kept_ref[pl.ds(pl.multiple_of(t * STEP, STEP), STEP)]
+        both = lax.dot_general(probe, block, (((1,), (1,)), ((), ())), preferred_element_type=jnp.float32)
+        place = column + step * STEP
+        own = jnp.where(place < (line + 1) * plan.per_line, both[:8], both[8:])
+        own = jnp.where(place < plan.rows, own, 0.0)
+        left, right = own[:, :LANES], own[:, LANES:]
+        direct = jnp.where(low, left, roll(right, 4, 0))
+        crossed = jnp.where(low, roll(left, 4, 0), right)
+        out_ref[t] = direct + jnp.where(even, -roll(crossed, -1, 1), roll(crossed, 1, 1))
+        return 0
+
+    lax.fori_loop(0, plan.quarter, body, 0, unroll=True)
+
+
+def sent_kernel(plan, blocks_ref, probes_ref, *rest):
+    count = QUAD - 1
+    outs, kepts, (lhs_ref, held_ref, held_sem, sems) = rest[:count], rest[count : 2 * count], rest[2 * count :]
     load = pltpu.make_async_copy(probes_ref, held_ref, held_sem)
     load.start()
+    copies = {k: quarter_copies(plan, k, blocks_ref, kept_ref, sems.at[k]) for k, kept_ref in zip(REDUCE, kepts)}
     for order, group in enumerate(ARRIVALS):
         for k in group:
-            for copy in copies(k):
+            for copy in copies[k]:
                 copy.start(priority=URGENCY[order])
     load.wait()
     held = plan.lines * 2 * PROBES
     lhs_ref[pl.ds(0, held)] = held_ref[...].astype(jnp.float32)
     lhs_ref[pl.ds(held, 8)] = jnp.zeros((8, LANES), jnp.float32)
-    low_rows = row_of() < 4
-    even = lane_of() % 2 == 0
-    column = lane_of((8, STEP))
     for group in ARRIVALS:
         for k in group:
-            for copy in copies(k):
+            for copy in copies[k]:
                 copy.wait()
         for k in group:
-            first = (me ^ k) * plan.quarter
-
-            def body(t, _, k=k, first=first):
-                step = first + t
-                line = first_line(plan, jnp.minimum(step, plan.steps - 1))
-                probe = lhs_ref[pl.ds(pl.multiple_of(line * 8, 8), 16)].astype(jnp.bfloat16)
-                block = kept_ref[k, pl.ds(pl.multiple_of(t * STEP, STEP), STEP)]
-                both = lax.dot_general(probe, block, (((1,), (1,)), ((), ())), preferred_element_type=jnp.float32)
-                place = column + step * STEP
-                own = jnp.where(place < (line + 1) * plan.per_line, both[:8], both[8:])
-                own = jnp.where(place < plan.rows, own, 0.0)
-                left, right = own[:, :LANES], own[:, LANES:]
-                direct = jnp.where(low_rows, left, roll(right, 4, 0))
-                crossed = jnp.where(low_rows, roll(left, 4, 0), right)
-                outs[k][t] = direct + jnp.where(even, -roll(crossed, -1, 1), roll(crossed, 1, 1))
-                return 0
-
-            lax.fori_loop(0, plan.quarter, body, 0, unroll=True)
+            at = REDUCE.index(k)
+            quarter_terms(plan, k, kepts[at], lhs_ref, outs[at])
+
+
+def own_kernel(plan, blocks_ref, lhs_ref, out_ref, kept_ref, sems):
+    copies = quarter_copies(plan, 0, blocks_ref, kept_ref, sems)
+    for copy in copies:
+        copy.start()
+    for copy in copies:
+        copy.wait()
+    quarter_terms(plan, 0, kept_ref, lhs_ref, out_ref)
 
 
 def sketch_terms(plan, blocks, probes):
     piece = in_vmem((plan.quarter, 8, LANES), jnp.float32)
-    kept = in_vmem((QUAD, plan.quarter * STEP, LANES), jnp.bfloat16)
-    vmem = pl.BlockSpec(memory_space=pltpu.VMEM)
-    return pl.pallas_call(
-        functools.partial(sketch_kernel, plan),
-        out_shape=[piece] * QUAD + [kept],
+    kept = in_vmem((plan.quarter * STEP, LANES), jnp.bfloat16)
+    lhs = in_vmem((plan.lines * 8 + 8, LANES), jnp.float32)
+    vmem = pl.BlockSpec(memory_space=pltpu.VMEM)
+    count = QUAD - 1
+    out = pl.pallas_call(
+        functools.partial(sent_kernel, plan),
+        out_shape=[piece] * count + [kept] * count + [lhs],
         in_specs=[pl.BlockSpec(memory_space=pl.ANY)] * 2,
-        out_specs=[vmem] * (QUAD + 1),
+        out_specs=[vmem] * (2 * count + 1),
         scratch_shapes=[
             pltpu.VMEM((plan.lines * 8, LANES), jnp.bfloat16),
-            pltpu.VMEM((plan.lines * 8 + 8, LANES), jnp.float32),
             pltpu.SemaphoreType.DMA(()),
             pltpu.SemaphoreType.DMA((QUAD, 2)),
         ],
         compiler_params=params(16),
-        name="sketch_terms",
+        name="sent_terms",
     )(*[pltpu.with_memory_space_constraint(x, pltpu.HBM) for x in (blocks, probes)])
+    return dict(zip(REDUCE, out[:count])), dict(zip(REDUCE, out[count:-1])), out[-1]
+
+
+def own_terms(plan, blocks, lhs):
+    vmem = pl.BlockSpec(memory_space=pltpu.VMEM)
+    return pl.pallas_call(
+        functools.partial(own_kernel, plan),
+        out_shape=[
+            in_vmem((plan.quarter, 8, LANES), jnp.float32),
+            in_vmem((plan.quarter * STEP, LANES), jnp.bfloat16),
+        ],
+        in_specs=[pl.BlockSpec(memory_space=pl.ANY), vmem],
+        out_specs=[vmem] * 2,
+        scratch_shapes=[pltpu.SemaphoreType.DMA((2,))],
+        compiler_params=params(16),
+        name="own_terms",
+    )(pltpu.with_memory_space_constraint(blocks, pltpu.HBM), *from_vmem(lhs))
 
 
 def gram_kernel(plan, *refs):
@@ -169,21 +204,22 @@
     )(*from_vmem(*pieces))
 
 
-def adjoint_kernel(plan, kept_ref, *rest):
-    ins, outs, acc_ref = rest[:QUAD], rest[QUAD : QUAD + plan.shards], rest[QUAD + plan.shards]
-    me = lax.axis_index("param") & (QUAD - 1)
-    spot = lax.axis_index("sensor")
+def adjoint_kernel(plan, distances, count, *refs):
+    ins, kepts, rest = refs[:count], refs[count : 2 * count], refs[2 * count :]
+    earlier = rest[0] if len(rest) > 1 else None
+    acc_ref = rest[-1]
+    param = lax.axis_index("param")
     low = row_of() < 4
     even = lane_of() % 2 == 0
     column = lane_of((8, STEP))
     acc_ref[...] = jnp.zeros(acc_ref.shape, jnp.float32)
-    for k in range(QUAD):
-        first = (me ^ k) * plan.quarter
-
-        def body(t, _, k=k, first=first):
+    for k, in_ref, kept_ref in zip(distances, ins, kepts):
+        first = (param & (QUAD - 1) ^ k) * plan.quarter
+
+        def body(t, _, first=first, in_ref=in_ref, kept_ref=kept_ref):
             step = jnp.minimum(first + t, plan.steps - 1)
             line = first_line(plan, step)
-            x = ins[k][t]
+            x = in_ref[t]
             y = jnp.where(even, roll(x, -1, 1), -roll(x, 1, 1))
             left = jnp.where(low, x, roll(y, 4, 0))
             right = jnp.where(low, roll(x, 4, 0), y)
@@ -196,7 +232,7 @@
                 terms.append(jnp.where(mine, 0.0, term))
                 value = value - term
             lhs = jnp.concatenate(terms, axis=0).astype(jnp.bfloat16)
-            block = kept_ref[k, pl.ds(pl.multiple_of(t * STEP, STEP), STEP)]
+            block = kept_ref[pl.ds(pl.multiple_of(t * STEP, STEP), STEP)]
             got = jnp.dot(lhs, block, preferred_element_type=jnp.float32)
             here = sum(got[16 * i : 16 * i + 8] for i in range(SPLITS))
             after = sum(got[16 * i + 8 : 16 * i + 16] for i in range(SPLITS))
@@ -206,23 +242,33 @@
 
         lax.fori_loop(0, plan.quarter, body, 0, unroll=True)
     packed = sum(ref[plan.quarter] for ref in ins)
-    for k in range(plan.shards):
-        start = (spot ^ k) * plan.shard_lines
-        outs[k][pl.ds(0, plan.shard_lines)] = acc_ref[pl.ds(start, plan.shard_lines)]
-        outs[k][plan.shard_lines] = packed
-
-
-def adjoint_terms(plan, kept, pieces):
-    vmem = pl.BlockSpec(memory_space=pltpu.VMEM)
+    if earlier is None:
+        acc_ref[plan.lines] = packed
+        return
+    packed = packed + earlier[plan.lines]
+    spot = lax.axis_index("sensor")
+    for k, out_ref in enumerate(rest[1:-1]):
+        lines = pl.ds((spot ^ k) * plan.shard_lines, plan.shard_lines)
+        out_ref[pl.ds(0, plan.shard_lines)] = acc_ref[lines] + earlier[lines]
+        out_ref[plan.shard_lines] = packed
+
+
+def adjoint_terms(plan, distances, pieces, kept, earlier=None):
+    vmem = pl.BlockSpec(memory_space=pltpu.VMEM)
+    whole = in_vmem((plan.lines + 1, 8, LANES), jnp.float32)
+    shard = in_vmem((plan.shard_lines + 1, 8, LANES), jnp.float32)
+    given = [pieces[k] for k in distances] + [kept[k] for k in distances]
+    if earlier is not None:
+        given.append(earlier)
     return pl.pallas_call(
-        functools.partial(adjoint_kernel, plan),
-        out_shape=[in_vmem((plan.shard_lines + 1, 8, LANES), jnp.float32)] * plan.shards,
-        in_specs=[vmem] * (1 + QUAD),
-        out_specs=[vmem] * plan.shards,
-        scratch_shapes=[pltpu.VMEM((plan.lines + 1, 8, LANES), jnp.float32)],
-        compiler_params=params(16),
-        name="adjoint_terms",
-    )(*from_vmem(kept, *pieces))
+        functools.partial(adjoint_kernel, plan, distances, len(distances)),
+        out_shape=whole if earlier is None else [shard] * plan.shards,
+        in_specs=[vmem] * len(given),
+        out_specs=vmem if earlier is None else [vmem] * plan.shards,
+        scratch_shapes=[] if earlier is None else [whole],
+        compiler_params=params(16),
+        name="adjoint_first" if earlier is None else "adjoint_rest",
+    )(*from_vmem(*given))
 
 
 def by_line_kernel(plan, *rest):
@@ -337,13 +383,15 @@
     return lax.ppermute(x, axis, [(i, i ^ k) for i in range(size)])
 
 
-def on_device(param, sensor, blocks, probes):
+def sketch_and_adjoint(param, sensor, blocks, probes):
     lines, parts, group, nodes = blocks.shape
     plan = Plan(lines, parts, group, nodes, sensor)
     flat_blocks = blocks.transpose(0, 2, 1, 3).reshape(plan.rows, nodes)
     flat_probes = probes.reshape(lines * parts * PROBES, nodes)
-    *terms, kept = sketch_terms(plan, flat_blocks, flat_probes)
-    total = terms[0] + sum(trade(terms[k], "param", param, k) for k in reversed(range(1, QUAD)))
+    terms, kept, lhs = sketch_terms(plan, flat_blocks, flat_probes)
+    total, kept[0] = own_terms(plan, flat_blocks, lhs)
+    for k in REDUCE:
+        total = total + trade(terms[k], "param", param, k)
     span = QUAD
     while span * 2 < param:
         total = total + trade(total, "param", param, span)
@@ -351,11 +399,16 @@
     sums = [total] + ([trade(total, "param", param, span)] if span < param else [])
     own = add_with_gram(plan, *sums)
     pieces = [own] + [trade(own, "param", param, k) for k in range(1, QUAD)]
-    adjoint = adjoint_terms(plan, kept, pieces)
+    adjoint = adjoint_terms(plan, (0, GATHER[0]), pieces, kept)
+    adjoint = adjoint_terms(plan, GATHER[1:], pieces, kept, adjoint)
     gathered = [adjoint[0]] + [trade(adjoint[k], "sensor", sensor, k) for k in range(1, sensor)]
     sketch = sketch_by_line(plan, pieces)
     basis, coeffs = finish(plan, sketch, gathered)
     return basis, coeffs.reshape(plan.shard_lines, parts, PROBES, nodes)
+
+
+def on_device(param, sensor, blocks, probes):
+    return sketch_and_adjoint(param, sensor, blocks, probes)
 
 
 def solution(mesh):

time: 33.7 us -> 33 us (0.979)
  waiting for transfers between devices: 13.7 us -> 11.3 us
  Pallas kernels: 6.33 us -> 8.06 us
    ppermute x10, waiting for transfers between devices: 13.7 us -> 11.3 us  [trade(): return lax.ppermute(x, axis, [(i, i ^ k) for i in range(size)])]
    pallas_call x2 -> x4, Pallas kernels: 4.48 us -> 6.22 us  [the longest x1 3.18 us: sketch_terms(): pl.pallas_call(functools.partial(sent_kernel, plan), out_shape=[piece] *...]
  transfers between devices with their start and end apart: 10 -> 10, of which waited for: 9 -> 9; matrix products, arithmetic and copies ran while one was open for 0% -> 0% of each run, Pallas kernels for 2% -> 9%
where the time goes in v5:
time: 33 us; the launch traced here: 32.9 us
  starting transfers between devices  12.8 us (39%)
  waiting for transfers between devices  11.3 us (34%)
  Pallas kernels  8.06 us (24%)
  between operations  0.69 us (2%)
    ppermute x10, starting transfers between devices, trade(): return lax.ppermute(x, axis, [(i, i ^ k) for i in range(size)])  12.8 us
    ppermute x10, waiting for transfers between devices, trade(): return lax.ppermute(x, axis, [(i, i ^ k) for i in range(size)])  11.3 us
    pallas_call x1, Pallas kernels, sketch_terms(): pl.pallas_call(functools.partial(sent_kernel, plan), out_shape=[piece] *...  3.18 us
    pallas_call x1, Pallas kernels, own_terms(): pl.pallas_call(functools.partial(own_kernel, plan), out_shape=[in_vmem((p...  1.82 us
    pallas_call x2, Pallas kernels, adjoint_terms(): pl.pallas_call(functools.partial(adjoint_kernel, plan, distances, len(dis...  1.22 us
    pallas_call x1, Pallas kernels, finish(): pl.pallas_call(functools.partial(final_kernel, plan), out_shape=[jax.Shap...  1.16 us
  transfers between devices with their start and end apart: 10, of which 9 were waited for; matrix products, arithmetic and copies ran while one was open for 0% of the time, Pallas kernels for 9%

profile of v5, /device:TPU:0, one launch (start us, length us, event | category | flops | bytes accessed | tf_op | source)
XLA Modules:
  0.0 32.9 jit_solution(14687292792111004745)
XLA Ops:
  0.6 3.2 %sent_terms.1 = (f32[19,8,128]{2,1,0:T(8,128)S(1)}, f32[19,8,128]{2,1,0:T(8,128)S(1)}, f32[19,8,128]{2,1,0:T(8,128)S(1)}, bf16[4864,128]{1,0:T(8,128)(2,1)S(1)},...) custom-call(bf16[19200,128]{1,0:T(8,128)(2,1)} %bitcast.5, ...), custom_call_target="tpu_custom_call" | custom-call | tf_op jit(solution)/shard_map/sent_terms/pallas_call | solution.py:144
  3.8 4.1 %collective-permute-start = (f32[19,8,128]{2,1,0:T(8,128)S(1)}, f32[19,8,128]{2,1,0:T(8,128)S(1)}, u32[]{:S(2)}, u32[]{:S(2)}) collective-permute-start(f32[19,8,128]{2,1,0:T(8,128)S(1)} %get-tuple-element.19), channel_id=1, source_target_pairs={{0,12},{4,8},{8,4},{12,0},{16,28},{20,24},{24,20},{28,16},{1,13},{... | collective-permute-start | bytes 233480 | tf_op jit(solution)/shard_map/ppermute | solution.py:383
  7.9 0.4 %collective-permute-start.1 = (f32[19,8,128]{2,1,0:T(8,128)S(1)}, f32[19,8,128]{2,1,0:T(8,128)S(1)}, u32[]{:S(2)}, u32[]{:S(2)}) collective-permute-start(f32[19,8,128]{2,1,0:T(8,128)S(1)} %get-tuple-element.20), channel_id=1, source_target_pairs={{0,8},{4,12},{8,0},{12,4},{16,24},{20,28},{24,16},{28,20},{1,9},{5... | collective-permute-start | bytes 233480 | tf_op jit(solution)/shard_map/ppermute | solution.py:383
  8.3 0.2 collective-permute-start.2
  8.5 1.8 %own_terms.1 = (f32[19,8,128]{2,1,0:T(8,128)S(1)}, bf16[4864,128]{1,0:T(8,128)(2,1)S(1)}) custom-call(bf16[19200,128]{1,0:T(8,128)(2,1)} %bitcast.6, f32[520,128]{1,0:T(8,128)S(1)} %get-tuple-element.17.lhs_ref), custom_call_target="tpu_custom_call" | custom-call | tf_op jit(solution)/shard_map/own_terms/pallas_call | solution.py:162
  10.4 0.2 collective-permute-done
  10.6 1.8 %collective-permute-done.1 = f32[19,8,128]{2,1,0:T(8,128)S(1)} collective-permute-done((f32[19,8,128]{2,1,0:T(8,128)S(1)}, f32[19,8,128]{2,1,0:T(8,128)S(1)}, u32[]{:S(2)}, u32[]{:S(2)}) %collective-permute-start.1) | collective-permute-done | bytes 77856 | tf_op jit(solution)/shard_map/ppermute | solution.py:383
  12.4 0.4 %collective-permute-done.2 = f32[19,8,128]{2,1,0:T(8,128)S(1)} collective-permute-done((f32[19,8,128]{2,1,0:T(8,128)S(1)}, f32[19,8,128]{2,1,0:T(8,128)S(1)}, u32[]{:S(2)}, u32[]{:S(2)}) %collective-permute-start.2) | collective-permute-done | bytes 77856 | tf_op jit(solution)/shard_map/ppermute | solution.py:383
  12.8 2.7 %collective-permute-start.3 = (f32[19,8,128]{2,1,0:T(8,128)S(1)}, f32[19,8,128]{2,1,0:T(8,128)S(1)}, u32[]{:S(2)}, u32[]{:S(2)}) collective-permute-start(f32[19,8,128]{2,1,0:T(8,128)S(1)} %add_add_fusion.refs_0_), channel_id=1, source_target_pairs={{0,16},{4,20},{8,24},{12,28},{16,0},{20,4},{24,8},{28,12},{1,17},{... | collective-permute-start | bytes 233480 | tf_op jit(solution)/shard_map/ppermute | solution.py:383
  15.4 2.7 %collective-permute-done.3.refs_1_ = f32[19,8,128]{2,1,0:T(8,128)S(1)} collective-permute-done((f32[19,8,128]{2,1,0:T(8,128)S(1)}, f32[19,8,128]{2,1,0:T(8,128)S(1)}, u32[]{:S(2)}, u32[]{:S(2)}) %collective-permute-start.3) | collective-permute-done | bytes 77856 | tf_op jit(solution)/shard_map/ppermute | solution.py:383
  18.2 1.9 %collective-permute-start.6 = (f32[20,8,128]{2,1,0:T(8,128)S(1)}, f32[20,8,128]{2,1,0:T(8,128)S(1)}, u32[]{:S(2)}, u32[]{:S(2)}) collective-permute-start(f32[20,8,128]{2,1,0:T(8,128)S(1)} %add_with_gram.1.rest_0_.refs_0_), channel_id=1, source_target_pairs={{0,12},{4,8},{8,4},{12,0},{16,28},{20,24},{24,20},{28,16},{1,13},{... | collective-permute-start | bytes 245768 | tf_op jit(solution)/shard_map/ppermute | solution.py:383
  20.1 0.6 %collective-permute-start.5 = (f32[20,8,128]{2,1,0:T(8,128)S(1)}, f32[20,8,128]{2,1,0:T(8,128)S(1)}, u32[]{:S(2)}, u32[]{:S(2)}) collective-permute-start(f32[20,8,128]{2,1,0:T(8,128)S(1)} %add_with_gram.1.rest_0_.refs_0_), channel_id=1, source_target_pairs={{0,8},{4,12},{8,0},{12,4},{16,24},{20,28},{24,16},{28,20},{1,9},{5... | collective-permute-start | bytes 245768 | tf_op jit(solution)/shard_map/ppermute | solution.py:383
  20.7 1.0 %collective-permute-start.4 = (f32[20,8,128]{2,1,0:T(8,128)S(1)}, f32[20,8,128]{2,1,0:T(8,128)S(1)}, u32[]{:S(2)}, u32[]{:S(2)}) collective-permute-start(f32[20,8,128]{2,1,0:T(8,128)S(1)} %add_with_gram.1.rest_0_.refs_0_), channel_id=1, source_target_pairs={{0,4},{4,0},{8,12},{12,8},{16,20},{20,16},{24,28},{28,24},{1,5},{5... | collective-permute-start | bytes 245768 | tf_op jit(solution)/shard_map/ppermute | solution.py:383
  21.7 2.0 %collective-permute-done.6.rest_3_.refs_1_ = f32[20,8,128]{2,1,0:T(8,128)S(1)} collective-permute-done((f32[20,8,128]{2,1,0:T(8,128)S(1)}, f32[20,8,128]{2,1,0:T(8,128)S(1)}, u32[]{:S(2)}, u32[]{:S(2)}) %collective-permute-start.6) | collective-permute-done | bytes 81952 | tf_op jit(solution)/shard_map/ppermute | solution.py:383
  23.7 0.6 %adjoint_first.1.refs_4_ = f32[65,8,128]{2,1,0:T(8,128)S(1)} custom-call(f32[20,8,128]{2,1,0:T(8,128)S(1)} %add_with_gram.1.rest_0_.refs_0_, f32[20,8,128]{2,1,0:T(8,128)S(1)} %collective-permute-done.6.rest_3_.refs_1_, bf16[4864,128]{1,0:T(8,128)(2,1)S(1)} %get-tuple-element.24.refs_2_, bf16[4864,128]{1,0:T(8,128)(2,1)S(1)} %get-tuple-element.25.refs_3_), custom_call_target="tpu_custom_call" | custom-call | tf_op jit(solution)/shard_map/adjoint_first/pallas_call | solution.py:263
  24.3 0.2 collective-permute-done.5.rest_2_.refs_0_
  24.5 0.6 %collective-permute-done.4.rest_1_.refs_1_ = f32[20,8,128]{2,1,0:T(8,128)S(1)} collective-permute-done((f32[20,8,128]{2,1,0:T(8,128)S(1)}, f32[20,8,128]{2,1,0:T(8,128)S(1)}, u32[]{:S(2)}, u32[]{:S(2)}) %collective-permute-start.4) | collective-permute-done | bytes 81952 | tf_op jit(solution)/shard_map/ppermute | solution.py:383
  25.2 0.6 %adjoint_rest.1 = (f32[17,8,128]{2,1,0:T(8,128)S(1)}, f32[17,8,128]{2,1,0:T(8,128)S(1)}, f32[17,8,128]{2,1,0:T(8,128)S(1)}, f32[17,8,128]{2,1,0:T(8,128)S(1)}) custom-call(f32[20,8,128]{2,1,0:T(8,128)S(1)} %collective-permute-done.5.rest_2_.refs_0_, f32[20,8,128]{2,1,0:T(8,128)S(1)} %collective-permute-done.4.rest_1_.refs_1_, ...), custom_call_target="tpu_custom_call" | custom-call | tf_op jit(solution)/shard_map/adjoint_rest/pallas_call | solution.py:263
  25.9 1.3 %collective-permute-start.8 = (f32[17,8,128]{2,1,0:T(8,128)S(1)}, f32[17,8,128]{2,1,0:T(8,128)S(1)}, u32[]{:S(2)}, u32[]{:S(2)}) collective-permute-start(f32[17,8,128]{2,1,0:T(8,128)S(1)} %get-tuple-element.28), channel_id=1, source_target_pairs={{0,2},{1,3},{2,0},{3,1},{4,6},{5,7},{6,4},{7,5},{8,10},{9,11},{10,... | collective-permute-start | bytes 208904 | tf_op jit(solution)/shard_map/ppermute | solution.py:383
  27.2 0.5 %collective-permute-start.9 = (f32[17,8,128]{2,1,0:T(8,128)S(1)}, f32[17,8,128]{2,1,0:T(8,128)S(1)}, u32[]{:S(2)}, u32[]{:S(2)}) collective-permute-start(f32[17,8,128]{2,1,0:T(8,128)S(1)} %get-tuple-element.29), channel_id=1, source_target_pairs={{0,3},{1,2},{2,1},{3,0},{4,7},{5,6},{6,5},{7,4},{8,11},{9,10},{10,... | collective-permute-start | bytes 208904 | tf_op jit(solution)/shard_map/ppermute | solution.py:383
  27.7 0.6 %sketch_by_line.1.sketch_ref = f32[64,8,150]{2,1,0:T(8,128)S(1)} custom-call(f32[20,8,128]{2,1,0:T(8,128)S(1)} %add_with_gram.1.rest_0_.refs_0_, f32[20,8,128]{2,1,0:T(8,128)S(1)} %collective-permute-done.4.rest_1_.refs_1_, f32[20,8,128]{2,1,0:T(8,128)S(1)} %collective-permute-done.5.rest_2_.refs_0_, f32[20,8,128]{2,1,0:T(8,128)S(1)} %collective-permute-done.6.rest_3_.refs_1_), custom_call_target="tpu_custom_call" | custom-call | tf_op jit(solution)/shard_map/sketch_by_line/pallas_call | solution.py:298
  28.3 2.4 %collective-permute-done.8.rest_2_ = f32[17,8,128]{2,1,0:T(8,128)S(1)} collective-permute-done((f32[17,8,128]{2,1,0:T(8,128)S(1)}, f32[17,8,128]{2,1,0:T(8,128)S(1)}, u32[]{:S(2)}, u32[]{:S(2)}) %collective-permute-start.8) | collective-permute-done | bytes 69664 | tf_op jit(solution)/shard_map/ppermute | solution.py:383
  30.7 1.0 %collective-permute-done.9.rest_3_ = f32[17,8,128]{2,1,0:T(8,128)S(1)} collective-permute-done((f32[17,8,128]{2,1,0:T(8,128)S(1)}, f32[17,8,128]{2,1,0:T(8,128)S(1)}, u32[]{:S(2)}, u32[]{:S(2)}) %collective-permute-start.9) | collective-permute-done | bytes 69664 | tf_op jit(solution)/shard_map/ppermute | solution.py:383
  31.7 1.2 %finish.1 = (f32[64,2,4,150]{3,2,1,0:T(4,128)}, bf16[128,128]{1,0:T(8,128)(2,1)}) custom-call(f32[64,8,150]{2,1,0:T(8,128)S(1)} %sketch_by_line.1.sketch_ref, f32[17,8,128]{2,1,0:T(8,128)S(1)} %get-tuple-element.26.rest_0_, f32[17,8,128]{2,1,0:T(8,128)S(1)} %collective-permute-done.7.rest_1_, f32[17,8,128]{2,1,0:T(8,128)S(1)} %collective-permute-done.8.rest_2_, ...), custom_call_target="tpu_custom_call" | custom-call | tf_op jit(solution)/shard_map/finish/pallas_call | solution.py:369
  (4 shorter events, 0.2 us)
Async XLA Ops:
  3.8 6.7 %collective-permute-start = (f32[19,8,128]{2,1,0:T(8,128)S(1)}, f32[19,8,128]{2,1,0:T(8,128)S(1)}, u32[]{:S(2)}, u32[]{:S(2)}) collective-permute-start(f32[19,8,128]{2,1,0:T(8,128)S(1)} %get-tuple-element.19), channel_id=1, source_target_pairs={{0,12},{4,8},{8,4},{12,0},{16,28},{20,24},{24,20},{28,16},{1,13},{... | collective-permute-start | bytes 233480 | tf_op jit(solution)/shard_map/ppermute | solution.py:383
  7.9 4.5 %collective-permute-start.1 = (f32[19,8,128]{2,1,0:T(8,128)S(1)}, f32[19,8,128]{2,1,0:T(8,128)S(1)}, u32[]{:S(2)}, u32[]{:S(2)}) collective-permute-start(f32[19,8,128]{2,1,0:T(8,128)S(1)} %get-tuple-element.20), channel_id=1, source_target_pairs={{0,8},{4,12},{8,0},{12,4},{16,24},{20,28},{24,16},{28,20},{1,9},{5... | collective-permute-start | bytes 233480 | tf_op jit(solution)/shard_map/ppermute | solution.py:383
  8.3 4.4 %collective-permute-start.2 = (f32[19,8,128]{2,1,0:T(8,128)S(1)}, f32[19,8,128]{2,1,0:T(8,128)S(1)}, u32[]{:S(2)}, u32[]{:S(2)}) collective-permute-start(f32[19,8,128]{2,1,0:T(8,128)S(1)} %get-tuple-element.21), channel_id=1, source_target_pairs={{0,4},{4,0},{8,12},{12,8},{16,20},{20,16},{24,28},{28,24},{1,5},{5... | collective-permute-start | bytes 233480 | tf_op jit(solution)/shard_map/ppermute | solution.py:383
  12.8 5.4 %collective-permute-start.3 = (f32[19,8,128]{2,1,0:T(8,128)S(1)}, f32[19,8,128]{2,1,0:T(8,128)S(1)}, u32[]{:S(2)}, u32[]{:S(2)}) collective-permute-start(f32[19,8,128]{2,1,0:T(8,128)S(1)} %add_add_fusion.refs_0_), channel_id=1, source_target_pairs={{0,16},{4,20},{8,24},{12,28},{16,0},{20,4},{24,8},{28,12},{1,17},{... | collective-permute-start | bytes 233480 | tf_op jit(solution)/shard_map/ppermute | solution.py:383
  18.2 5.4 %collective-permute-start.6 = (f32[20,8,128]{2,1,0:T(8,128)S(1)}, f32[20,8,128]{2,1,0:T(8,128)S(1)}, u32[]{:S(2)}, u32[]{:S(2)}) collective-permute-start(f32[20,8,128]{2,1,0:T(8,128)S(1)} %add_with_gram.1.rest_0_.refs_0_), channel_id=1, source_target_pairs={{0,12},{4,8},{8,4},{12,0},{16,28},{20,24},{24,20},{28,16},{1,13},{... | collective-permute-start | bytes 245768 | tf_op jit(solution)/shard_map/ppermute | solution.py:383
  20.1 4.4 %collective-permute-start.5 = (f32[20,8,128]{2,1,0:T(8,128)S(1)}, f32[20,8,128]{2,1,0:T(8,128)S(1)}, u32[]{:S(2)}, u32[]{:S(2)}) collective-permute-start(f32[20,8,128]{2,1,0:T(8,128)S(1)} %add_with_gram.1.rest_0_.refs_0_), channel_id=1, source_target_pairs={{0,8},{4,12},{8,0},{12,4},{16,24},{20,28},{24,16},{28,20},{1,9},{5... | collective-permute-start | bytes 245768 | tf_op jit(solution)/shard_map/ppermute | solution.py:383
  20.7 4.4 %collective-permute-start.4 = (f32[20,8,128]{2,1,0:T(8,128)S(1)}, f32[20,8,128]{2,1,0:T(8,128)S(1)}, u32[]{:S(2)}, u32[]{:S(2)}) collective-permute-start(f32[20,8,128]{2,1,0:T(8,128)S(1)} %add_with_gram.1.rest_0_.refs_0_), channel_id=1, source_target_pairs={{0,4},{4,0},{8,12},{12,8},{16,20},{20,16},{24,28},{28,24},{1,5},{5... | collective-permute-start | bytes 245768 | tf_op jit(solution)/shard_map/ppermute | solution.py:383
  25.8 2.5 %collective-permute-start.7 = (f32[17,8,128]{2,1,0:T(8,128)S(1)}, f32[17,8,128]{2,1,0:T(8,128)S(1)}, u32[]{:S(2)}, u32[]{:S(2)}) collective-permute-start(f32[17,8,128]{2,1,0:T(8,128)S(1)} %get-tuple-element.27), channel_id=1, source_target_pairs={{0,1},{1,0},{2,3},{3,2},{4,5},{5,4},{6,7},{7,6},{8,9},{9,8},{10,11... | collective-permute-start | bytes 208904 | tf_op jit(solution)/shard_map/ppermute | solution.py:383
  25.9 4.8 %collective-permute-start.8 = (f32[17,8,128]{2,1,0:T(8,128)S(1)}, f32[17,8,128]{2,1,0:T(8,128)S(1)}, u32[]{:S(2)}, u32[]{:S(2)}) collective-permute-start(f32[17,8,128]{2,1,0:T(8,128)S(1)} %get-tuple-element.28), channel_id=1, source_target_pairs={{0,2},{1,3},{2,0},{3,1},{4,6},{5,7},{6,4},{7,5},{8,10},{9,11},{10,... | collective-permute-start | bytes 208904 | tf_op jit(solution)/shard_map/ppermute | solution.py:383
  27.2 4.5 %collective-permute-start.9 = (f32[17,8,128]{2,1,0:T(8,128)S(1)}, f32[17,8,128]{2,1,0:T(8,128)S(1)}, u32[]{:S(2)}, u32[]{:S(2)}) collective-permute-start(f32[17,8,128]{2,1,0:T(8,128)S(1)} %get-tuple-element.29), channel_id=1, source_target_pairs={{0,3},{1,2},{2,1},{3,0},{4,7},{5,6},{6,5},{7,4},{8,11},{9,10},{10,... | collective-permute-start | bytes 208904 | tf_op jit(solution)/shard_map/ppermute | solution.py:383

commit v6 on v5

--- a/solution.py
+++ b/solution.py
@@ -12,9 +12,10 @@
 STEP = 2 * LANES
 QUAD = 4
 PROBES = 4
-ARRIVALS = ((3, 2), (1,))
+ARRIVALS = ((3,), (2,), (1,))
 REDUCE, GATHER = (3, 2, 1), (3, 2, 1)
-URGENCY = (0, 1)
+URGENCY = (0, 1, 1)
+PIECES = 8
 SPLITS = 3
 
 
@@ -204,15 +205,19 @@
     )(*from_vmem(*pieces))
 
 
-def adjoint_kernel(plan, distances, count, *refs):
+def adjoint_kernel(plan, distances, follows, last, *refs):
+    count = len(distances)
     ins, kepts, rest = refs[:count], refs[count : 2 * count], refs[2 * count :]
-    earlier = rest[0] if len(rest) > 1 else None
+    earlier = rest[0] if follows else None
     acc_ref = rest[-1]
     param = lax.axis_index("param")
     low = row_of() < 4
     even = lane_of() % 2 == 0
     column = lane_of((8, STEP))
-    acc_ref[...] = jnp.zeros(acc_ref.shape, jnp.float32)
+    if follows and not last:
+        acc_ref[...] = earlier[...]
+    else:
+        acc_ref[...] = jnp.zeros(acc_ref.shape, jnp.float32)
     for k, in_ref, kept_ref in zip(distances, ins, kepts):
         first = (param & (QUAD - 1) ^ k) * plan.quarter
 
@@ -242,10 +247,11 @@
 
         lax.fori_loop(0, plan.quarter, body, 0, unroll=True)
     packed = sum(ref[plan.quarter] for ref in ins)
-    if earlier is None:
+    if follows:
+        packed = packed + earlier[plan.lines]
+    if not last:
         acc_ref[plan.lines] = packed
         return
-    packed = packed + earlier[plan.lines]
     spot = lax.axis_index("sensor")
     for k, out_ref in enumerate(rest[1:-1]):
         lines = pl.ds((spot ^ k) * plan.shard_lines, plan.shard_lines)
@@ -253,7 +259,7 @@
         out_ref[plan.shard_lines] = packed
 
 
-def adjoint_terms(plan, distances, pieces, kept, earlier=None):
+def adjoint_terms(plan, distances, pieces, kept, earlier=None, last=False):
     vmem = pl.BlockSpec(memory_space=pltpu.VMEM)
     whole = in_vmem((plan.lines + 1, 8, LANES), jnp.float32)
     shard = in_vmem((plan.shard_lines + 1, 8, LANES), jnp.float32)
@@ -261,13 +267,13 @@
     if earlier is not None:
         given.append(earlier)
     return pl.pallas_call(
-        functools.partial(adjoint_kernel, plan, distances, len(distances)),
-        out_shape=whole if earlier is None else [shard] * plan.shards,
+        functools.partial(adjoint_kernel, plan, distances, earlier is not None, last),
+        out_shape=[shard] * plan.shards if last else whole,
         in_specs=[vmem] * len(given),
-        out_specs=vmem if earlier is None else [vmem] * plan.shards,
-        scratch_shapes=[] if earlier is None else [whole],
-        compiler_params=params(16),
-        name="adjoint_first" if earlier is None else "adjoint_rest",
+        out_specs=[vmem] * plan.shards if last else vmem,
+        scratch_shapes=[whole] if last else [],
+        compiler_params=params(16),
+        name="adjoint_last" if last else "adjoint_part",
     )(*from_vmem(*given))
 
 
@@ -345,7 +351,7 @@
 
 
 def final_kernel(plan, sketch_ref, *rest):
-    ins, basis_ref, coeffs_ref = rest[: plan.shards], rest[plan.shards], rest[plan.shards + 1]
+    ins, (basis_out, coeffs_out, basis_ref, coeffs_ref, sems) = rest[: plan.shards], rest[plan.shards :]
     packed = sum(ref[plan.shard_lines] for ref in ins)
     rows = inverse_rows(plan, packed)
 
@@ -353,27 +359,41 @@
         width = x.shape[1]
         return sum((rows[d][:, :width] * (roll(x, d, 0) if d else x)) for d in range(PROBES))
 
+    copies = []
+    for at in range(PIECES):
+        low, high = at * plan.lines // PIECES, (at + 1) * plan.lines // PIECES
+        for line in range(low, high):
+            for start in range(0, plan.group, LANES):
+                width = min(LANES, plan.group - start)
+                value = scaled(sketch_ref[line, :, pl.ds(start, width)])
+                for part in range(2):
+                    basis_ref[line, part, :, pl.ds(start, width)] = value[4 * part : 4 * part + 4]
+        made = pl.ds(low, high - low)
+        copies.append(pltpu.make_async_copy(basis_ref.at[made], basis_out.at[made], sems.at[at]))
+        copies[-1].start()
     for pair in range(plan.shard_lines // 2):
         two = [scaled(sum(ref[2 * pair + i] for ref in ins)) for i in range(2)]
         coeffs_ref[pl.ds(16 * pair, 16)] = jnp.concatenate(two, axis=0).astype(jnp.bfloat16)
-    for line in range(plan.lines):
-        for start in range(0, plan.group, LANES):
-            width = min(LANES, plan.group - start)
-            value = scaled(sketch_ref[line, :, pl.ds(start, width)])
-            for part in range(2):
-                basis_ref[line, part, :, pl.ds(start, width)] = value[4 * part : 4 * part + 4]
+    copies.append(pltpu.make_async_copy(coeffs_ref, coeffs_out, sems.at[PIECES]))
+    copies[-1].start()
+    for copy in copies:
+        copy.wait()
 
 
 def finish(plan, sketch, pieces):
     vmem = pl.BlockSpec(memory_space=pltpu.VMEM)
+    basis = (plan.lines, 2, PROBES, plan.group)
+    coeffs = (plan.shard_lines * 8, LANES)
     return pl.pallas_call(
         functools.partial(final_kernel, plan),
-        out_shape=[
-            jax.ShapeDtypeStruct((plan.lines, 2, PROBES, plan.group), jnp.float32),
-            jax.ShapeDtypeStruct((plan.shard_lines * 8, LANES), jnp.bfloat16),
+        out_shape=[jax.ShapeDtypeStruct(basis, jnp.float32), jax.ShapeDtypeStruct(coeffs, jnp.bfloat16)],
+        in_specs=[vmem] * (1 + plan.shards),
+        out_specs=[pl.BlockSpec(memory_space=pltpu.HBM)] * 2,
+        scratch_shapes=[
+            pltpu.VMEM(basis, jnp.float32),
+            pltpu.VMEM(coeffs, jnp.bfloat16),
+            pltpu.SemaphoreType.DMA((PIECES + 1,)),
         ],
-        in_specs=[vmem] * (1 + plan.shards),
-        out_specs=[vmem] * 2,
         compiler_params=params(16),
         name="finish",
     )(*from_vmem(sketch, *pieces))
@@ -399,8 +419,9 @@
     sums = [total] + ([trade(total, "param", param, span)] if span < param else [])
     own = add_with_gram(plan, *sums)
     pieces = [own] + [trade(own, "param", param, k) for k in range(1, QUAD)]
-    adjoint = adjoint_terms(plan, (0, GATHER[0]), pieces, kept)
-    adjoint = adjoint_terms(plan, GATHER[1:], pieces, kept, adjoint)
+    adjoint = adjoint_terms(plan, (0,), pieces, kept)
+    adjoint = adjoint_terms(plan, GATHER[:-1], pieces, kept, adjoint)
+    adjoint = adjoint_terms(plan, GATHER[-1:], pieces, kept, adjoint, True)
     gathered = [adjoint[0]] + [trade(adjoint[k], "sensor", sensor, k) for k in range(1, sensor)]
     sketch = sketch_by_line(plan, pieces)
     basis, coeffs = finish(plan, sketch, gathered)

time: 33 us -> 32.6 us (0.988)
  waiting for transfers between devices: 11.3 us -> 10.9 us
    ppermute x10, waiting for transfers between devices: 11.3 us -> 10.9 us  [trade(): return lax.ppermute(x, axis, [(i, i ^ k) for i in range(size)])]
    pallas_call x2 -> x3, Pallas kernels: 1.22 us -> 1.45 us  [adjoint_terms(): pl.pallas_call(functools.partial(adjoint_kernel, plan, distances, earlier...]
  transfers between devices with their start and end apart: 10 -> 10, of which waited for: 9 -> 8; matrix products, arithmetic and copies ran while one was open for 0% -> 0% of each run, Pallas kernels for 9% -> 10%
where the time goes in v6:
time: 32.6 us; the launch traced here: 32.4 us
  starting transfers between devices  12.8 us (39%)
  waiting for transfers between devices  10.9 us (33%)
  Pallas kernels  8.05 us (25%)
  between operations  0.69 us (2%)
    ppermute x10, starting transfers between devices, trade(): return lax.ppermute(x, axis, [(i, i ^ k) for i in range(size)])  12.8 us
    ppermute x10, waiting for transfers between devices, trade(): return lax.ppermute(x, axis, [(i, i ^ k) for i in range(size)])  10.9 us
    pallas_call x1, Pallas kernels, sketch_terms(): pl.pallas_call(functools.partial(sent_kernel, plan), out_shape=[piece] *...  3.03 us
    pallas_call x1, Pallas kernels, own_terms(): pl.pallas_call(functools.partial(own_kernel, plan), out_shape=[in_vmem((p...  1.82 us
    pallas_call x3, Pallas kernels, adjoint_terms(): pl.pallas_call(functools.partial(adjoint_kernel, plan, distances, earlier...  1.45 us
    pallas_call x1, Pallas kernels, finish(): pl.pallas_call(functools.partial(final_kernel, plan), out_shape=[jax.Shap...  1.07 us
  transfers between devices with their start and end apart: 10, of which 8 were waited for; matrix products, arithmetic and copies ran while one was open for 0% of the time, Pallas kernels for 10%

profile of v6, /device:TPU:0, one launch (start us, length us, event | category | flops | bytes accessed | tf_op | source)
XLA Modules:
  0.0 32.4 jit_solution(14839182175730826294)
XLA Ops:
  0.6 3.0 %sent_terms.1 = (f32[19,8,128]{2,1,0:T(8,128)S(1)}, f32[19,8,128]{2,1,0:T(8,128)S(1)}, f32[19,8,128]{2,1,0:T(8,128)S(1)}, bf16[4864,128]{1,0:T(8,128)(2,1)S(1)},...) custom-call(bf16[19200,128]{1,0:T(8,128)(2,1)} %bitcast.5, ...), custom_call_target="tpu_custom_call" | custom-call | tf_op jit(solution)/shard_map/sent_terms/pallas_call | solution.py:145
  3.7 4.1 %collective-permute-start = (f32[19,8,128]{2,1,0:T(8,128)S(1)}, f32[19,8,128]{2,1,0:T(8,128)S(1)}, u32[]{:S(2)}, u32[]{:S(2)}) collective-permute-start(f32[19,8,128]{2,1,0:T(8,128)S(1)} %get-tuple-element.19), channel_id=1, source_target_pairs={{0,12},{4,8},{8,4},{12,0},{16,28},{20,24},{24,20},{28,16},{1,13},{... | collective-permute-start | bytes 233480 | tf_op jit(solution)/shard_map/ppermute | solution.py:403
  7.7 0.4 %collective-permute-start.1 = (f32[19,8,128]{2,1,0:T(8,128)S(1)}, f32[19,8,128]{2,1,0:T(8,128)S(1)}, u32[]{:S(2)}, u32[]{:S(2)}) collective-permute-start(f32[19,8,128]{2,1,0:T(8,128)S(1)} %get-tuple-element.20), channel_id=1, source_target_pairs={{0,8},{4,12},{8,0},{12,4},{16,24},{20,28},{24,16},{28,20},{1,9},{5... | collective-permute-start | bytes 233480 | tf_op jit(solution)/shard_map/ppermute | solution.py:403
  8.2 0.2 collective-permute-start.2
  8.4 1.8 %own_terms.1 = (f32[19,8,128]{2,1,0:T(8,128)S(1)}, bf16[4864,128]{1,0:T(8,128)(2,1)S(1)}) custom-call(bf16[19200,128]{1,0:T(8,128)(2,1)} %bitcast.6, f32[520,128]{1,0:T(8,128)S(1)} %get-tuple-element.17.lhs_ref), custom_call_target="tpu_custom_call" | custom-call | tf_op jit(solution)/shard_map/own_terms/pallas_call | solution.py:163
  10.2 0.2 collective-permute-done
  10.4 1.8 %collective-permute-done.1 = f32[19,8,128]{2,1,0:T(8,128)S(1)} collective-permute-done((f32[19,8,128]{2,1,0:T(8,128)S(1)}, f32[19,8,128]{2,1,0:T(8,128)S(1)}, u32[]{:S(2)}, u32[]{:S(2)}) %collective-permute-start.1) | collective-permute-done | bytes 77856 | tf_op jit(solution)/shard_map/ppermute | solution.py:403
  12.2 0.4 %collective-permute-done.2 = f32[19,8,128]{2,1,0:T(8,128)S(1)} collective-permute-done((f32[19,8,128]{2,1,0:T(8,128)S(1)}, f32[19,8,128]{2,1,0:T(8,128)S(1)}, u32[]{:S(2)}, u32[]{:S(2)}) %collective-permute-start.2) | collective-permute-done | bytes 77856 | tf_op jit(solution)/shard_map/ppermute | solution.py:403
  12.6 2.7 %collective-permute-start.3 = (f32[19,8,128]{2,1,0:T(8,128)S(1)}, f32[19,8,128]{2,1,0:T(8,128)S(1)}, u32[]{:S(2)}, u32[]{:S(2)}) collective-permute-start(f32[19,8,128]{2,1,0:T(8,128)S(1)} %add_add_fusion.refs_0_), channel_id=1, source_target_pairs={{0,16},{4,20},{8,24},{12,28},{16,0},{20,4},{24,8},{28,12},{1,17},{... | collective-permute-start | bytes 233480 | tf_op jit(solution)/shard_map/ppermute | solution.py:403
  15.3 2.7 %collective-permute-done.3.refs_1_ = f32[19,8,128]{2,1,0:T(8,128)S(1)} collective-permute-done((f32[19,8,128]{2,1,0:T(8,128)S(1)}, f32[19,8,128]{2,1,0:T(8,128)S(1)}, u32[]{:S(2)}, u32[]{:S(2)}) %collective-permute-start.3) | collective-permute-done | bytes 77856 | tf_op jit(solution)/shard_map/ppermute | solution.py:403
  18.1 1.9 %collective-permute-start.6 = (f32[20,8,128]{2,1,0:T(8,128)S(1)}, f32[20,8,128]{2,1,0:T(8,128)S(1)}, u32[]{:S(2)}, u32[]{:S(2)}) collective-permute-start(f32[20,8,128]{2,1,0:T(8,128)S(1)} %add_with_gram.1.rest_0_.refs_0_), channel_id=1, source_target_pairs={{0,12},{4,8},{8,4},{12,0},{16,28},{20,24},{24,20},{28,16},{1,13},{... | collective-permute-start | bytes 245768 | tf_op jit(solution)/shard_map/ppermute | solution.py:403
  20.0 0.6 %collective-permute-start.5 = (f32[20,8,128]{2,1,0:T(8,128)S(1)}, f32[20,8,128]{2,1,0:T(8,128)S(1)}, u32[]{:S(2)}, u32[]{:S(2)}) collective-permute-start(f32[20,8,128]{2,1,0:T(8,128)S(1)} %add_with_gram.1.rest_0_.refs_0_), channel_id=1, source_target_pairs={{0,8},{4,12},{8,0},{12,4},{16,24},{20,28},{24,16},{28,20},{1,9},{5... | collective-permute-start | bytes 245768 | tf_op jit(solution)/shard_map/ppermute | solution.py:403
  20.6 1.0 %collective-permute-start.4 = (f32[20,8,128]{2,1,0:T(8,128)S(1)}, f32[20,8,128]{2,1,0:T(8,128)S(1)}, u32[]{:S(2)}, u32[]{:S(2)}) collective-permute-start(f32[20,8,128]{2,1,0:T(8,128)S(1)} %add_with_gram.1.rest_0_.refs_0_), channel_id=1, source_target_pairs={{0,4},{4,0},{8,12},{12,8},{16,20},{20,16},{24,28},{28,24},{1,5},{5... | collective-permute-start | bytes 245768 | tf_op jit(solution)/shard_map/ppermute | solution.py:403
  21.6 0.4 %adjoint_part.2.refs_4_ = f32[65,8,128]{2,1,0:T(8,128)S(1)} custom-call(f32[20,8,128]{2,1,0:T(8,128)S(1)} %add_with_gram.1.rest_0_.refs_0_, bf16[4864,128]{1,0:T(8,128)(2,1)S(1)} %get-tuple-element.25.refs_1_), custom_call_target="tpu_custom_call" | custom-call | tf_op jit(solution)/shard_map/adjoint_part/pallas_call | solution.py:269
  22.0 1.5 %collective-permute-done.6.rest_3_.refs_0_ = f32[20,8,128]{2,1,0:T(8,128)S(1)} collective-permute-done((f32[20,8,128]{2,1,0:T(8,128)S(1)}, f32[20,8,128]{2,1,0:T(8,128)S(1)}, u32[]{:S(2)}, u32[]{:S(2)}) %collective-permute-start.6) | collective-permute-done | bytes 81952 | tf_op jit(solution)/shard_map/ppermute | solution.py:403
  23.5 0.9 %collective-permute-done.5.rest_2_.refs_1_ = f32[20,8,128]{2,1,0:T(8,128)S(1)} collective-permute-done((f32[20,8,128]{2,1,0:T(8,128)S(1)}, f32[20,8,128]{2,1,0:T(8,128)S(1)}, u32[]{:S(2)}, u32[]{:S(2)}) %collective-permute-start.5) | collective-permute-done | bytes 81952 | tf_op jit(solution)/shard_map/ppermute | solution.py:403
  24.4 0.6 %adjoint_part.3.refs_2_ = f32[65,8,128]{2,1,0:T(8,128)S(1)} custom-call(f32[20,8,128]{2,1,0:T(8,128)S(1)} %collective-permute-done.6.rest_3_.refs_0_, f32[20,8,128]{2,1,0:T(8,128)S(1)} %collective-permute-done.5.rest_2_.refs_1_, bf16[4864,128]{1,0:T(8,128)(2,1)S(1)} %get-tuple-element.23.refs_2_, bf16[4864,128]{1,0:T(8,128)(2,1)S(1)} %get-tuple-element.24.refs_3_, ...), custom_call_target="tpu_custom_call" | custom-call | tf_op jit(solution)/shard_map/adjoint_part/pallas_call | solution.py:269
  25.0 0.4 %adjoint_last.1 = (f32[17,8,128]{2,1,0:T(8,128)S(1)}, f32[17,8,128]{2,1,0:T(8,128)S(1)}, f32[17,8,128]{2,1,0:T(8,128)S(1)}, f32[17,8,128]{2,1,0:T(8,128)S(1)}) custom-call(f32[20,8,128]{2,1,0:T(8,128)S(1)} %collective-permute-done.4.rest_1_.refs_0_, bf16[4864,128]{1,0:T(8,128)(2,1)S(1)} %get-tuple-element.22.refs_1_, f32[65,8,128]{2,1,0:T(8,128)S(1)} %adjoint_part.3.refs_2_), custom_call_target="tpu_custom_call" | custom-call | tf_op jit(solution)/shard_map/adjoint_last/pallas_call | solution.py:269
  25.6 1.5 %collective-permute-start.8 = (f32[17,8,128]{2,1,0:T(8,128)S(1)}, f32[17,8,128]{2,1,0:T(8,128)S(1)}, u32[]{:S(2)}, u32[]{:S(2)}) collective-permute-start(f32[17,8,128]{2,1,0:T(8,128)S(1)} %get-tuple-element.28), channel_id=1, source_target_pairs={{0,2},{1,3},{2,0},{3,1},{4,6},{5,7},{6,4},{7,5},{8,10},{9,11},{10,... | collective-permute-start | bytes 208904 | tf_op jit(solution)/shard_map/ppermute | solution.py:403
  27.1 0.3 %collective-permute-start.9 = (f32[17,8,128]{2,1,0:T(8,128)S(1)}, f32[17,8,128]{2,1,0:T(8,128)S(1)}, u32[]{:S(2)}, u32[]{:S(2)}) collective-permute-start(f32[17,8,128]{2,1,0:T(8,128)S(1)} %get-tuple-element.29), channel_id=1, source_target_pairs={{0,3},{1,2},{2,1},{3,0},{4,7},{5,6},{6,5},{7,4},{8,11},{9,10},{10,... | collective-permute-start | bytes 208904 | tf_op jit(solution)/shard_map/ppermute | solution.py:403
  27.4 0.6 %sketch_by_line.1.sketch_ref = f32[64,8,150]{2,1,0:T(8,128)S(1)} custom-call(f32[20,8,128]{2,1,0:T(8,128)S(1)} %add_with_gram.1.rest_0_.refs_0_, f32[20,8,128]{2,1,0:T(8,128)S(1)} %collective-permute-done.4.rest_1_.refs_0_, f32[20,8,128]{2,1,0:T(8,128)S(1)} %collective-permute-done.5.rest_2_.refs_1_, f32[20,8,128]{2,1,0:T(8,128)S(1)} %collective-permute-done.6.rest_3_.refs_0_), custom_call_target="tpu_custom_call" | custom-call | tf_op jit(solution)/shard_map/sketch_by_line/pallas_call | solution.py:304
  28.0 2.2 %collective-permute-done.8.rest_2_ = f32[17,8,128]{2,1,0:T(8,128)S(1)} collective-permute-done((f32[17,8,128]{2,1,0:T(8,128)S(1)}, f32[17,8,128]{2,1,0:T(8,128)S(1)}, u32[]{:S(2)}, u32[]{:S(2)}) %collective-permute-start.8) | collective-permute-done | bytes 69664 | tf_op jit(solution)/shard_map/ppermute | solution.py:403
  30.2 1.2 %collective-permute-done.9.rest_3_ = f32[17,8,128]{2,1,0:T(8,128)S(1)} collective-permute-done((f32[17,8,128]{2,1,0:T(8,128)S(1)}, f32[17,8,128]{2,1,0:T(8,128)S(1)}, u32[]{:S(2)}, u32[]{:S(2)}) %collective-permute-start.9) | collective-permute-done | bytes 69664 | tf_op jit(solution)/shard_map/ppermute | solution.py:403
  31.4 1.1 %finish.1 = (f32[64,2,4,150]{3,2,1,0:T(4,128)}, bf16[128,128]{1,0:T(8,128)(2,1)}) custom-call(f32[64,8,150]{2,1,0:T(8,128)S(1)} %sketch_by_line.1.sketch_ref, f32[17,8,128]{2,1,0:T(8,128)S(1)} %get-tuple-element.26.rest_0_, f32[17,8,128]{2,1,0:T(8,128)S(1)} %collective-permute-done.7.rest_1_, f32[17,8,128]{2,1,0:T(8,128)S(1)} %collective-permute-done.8.rest_2_, ...), custom_call_target="tpu_custom_call" | custom-call | tf_op jit(solution)/shard_map/finish/pallas_call | solution.py:387
  (5 shorter events, 0.2 us)
Async XLA Ops:
  3.7 6.7 %collective-permute-start = (f32[19,8,128]{2,1,0:T(8,128)S(1)}, f32[19,8,128]{2,1,0:T(8,128)S(1)}, u32[]{:S(2)}, u32[]{:S(2)}) collective-permute-start(f32[19,8,128]{2,1,0:T(8,128)S(1)} %get-tuple-element.19), channel_id=1, source_target_pairs={{0,12},{4,8},{8,4},{12,0},{16,28},{20,24},{24,20},{28,16},{1,13},{... | collective-permute-start | bytes 233480 | tf_op jit(solution)/shard_map/ppermute | solution.py:403
  7.7 4.5 %collective-permute-start.1 = (f32[19,8,128]{2,1,0:T(8,128)S(1)}, f32[19,8,128]{2,1,0:T(8,128)S(1)}, u32[]{:S(2)}, u32[]{:S(2)}) collective-permute-start(f32[19,8,128]{2,1,0:T(8,128)S(1)} %get-tuple-element.20), channel_id=1, source_target_pairs={{0,8},{4,12},{8,0},{12,4},{16,24},{20,28},{24,16},{28,20},{1,9},{5... | collective-permute-start | bytes 233480 | tf_op jit(solution)/shard_map/ppermute | solution.py:403
  8.2 4.4 %collective-permute-start.2 = (f32[19,8,128]{2,1,0:T(8,128)S(1)}, f32[19,8,128]{2,1,0:T(8,128)S(1)}, u32[]{:S(2)}, u32[]{:S(2)}) collective-permute-start(f32[19,8,128]{2,1,0:T(8,128)S(1)} %get-tuple-element.21), channel_id=1, source_target_pairs={{0,4},{4,0},{8,12},{12,8},{16,20},{20,16},{24,28},{28,24},{1,5},{5... | collective-permute-start | bytes 233480 | tf_op jit(solution)/shard_map/ppermute | solution.py:403
  12.6 5.4 %collective-permute-start.3 = (f32[19,8,128]{2,1,0:T(8,128)S(1)}, f32[19,8,128]{2,1,0:T(8,128)S(1)}, u32[]{:S(2)}, u32[]{:S(2)}) collective-permute-start(f32[19,8,128]{2,1,0:T(8,128)S(1)} %add_add_fusion.refs_0_), channel_id=1, source_target_pairs={{0,16},{4,20},{8,24},{12,28},{16,0},{20,4},{24,8},{28,12},{1,17},{... | collective-permute-start | bytes 233480 | tf_op jit(solution)/shard_map/ppermute | solution.py:403
  18.1 5.4 %collective-permute-start.6 = (f32[20,8,128]{2,1,0:T(8,128)S(1)}, f32[20,8,128]{2,1,0:T(8,128)S(1)}, u32[]{:S(2)}, u32[]{:S(2)}) collective-permute-start(f32[20,8,128]{2,1,0:T(8,128)S(1)} %add_with_gram.1.rest_0_.refs_0_), channel_id=1, source_target_pairs={{0,12},{4,8},{8,4},{12,0},{16,28},{20,24},{24,20},{28,16},{1,13},{... | collective-permute-start | bytes 245768 | tf_op jit(solution)/shard_map/ppermute | solution.py:403
  20.0 4.4 %collective-permute-start.5 = (f32[20,8,128]{2,1,0:T(8,128)S(1)}, f32[20,8,128]{2,1,0:T(8,128)S(1)}, u32[]{:S(2)}, u32[]{:S(2)}) collective-permute-start(f32[20,8,128]{2,1,0:T(8,128)S(1)} %add_with_gram.1.rest_0_.refs_0_), channel_id=1, source_target_pairs={{0,8},{4,12},{8,0},{12,4},{16,24},{20,28},{24,16},{28,20},{1,9},{5... | collective-permute-start | bytes 245768 | tf_op jit(solution)/shard_map/ppermute | solution.py:403
  20.6 4.4 %collective-permute-start.4 = (f32[20,8,128]{2,1,0:T(8,128)S(1)}, f32[20,8,128]{2,1,0:T(8,128)S(1)}, u32[]{:S(2)}, u32[]{:S(2)}) collective-permute-start(f32[20,8,128]{2,1,0:T(8,128)S(1)} %add_with_gram.1.rest_0_.refs_0_), channel_id=1, source_target_pairs={{0,4},{4,0},{8,12},{12,8},{16,20},{20,16},{24,28},{28,24},{1,5},{5... | collective-permute-start | bytes 245768 | tf_op jit(solution)/shard_map/ppermute | solution.py:403
  25.5 2.5 %collective-permute-start.7 = (f32[17,8,128]{2,1,0:T(8,128)S(1)}, f32[17,8,128]{2,1,0:T(8,128)S(1)}, u32[]{:S(2)}, u32[]{:S(2)}) collective-permute-start(f32[17,8,128]{2,1,0:T(8,128)S(1)} %get-tuple-element.27), channel_id=1, source_target_pairs={{0,1},{1,0},{2,3},{3,2},{4,5},{5,4},{6,7},{7,6},{8,9},{9,8},{10,11... | collective-permute-start | bytes 208904 | tf_op jit(solution)/shard_map/ppermute | solution.py:403
  25.6 4.7 %collective-permute-start.8 = (f32[17,8,128]{2,1,0:T(8,128)S(1)}, f32[17,8,128]{2,1,0:T(8,128)S(1)}, u32[]{:S(2)}, u32[]{:S(2)}) collective-permute-start(f32[17,8,128]{2,1,0:T(8,128)S(1)} %get-tuple-element.28), channel_id=1, source_target_pairs={{0,2},{1,3},{2,0},{3,1},{4,6},{5,7},{6,4},{7,5},{8,10},{9,11},{10,... | collective-permute-start | bytes 208904 | tf_op jit(solution)/shard_map/ppermute | solution.py:403
  27.1 4.3 %collective-permute-start.9 = (f32[17,8,128]{2,1,0:T(8,128)S(1)}, f32[17,8,128]{2,1,0:T(8,128)S(1)}, u32[]{:S(2)}, u32[]{:S(2)}) collective-permute-start(f32[17,8,128]{2,1,0:T(8,128)S(1)} %get-tuple-element.29), channel_id=1, source_target_pairs={{0,3},{1,2},{2,1},{3,0},{4,7},{5,6},{6,5},{7,4},{8,11},{9,10},{10,... | collective-permute-start | bytes 208904 | tf_op jit(solution)/shard_map/ppermute | solution.py:403

commit v7 on v6

--- a/solution.py
+++ b/solution.py
@@ -174,35 +174,20 @@
     )(pltpu.with_memory_space_constraint(blocks, pltpu.HBM), *from_vmem(lhs))
 
 
-def gram_kernel(plan, *refs):
-    ins, out_ref = refs[:-1], refs[-1]
+def gram_terms(plan, ins):
     row = row_of()
     lane = lane_of()
     sums = [jnp.zeros((8, LANES), jnp.float32) for _ in range(3)]
-    for t in range(plan.quarter):
-        x = ins[0][t]
-        for other in ins[1:]:
-            x = x + other[t]
-        out_ref[t] = x
-        for d in range(3):
-            y = x if d == 0 else jnp.where(row % 4 + d < 4, roll(x, -d, 0), roll(x, 4 - d, 0))
-            sums[d] = sums[d] + x * y
+    for in_ref in ins:
+        for t in range(plan.quarter):
+            x = in_ref[t]
+            for d in range(3):
+                y = x if d == 0 else jnp.where(row % 4 + d < 4, roll(x, -d, 0), roll(x, 4 - d, 0))
+                sums[d] = sums[d] + x * y
     packed = jnp.zeros((8, LANES), jnp.float32)
     for d in range(3):
         packed = jnp.where(lane == d, jnp.sum(sums[d], axis=1, keepdims=True), packed)
-    out_ref[plan.quarter] = packed
-
-
-def add_with_gram(plan, *pieces):
-    vmem = pl.BlockSpec(memory_space=pltpu.VMEM)
-    return pl.pallas_call(
-        functools.partial(gram_kernel, plan),
-        out_shape=in_vmem((plan.quarter + 1, 8, LANES), jnp.float32),
-        in_specs=[vmem] * len(pieces),
-        out_specs=vmem,
-        compiler_params=params(16),
-        name="add_with_gram",
-    )(*from_vmem(*pieces))
+    return packed
 
 
 def adjoint_kernel(plan, distances, follows, last, *refs):
@@ -246,7 +231,7 @@
             return 0
 
         lax.fori_loop(0, plan.quarter, body, 0, unroll=True)
-    packed = sum(ref[plan.quarter] for ref in ins)
+    packed = gram_terms(plan, ins)
     if follows:
         packed = packed + earlier[plan.lines]
     if not last:
@@ -417,7 +402,7 @@
         total = total + trade(total, "param", param, span)
         span *= 2
     sums = [total] + ([trade(total, "param", param, span)] if span < param else [])
-    own = add_with_gram(plan, *sums)
+    own = sum(sums)
     pieces = [own] + [trade(own, "param", param, k) for k in range(1, QUAD)]
     adjoint = adjoint_terms(plan, (0,), pieces, kept)
     adjoint = adjoint_terms(plan, GATHER[:-1], pieces, kept, adjoint)

time: 32.6 us -> 32.5 us (level)
  no operation moved by 1% of the time
where the time goes in v7:
time: 32.5 us; the launch traced here: 32.4 us
  starting transfers between devices  12.8 us (39%)
  waiting for transfers between devices  10.9 us (34%)
  Pallas kernels  7.93 us (24%)
  between operations  0.69 us (2%)
    ppermute x10, starting transfers between devices, trade(): return lax.ppermute(x, axis, [(i, i ^ k) for i in range(size)])  12.8 us
    ppermute x10, waiting for transfers between devices, trade(): return lax.ppermute(x, axis, [(i, i ^ k) for i in range(size)])  10.9 us
    pallas_call x1, Pallas kernels, sketch_terms(): pl.pallas_call(functools.partial(sent_kernel, plan), out_shape=[piece] *...  3.03 us
    pallas_call x1, Pallas kernels, own_terms(): pl.pallas_call(functools.partial(own_kernel, plan), out_shape=[in_vmem((p...  1.82 us
    pallas_call x3, Pallas kernels, adjoint_terms(): pl.pallas_call(functools.partial(adjoint_kernel, plan, distances, earlier...  1.45 us
    pallas_call x1, Pallas kernels, finish(): pl.pallas_call(functools.partial(final_kernel, plan), out_shape=[jax.Shap...  1.07 us
  transfers between devices with their start and end apart: 10, of which 8 were waited for; matrix products, arithmetic and copies ran while one was open for 0% of the time, Pallas kernels for 10%

profile of v7, /device:TPU:0, one launch (start us, length us, event | category | flops | bytes accessed | tf_op | source)
XLA Modules:
  0.0 32.4 jit_solution(420503436540638188)
XLA Ops:
  0.6 3.0 %sent_terms.1 = (f32[19,8,128]{2,1,0:T(8,128)S(1)}, f32[19,8,128]{2,1,0:T(8,128)S(1)}, f32[19,8,128]{2,1,0:T(8,128)S(1)}, bf16[4864,128]{1,0:T(8,128)(2,1)S(1)},...) custom-call(bf16[19200,128]{1,0:T(8,128)(2,1)} %bitcast.5, ...), custom_call_target="tpu_custom_call" | custom-call | tf_op jit(solution)/shard_map/sent_terms/pallas_call | solution.py:145
  3.7 4.1 %collective-permute-start = (f32[19,8,128]{2,1,0:T(8,128)S(1)}, f32[19,8,128]{2,1,0:T(8,128)S(1)}, u32[]{:S(2)}, u32[]{:S(2)}) collective-permute-start(f32[19,8,128]{2,1,0:T(8,128)S(1)} %get-tuple-element.19), channel_id=1, source_target_pairs={{0,12},{4,8},{8,4},{12,0},{16,28},{20,24},{24,20},{28,16},{1,13},{... | collective-permute-start | bytes 233480 | tf_op jit(solution)/shard_map/ppermute | solution.py:388
  7.7 0.4 %collective-permute-start.1 = (f32[19,8,128]{2,1,0:T(8,128)S(1)}, f32[19,8,128]{2,1,0:T(8,128)S(1)}, u32[]{:S(2)}, u32[]{:S(2)}) collective-permute-start(f32[19,8,128]{2,1,0:T(8,128)S(1)} %get-tuple-element.20), channel_id=1, source_target_pairs={{0,8},{4,12},{8,0},{12,4},{16,24},{20,28},{24,16},{28,20},{1,9},{5... | collective-permute-start | bytes 233480 | tf_op jit(solution)/shard_map/ppermute | solution.py:388
  8.2 0.2 collective-permute-start.2
  8.4 1.8 %own_terms.1 = (f32[19,8,128]{2,1,0:T(8,128)S(1)}, bf16[4864,128]{1,0:T(8,128)(2,1)S(1)}) custom-call(bf16[19200,128]{1,0:T(8,128)(2,1)} %bitcast.6, f32[520,128]{1,0:T(8,128)S(1)} %get-tuple-element.17.lhs_ref), custom_call_target="tpu_custom_call" | custom-call | tf_op jit(solution)/shard_map/own_terms/pallas_call | solution.py:163
  10.2 0.2 collective-permute-done
  10.4 1.8 %collective-permute-done.1 = f32[19,8,128]{2,1,0:T(8,128)S(1)} collective-permute-done((f32[19,8,128]{2,1,0:T(8,128)S(1)}, f32[19,8,128]{2,1,0:T(8,128)S(1)}, u32[]{:S(2)}, u32[]{:S(2)}) %collective-permute-start.1) | collective-permute-done | bytes 77856 | tf_op jit(solution)/shard_map/ppermute | solution.py:388
  12.2 0.4 %collective-permute-done.2 = f32[19,8,128]{2,1,0:T(8,128)S(1)} collective-permute-done((f32[19,8,128]{2,1,0:T(8,128)S(1)}, f32[19,8,128]{2,1,0:T(8,128)S(1)}, u32[]{:S(2)}, u32[]{:S(2)}) %collective-permute-start.2) | collective-permute-done | bytes 77856 | tf_op jit(solution)/shard_map/ppermute | solution.py:388
  12.6 2.7 %collective-permute-start.3 = (f32[19,8,128]{2,1,0:T(8,128)S(1)}, f32[19,8,128]{2,1,0:T(8,128)S(1)}, u32[]{:S(2)}, u32[]{:S(2)}) collective-permute-start(f32[19,8,128]{2,1,0:T(8,128)S(1)} %add_add_fusion), channel_id=1, source_target_pairs={{0,16},{4,20},{8,24},{12,28},{16,0},{20,4},{24,8},{28,12},{1,17},{... | collective-permute-start | bytes 233480 | tf_op jit(solution)/shard_map/ppermute | solution.py:388
  15.3 2.7 %collective-permute-done.3 = f32[19,8,128]{2,1,0:T(8,128)S(1)} collective-permute-done((f32[19,8,128]{2,1,0:T(8,128)S(1)}, f32[19,8,128]{2,1,0:T(8,128)S(1)}, u32[]{:S(2)}, u32[]{:S(2)}) %collective-permute-start.3) | collective-permute-done | bytes 77856 | tf_op jit(solution)/shard_map/ppermute | solution.py:388
  18.0 1.9 %collective-permute-start.6 = (f32[19,8,128]{2,1,0:T(8,128)S(1)}, f32[19,8,128]{2,1,0:T(8,128)S(1)}, u32[]{:S(2)}, u32[]{:S(2)}) collective-permute-start(f32[19,8,128]{2,1,0:T(8,128)S(1)} %add.15.rest_0_.refs_0_), channel_id=1, source_target_pairs={{0,12},{4,8},{8,4},{12,0},{16,28},{20,24},{24,20},{28,16},{1,13},{... | collective-permute-start | bytes 233480 | tf_op jit(solution)/shard_map/ppermute | solution.py:388
  19.9 0.6 %collective-permute-start.5 = (f32[19,8,128]{2,1,0:T(8,128)S(1)}, f32[19,8,128]{2,1,0:T(8,128)S(1)}, u32[]{:S(2)}, u32[]{:S(2)}) collective-permute-start(f32[19,8,128]{2,1,0:T(8,128)S(1)} %add.15.rest_0_.refs_0_), channel_id=1, source_target_pairs={{0,8},{4,12},{8,0},{12,4},{16,24},{20,28},{24,16},{28,20},{1,9},{5... | collective-permute-start | bytes 233480 | tf_op jit(solution)/shard_map/ppermute | solution.py:388
  20.5 1.0 %collective-permute-start.4 = (f32[19,8,128]{2,1,0:T(8,128)S(1)}, f32[19,8,128]{2,1,0:T(8,128)S(1)}, u32[]{:S(2)}, u32[]{:S(2)}) collective-permute-start(f32[19,8,128]{2,1,0:T(8,128)S(1)} %add.15.rest_0_.refs_0_), channel_id=1, source_target_pairs={{0,4},{4,0},{8,12},{12,8},{16,20},{20,16},{24,28},{28,24},{1,5},{5... | collective-permute-start | bytes 233480 | tf_op jit(solution)/shard_map/ppermute | solution.py:388
  21.5 0.4 %adjoint_part.2.refs_4_ = f32[65,8,128]{2,1,0:T(8,128)S(1)} custom-call(f32[19,8,128]{2,1,0:T(8,128)S(1)} %add.15.rest_0_.refs_0_, bf16[4864,128]{1,0:T(8,128)(2,1)S(1)} %get-tuple-element.25.refs_1_), custom_call_target="tpu_custom_call" | custom-call | tf_op jit(solution)/shard_map/adjoint_part/pallas_call | solution.py:254
  21.9 1.5 %collective-permute-done.6.rest_3_.refs_0_ = f32[19,8,128]{2,1,0:T(8,128)S(1)} collective-permute-done((f32[19,8,128]{2,1,0:T(8,128)S(1)}, f32[19,8,128]{2,1,0:T(8,128)S(1)}, u32[]{:S(2)}, u32[]{:S(2)}) %collective-permute-start.6) | collective-permute-done | bytes 77856 | tf_op jit(solution)/shard_map/ppermute | solution.py:388
  23.5 0.9 %collective-permute-done.5.rest_2_.refs_1_ = f32[19,8,128]{2,1,0:T(8,128)S(1)} collective-permute-done((f32[19,8,128]{2,1,0:T(8,128)S(1)}, f32[19,8,128]{2,1,0:T(8,128)S(1)}, u32[]{:S(2)}, u32[]{:S(2)}) %collective-permute-start.5) | collective-permute-done | bytes 77856 | tf_op jit(solution)/shard_map/ppermute | solution.py:388
  24.3 0.6 %adjoint_part.3.refs_2_ = f32[65,8,128]{2,1,0:T(8,128)S(1)} custom-call(f32[19,8,128]{2,1,0:T(8,128)S(1)} %collective-permute-done.6.rest_3_.refs_0_, f32[19,8,128]{2,1,0:T(8,128)S(1)} %collective-permute-done.5.rest_2_.refs_1_, bf16[4864,128]{1,0:T(8,128)(2,1)S(1)} %get-tuple-element.23.refs_2_, bf16[4864,128]{1,0:T(8,128)(2,1)S(1)} %get-tuple-element.24.refs_3_, ...), custom_call_target="tpu_custom_call" | custom-call | tf_op jit(solution)/shard_map/adjoint_part/pallas_call | solution.py:254
  24.9 0.4 %adjoint_last.1 = (f32[17,8,128]{2,1,0:T(8,128)S(1)}, f32[17,8,128]{2,1,0:T(8,128)S(1)}, f32[17,8,128]{2,1,0:T(8,128)S(1)}, f32[17,8,128]{2,1,0:T(8,128)S(1)}) custom-call(f32[19,8,128]{2,1,0:T(8,128)S(1)} %collective-permute-done.4.rest_1_.refs_0_, bf16[4864,128]{1,0:T(8,128)(2,1)S(1)} %get-tuple-element.22.refs_1_, f32[65,8,128]{2,1,0:T(8,128)S(1)} %adjoint_part.3.refs_2_), custom_call_target="tpu_custom_call" | custom-call | tf_op jit(solution)/shard_map/adjoint_last/pallas_call | solution.py:254
  25.5 1.5 %collective-permute-start.8 = (f32[17,8,128]{2,1,0:T(8,128)S(1)}, f32[17,8,128]{2,1,0:T(8,128)S(1)}, u32[]{:S(2)}, u32[]{:S(2)}) collective-permute-start(f32[17,8,128]{2,1,0:T(8,128)S(1)} %get-tuple-element.28), channel_id=1, source_target_pairs={{0,2},{1,3},{2,0},{3,1},{4,6},{5,7},{6,4},{7,5},{8,10},{9,11},{10,... | collective-permute-start | bytes 208904 | tf_op jit(solution)/shard_map/ppermute | solution.py:388
  27.0 0.3 %collective-permute-start.9 = (f32[17,8,128]{2,1,0:T(8,128)S(1)}, f32[17,8,128]{2,1,0:T(8,128)S(1)}, u32[]{:S(2)}, u32[]{:S(2)}) collective-permute-start(f32[17,8,128]{2,1,0:T(8,128)S(1)} %get-tuple-element.29), channel_id=1, source_target_pairs={{0,3},{1,2},{2,1},{3,0},{4,7},{5,6},{6,5},{7,4},{8,11},{9,10},{10,... | collective-permute-start | bytes 208904 | tf_op jit(solution)/shard_map/ppermute | solution.py:388
  27.3 0.6 %sketch_by_line.1.sketch_ref = f32[64,8,150]{2,1,0:T(8,128)S(1)} custom-call(f32[19,8,128]{2,1,0:T(8,128)S(1)} %add.15.rest_0_.refs_0_, f32[19,8,128]{2,1,0:T(8,128)S(1)} %collective-permute-done.4.rest_1_.refs_0_, f32[19,8,128]{2,1,0:T(8,128)S(1)} %collective-permute-done.5.rest_2_.refs_1_, f32[19,8,128]{2,1,0:T(8,128)S(1)} %collective-permute-done.6.rest_3_.refs_0_), custom_call_target="tpu_custom_call" | custom-call | tf_op jit(solution)/shard_map/sketch_by_line/pallas_call | solution.py:289
  27.9 2.2 %collective-permute-done.8.rest_2_ = f32[17,8,128]{2,1,0:T(8,128)S(1)} collective-permute-done((f32[17,8,128]{2,1,0:T(8,128)S(1)}, f32[17,8,128]{2,1,0:T(8,128)S(1)}, u32[]{:S(2)}, u32[]{:S(2)}) %collective-permute-start.8) | collective-permute-done | bytes 69664 | tf_op jit(solution)/shard_map/ppermute | solution.py:388
  30.1 1.2 %collective-permute-done.9.rest_3_ = f32[17,8,128]{2,1,0:T(8,128)S(1)} collective-permute-done((f32[17,8,128]{2,1,0:T(8,128)S(1)}, f32[17,8,128]{2,1,0:T(8,128)S(1)}, u32[]{:S(2)}, u32[]{:S(2)}) %collective-permute-start.9) | collective-permute-done | bytes 69664 | tf_op jit(solution)/shard_map/ppermute | solution.py:388
  31.3 1.1 %finish.1 = (f32[64,2,4,150]{3,2,1,0:T(4,128)}, bf16[128,128]{1,0:T(8,128)(2,1)}) custom-call(f32[64,8,150]{2,1,0:T(8,128)S(1)} %sketch_by_line.1.sketch_ref, f32[17,8,128]{2,1,0:T(8,128)S(1)} %get-tuple-element.26.rest_0_, f32[17,8,128]{2,1,0:T(8,128)S(1)} %collective-permute-done.7.rest_1_, f32[17,8,128]{2,1,0:T(8,128)S(1)} %collective-permute-done.8.rest_2_, ...), custom_call_target="tpu_custom_call" | custom-call | tf_op jit(solution)/shard_map/finish/pallas_call | solution.py:372
  (5 shorter events, 0.1 us)
Async XLA Ops:
  3.7 6.7 %collective-permute-start = (f32[19,8,128]{2,1,0:T(8,128)S(1)}, f32[19,8,128]{2,1,0:T(8,128)S(1)}, u32[]{:S(2)}, u32[]{:S(2)}) collective-permute-start(f32[19,8,128]{2,1,0:T(8,128)S(1)} %get-tuple-element.19), channel_id=1, source_target_pairs={{0,12},{4,8},{8,4},{12,0},{16,28},{20,24},{24,20},{28,16},{1,13},{... | collective-permute-start | bytes 233480 | tf_op jit(solution)/shard_map/ppermute | solution.py:388
  7.7 4.5 %collective-permute-start.1 = (f32[19,8,128]{2,1,0:T(8,128)S(1)}, f32[19,8,128]{2,1,0:T(8,128)S(1)}, u32[]{:S(2)}, u32[]{:S(2)}) collective-permute-start(f32[19,8,128]{2,1,0:T(8,128)S(1)} %get-tuple-element.20), channel_id=1, source_target_pairs={{0,8},{4,12},{8,0},{12,4},{16,24},{20,28},{24,16},{28,20},{1,9},{5... | collective-permute-start | bytes 233480 | tf_op jit(solution)/shard_map/ppermute | solution.py:388
  8.2 4.4 %collective-permute-start.2 = (f32[19,8,128]{2,1,0:T(8,128)S(1)}, f32[19,8,128]{2,1,0:T(8,128)S(1)}, u32[]{:S(2)}, u32[]{:S(2)}) collective-permute-start(f32[19,8,128]{2,1,0:T(8,128)S(1)} %get-tuple-element.21), channel_id=1, source_target_pairs={{0,4},{4,0},{8,12},{12,8},{16,20},{20,16},{24,28},{28,24},{1,5},{5... | collective-permute-start | bytes 233480 | tf_op jit(solution)/shard_map/ppermute | solution.py:388
  12.6 5.4 %collective-permute-start.3 = (f32[19,8,128]{2,1,0:T(8,128)S(1)}, f32[19,8,128]{2,1,0:T(8,128)S(1)}, u32[]{:S(2)}, u32[]{:S(2)}) collective-permute-start(f32[19,8,128]{2,1,0:T(8,128)S(1)} %add_add_fusion), channel_id=1, source_target_pairs={{0,16},{4,20},{8,24},{12,28},{16,0},{20,4},{24,8},{28,12},{1,17},{... | collective-permute-start | bytes 233480 | tf_op jit(solution)/shard_map/ppermute | solution.py:388
  18.0 5.5 %collective-permute-start.6 = (f32[19,8,128]{2,1,0:T(8,128)S(1)}, f32[19,8,128]{2,1,0:T(8,128)S(1)}, u32[]{:S(2)}, u32[]{:S(2)}) collective-permute-start(f32[19,8,128]{2,1,0:T(8,128)S(1)} %add.15.rest_0_.refs_0_), channel_id=1, source_target_pairs={{0,12},{4,8},{8,4},{12,0},{16,28},{20,24},{24,20},{28,16},{1,13},{... | collective-permute-start | bytes 233480 | tf_op jit(solution)/shard_map/ppermute | solution.py:388
  19.9 4.4 %collective-permute-start.5 = (f32[19,8,128]{2,1,0:T(8,128)S(1)}, f32[19,8,128]{2,1,0:T(8,128)S(1)}, u32[]{:S(2)}, u32[]{:S(2)}) collective-permute-start(f32[19,8,128]{2,1,0:T(8,128)S(1)} %add.15.rest_0_.refs_0_), channel_id=1, source_target_pairs={{0,8},{4,12},{8,0},{12,4},{16,24},{20,28},{24,16},{28,20},{1,9},{5... | collective-permute-start | bytes 233480 | tf_op jit(solution)/shard_map/ppermute | solution.py:388
  20.5 4.4 %collective-permute-start.4 = (f32[19,8,128]{2,1,0:T(8,128)S(1)}, f32[19,8,128]{2,1,0:T(8,128)S(1)}, u32[]{:S(2)}, u32[]{:S(2)}) collective-permute-start(f32[19,8,128]{2,1,0:T(8,128)S(1)} %add.15.rest_0_.refs_0_), channel_id=1, source_target_pairs={{0,4},{4,0},{8,12},{12,8},{16,20},{20,16},{24,28},{28,24},{1,5},{5... | collective-permute-start | bytes 233480 | tf_op jit(solution)/shard_map/ppermute | solution.py:388
  25.4 2.5 %collective-permute-start.7 = (f32[17,8,128]{2,1,0:T(8,128)S(1)}, f32[17,8,128]{2,1,0:T(8,128)S(1)}, u32[]{:S(2)}, u32[]{:S(2)}) collective-permute-start(f32[17,8,128]{2,1,0:T(8,128)S(1)} %get-tuple-element.27), channel_id=1, source_target_pairs={{0,1},{1,0},{2,3},{3,2},{4,5},{5,4},{6,7},{7,6},{8,9},{9,8},{10,11... | collective-permute-start | bytes 208904 | tf_op jit(solution)/shard_map/ppermute | solution.py:388
  25.5 4.7 %collective-permute-start.8 = (f32[17,8,128]{2,1,0:T(8,128)S(1)}, f32[17,8,128]{2,1,0:T(8,128)S(1)}, u32[]{:S(2)}, u32[]{:S(2)}) collective-permute-start(f32[17,8,128]{2,1,0:T(8,128)S(1)} %get-tuple-element.28), channel_id=1, source_target_pairs={{0,2},{1,3},{2,0},{3,1},{4,6},{5,7},{6,4},{7,5},{8,10},{9,11},{10,... | collective-permute-start | bytes 208904 | tf_op jit(solution)/shard_map/ppermute | solution.py:388
  27.0 4.3 %collective-permute-start.9 = (f32[17,8,128]{2,1,0:T(8,128)S(1)}, f32[17,8,128]{2,1,0:T(8,128)S(1)}, u32[]{:S(2)}, u32[]{:S(2)}) collective-permute-start(f32[17,8,128]{2,1,0:T(8,128)S(1)} %get-tuple-element.29), channel_id=1, source_target_pairs={{0,3},{1,2},{2,1},{3,0},{4,7},{5,6},{6,5},{7,4},{8,11},{9,10},{10,... | collective-permute-start | bytes 208904 | tf_op jit(solution)/shard_map/ppermute | solution.py:388

commit v8 on v7

--- a/solution.py
+++ b/solution.py
@@ -12,10 +12,10 @@
 STEP = 2 * LANES
 QUAD = 4
 PROBES = 4
-ARRIVALS = ((3,), (2,), (1,))
+ARRIVALS = ((3,), (2, 1))
 REDUCE, GATHER = (3, 2, 1), (3, 2, 1)
 URGENCY = (0, 1, 1)
-PIECES = 8
+PIECES = 2
 SPLITS = 3
 
 
@@ -405,7 +405,8 @@
     own = sum(sums)
     pieces = [own] + [trade(own, "param", param, k) for k in range(1, QUAD)]
     adjoint = adjoint_terms(plan, (0,), pieces, kept)
-    adjoint = adjoint_terms(plan, GATHER[:-1], pieces, kept, adjoint)
+    adjoint = adjoint_terms(plan, GATHER[:1], pieces, kept, adjoint)
+    adjoint = adjoint_terms(plan, GATHER[1:-1], pieces, kept, adjoint)
     adjoint = adjoint_terms(plan, GATHER[-1:], pieces, kept, adjoint, True)
     gathered = [adjoint[0]] + [trade(adjoint[k], "sensor", sensor, k) for k in range(1, sensor)]
     sketch = sketch_by_line(plan, pieces)

time: 32.5 us -> 32.5 us (level)
    pallas_call x3 -> x4, Pallas kernels: 1.45 us -> 1.65 us  [adjoint_terms(): pl.pallas_call(functools.partial(adjoint_kernel, plan, distances, earlier...]
  transfers between devices with their start and end apart: 10 -> 10, of which waited for: 8 -> 9; matrix products, arithmetic and copies ran while one was open for 0% -> 0% of each run, Pallas kernels for 10% -> 11%
where the time goes in v8:
time: 32.5 us; the launch traced here: 32.3 us
  starting transfers between devices  12.8 us (39%)
  waiting for transfers between devices  10.7 us (33%)
  Pallas kernels  8.11 us (25%)
  between operations  0.69 us (2%)
    ppermute x10, starting transfers between devices, trade(): return lax.ppermute(x, axis, [(i, i ^ k) for i in range(size)])  12.8 us
    ppermute x10, waiting for transfers between devices, trade(): return lax.ppermute(x, axis, [(i, i ^ k) for i in range(size)])  10.7 us
    pallas_call x1, Pallas kernels, sketch_terms(): pl.pallas_call(functools.partial(sent_kernel, plan), out_shape=[piece] *...  3.01 us
    pallas_call x1, Pallas kernels, own_terms(): pl.pallas_call(functools.partial(own_kernel, plan), out_shape=[in_vmem((p...  1.82 us
    pallas_call x4, Pallas kernels, adjoint_terms(): pl.pallas_call(functools.partial(adjoint_kernel, plan, distances, earlier...  1.65 us
    pallas_call x1, Pallas kernels, finish(): pl.pallas_call(functools.partial(final_kernel, plan), out_shape=[jax.Shap...  1.07 us
  transfers between devices with their start and end apart: 10, of which 9 were waited for; matrix products, arithmetic and copies ran while one was open for 0% of the time, Pallas kernels for 11%

profile of v8, /device:TPU:0, one launch (start us, length us, event | category | flops | bytes accessed | tf_op | source)
XLA Modules:
  0.0 32.3 jit_solution(12784821996566600389)
XLA Ops:
  0.6 3.0 %sent_terms.1 = (f32[19,8,128]{2,1,0:T(8,128)S(1)}, f32[19,8,128]{2,1,0:T(8,128)S(1)}, f32[19,8,128]{2,1,0:T(8,128)S(1)}, bf16[4864,128]{1,0:T(8,128)(2,1)S(1)},...) custom-call(bf16[19200,128]{1,0:T(8,128)(2,1)} %bitcast.5, ...), custom_call_target="tpu_custom_call" | custom-call | tf_op jit(solution)/shard_map/sent_terms/pallas_call | solution.py:145
  3.6 4.1 %collective-permute-start = (f32[19,8,128]{2,1,0:T(8,128)S(1)}, f32[19,8,128]{2,1,0:T(8,128)S(1)}, u32[]{:S(2)}, u32[]{:S(2)}) collective-permute-start(f32[19,8,128]{2,1,0:T(8,128)S(1)} %get-tuple-element.19), channel_id=1, source_target_pairs={{0,12},{4,8},{8,4},{12,0},{16,28},{20,24},{24,20},{28,16},{1,13},{... | collective-permute-start | bytes 233480 | tf_op jit(solution)/shard_map/ppermute | solution.py:388
  7.7 0.4 %collective-permute-start.1 = (f32[19,8,128]{2,1,0:T(8,128)S(1)}, f32[19,8,128]{2,1,0:T(8,128)S(1)}, u32[]{:S(2)}, u32[]{:S(2)}) collective-permute-start(f32[19,8,128]{2,1,0:T(8,128)S(1)} %get-tuple-element.20), channel_id=1, source_target_pairs={{0,8},{4,12},{8,0},{12,4},{16,24},{20,28},{24,16},{28,20},{1,9},{5... | collective-permute-start | bytes 233480 | tf_op jit(solution)/shard_map/ppermute | solution.py:388
  8.4 1.8 %own_terms.1 = (f32[19,8,128]{2,1,0:T(8,128)S(1)}, bf16[4864,128]{1,0:T(8,128)(2,1)S(1)}) custom-call(bf16[19200,128]{1,0:T(8,128)(2,1)} %bitcast.6, f32[520,128]{1,0:T(8,128)S(1)} %get-tuple-element.17.lhs_ref), custom_call_target="tpu_custom_call" | custom-call | tf_op jit(solution)/shard_map/own_terms/pallas_call | solution.py:163
  10.4 1.8 %collective-permute-done.1 = f32[19,8,128]{2,1,0:T(8,128)S(1)} collective-permute-done((f32[19,8,128]{2,1,0:T(8,128)S(1)}, f32[19,8,128]{2,1,0:T(8,128)S(1)}, u32[]{:S(2)}, u32[]{:S(2)}) %collective-permute-start.1) | collective-permute-done | bytes 77856 | tf_op jit(solution)/shard_map/ppermute | solution.py:388
  12.2 0.4 %collective-permute-done.2 = f32[19,8,128]{2,1,0:T(8,128)S(1)} collective-permute-done((f32[19,8,128]{2,1,0:T(8,128)S(1)}, f32[19,8,128]{2,1,0:T(8,128)S(1)}, u32[]{:S(2)}, u32[]{:S(2)}) %collective-permute-start.2) | collective-permute-done | bytes 77856 | tf_op jit(solution)/shard_map/ppermute | solution.py:388
  12.6 2.7 %collective-permute-start.3 = (f32[19,8,128]{2,1,0:T(8,128)S(1)}, f32[19,8,128]{2,1,0:T(8,128)S(1)}, u32[]{:S(2)}, u32[]{:S(2)}) collective-permute-start(f32[19,8,128]{2,1,0:T(8,128)S(1)} %add_add_fusion), channel_id=1, source_target_pairs={{0,16},{4,20},{8,24},{12,28},{16,0},{20,4},{24,8},{28,12},{1,17},{... | collective-permute-start | bytes 233480 | tf_op jit(solution)/shard_map/ppermute | solution.py:388
  15.2 2.7 %collective-permute-done.3 = f32[19,8,128]{2,1,0:T(8,128)S(1)} collective-permute-done((f32[19,8,128]{2,1,0:T(8,128)S(1)}, f32[19,8,128]{2,1,0:T(8,128)S(1)}, u32[]{:S(2)}, u32[]{:S(2)}) %collective-permute-start.3) | collective-permute-done | bytes 77856 | tf_op jit(solution)/shard_map/ppermute | solution.py:388
  18.0 1.9 %collective-permute-start.6 = (f32[19,8,128]{2,1,0:T(8,128)S(1)}, f32[19,8,128]{2,1,0:T(8,128)S(1)}, u32[]{:S(2)}, u32[]{:S(2)}) collective-permute-start(f32[19,8,128]{2,1,0:T(8,128)S(1)} %add.15.rest_0_.refs_0_), channel_id=1, source_target_pairs={{0,12},{4,8},{8,4},{12,0},{16,28},{20,24},{24,20},{28,16},{1,13},{... | collective-permute-start | bytes 233480 | tf_op jit(solution)/shard_map/ppermute | solution.py:388
  19.9 0.6 %collective-permute-start.5 = (f32[19,8,128]{2,1,0:T(8,128)S(1)}, f32[19,8,128]{2,1,0:T(8,128)S(1)}, u32[]{:S(2)}, u32[]{:S(2)}) collective-permute-start(f32[19,8,128]{2,1,0:T(8,128)S(1)} %add.15.rest_0_.refs_0_), channel_id=1, source_target_pairs={{0,8},{4,12},{8,0},{12,4},{16,24},{20,28},{24,16},{28,20},{1,9},{5... | collective-permute-start | bytes 233480 | tf_op jit(solution)/shard_map/ppermute | solution.py:388
  20.5 1.0 %collective-permute-start.4 = (f32[19,8,128]{2,1,0:T(8,128)S(1)}, f32[19,8,128]{2,1,0:T(8,128)S(1)}, u32[]{:S(2)}, u32[]{:S(2)}) collective-permute-start(f32[19,8,128]{2,1,0:T(8,128)S(1)} %add.15.rest_0_.refs_0_), channel_id=1, source_target_pairs={{0,4},{4,0},{8,12},{12,8},{16,20},{20,16},{24,28},{28,24},{1,5},{5... | collective-permute-start | bytes 233480 | tf_op jit(solution)/shard_map/ppermute | solution.py:388
  21.5 0.4 %adjoint_part.3.refs_2_ = f32[65,8,128]{2,1,0:T(8,128)S(1)} custom-call(f32[19,8,128]{2,1,0:T(8,128)S(1)} %add.15.rest_0_.refs_0_, bf16[4864,128]{1,0:T(8,128)(2,1)S(1)} %get-tuple-element.25.refs_1_), custom_call_target="tpu_custom_call" | custom-call | tf_op jit(solution)/shard_map/adjoint_part/pallas_call | solution.py:254
  21.9 1.5 %collective-permute-done.6.rest_3_.refs_0_ = f32[19,8,128]{2,1,0:T(8,128)S(1)} collective-permute-done((f32[19,8,128]{2,1,0:T(8,128)S(1)}, f32[19,8,128]{2,1,0:T(8,128)S(1)}, u32[]{:S(2)}, u32[]{:S(2)}) %collective-permute-start.6) | collective-permute-done | bytes 77856 | tf_op jit(solution)/shard_map/ppermute | solution.py:388
  23.4 0.4 %adjoint_part.4.refs_2_ = f32[65,8,128]{2,1,0:T(8,128)S(1)} custom-call(f32[19,8,128]{2,1,0:T(8,128)S(1)} %collective-permute-done.6.rest_3_.refs_0_, bf16[4864,128]{1,0:T(8,128)(2,1)S(1)} %get-tuple-element.24.refs_1_, f32[65,8,128]{2,1,0:T(8,128)S(1)} %adjoint_part.3.refs_2_), custom_call_target="tpu_custom_call" | custom-call | tf_op jit(solution)/shard_map/adjoint_part/pallas_call | solution.py:254
  23.8 0.4 %collective-permute-done.5.rest_2_.refs_0_ = f32[19,8,128]{2,1,0:T(8,128)S(1)} collective-permute-done((f32[19,8,128]{2,1,0:T(8,128)S(1)}, f32[19,8,128]{2,1,0:T(8,128)S(1)}, u32[]{:S(2)}, u32[]{:S(2)}) %collective-permute-start.5) | collective-permute-done | bytes 77856 | tf_op jit(solution)/shard_map/ppermute | solution.py:388
  24.3 0.4 %adjoint_part.5.refs_2_ = f32[65,8,128]{2,1,0:T(8,128)S(1)} custom-call(f32[19,8,128]{2,1,0:T(8,128)S(1)} %collective-permute-done.5.rest_2_.refs_0_, bf16[4864,128]{1,0:T(8,128)(2,1)S(1)} %get-tuple-element.23.refs_1_, f32[65,8,128]{2,1,0:T(8,128)S(1)} %adjoint_part.4.refs_2_), custom_call_target="tpu_custom_call" | custom-call | tf_op jit(solution)/shard_map/adjoint_part/pallas_call | solution.py:254
  24.7 0.2 collective-permute-done.4.rest_1_.refs_0_
  24.9 0.4 %adjoint_last.1 = (f32[17,8,128]{2,1,0:T(8,128)S(1)}, f32[17,8,128]{2,1,0:T(8,128)S(1)}, f32[17,8,128]{2,1,0:T(8,128)S(1)}, f32[17,8,128]{2,1,0:T(8,128)S(1)}) custom-call(f32[19,8,128]{2,1,0:T(8,128)S(1)} %collective-permute-done.4.rest_1_.refs_0_, bf16[4864,128]{1,0:T(8,128)(2,1)S(1)} %get-tuple-element.22.refs_1_, f32[65,8,128]{2,1,0:T(8,128)S(1)} %adjoint_part.5.refs_2_), custom_call_target="tpu_custom_call" | custom-call | tf_op jit(solution)/shard_map/adjoint_last/pallas_call | solution.py:254
  25.4 1.3 %collective-permute-start.8 = (f32[17,8,128]{2,1,0:T(8,128)S(1)}, f32[17,8,128]{2,1,0:T(8,128)S(1)}, u32[]{:S(2)}, u32[]{:S(2)}) collective-permute-start(f32[17,8,128]{2,1,0:T(8,128)S(1)} %get-tuple-element.28), channel_id=1, source_target_pairs={{0,2},{1,3},{2,0},{3,1},{4,6},{5,7},{6,4},{7,5},{8,10},{9,11},{10,... | collective-permute-start | bytes 208904 | tf_op jit(solution)/shard_map/ppermute | solution.py:388
  26.8 0.5 %collective-permute-start.9 = (f32[17,8,128]{2,1,0:T(8,128)S(1)}, f32[17,8,128]{2,1,0:T(8,128)S(1)}, u32[]{:S(2)}, u32[]{:S(2)}) collective-permute-start(f32[17,8,128]{2,1,0:T(8,128)S(1)} %get-tuple-element.29), channel_id=1, source_target_pairs={{0,3},{1,2},{2,1},{3,0},{4,7},{5,6},{6,5},{7,4},{8,11},{9,10},{10,... | collective-permute-start | bytes 208904 | tf_op jit(solution)/shard_map/ppermute | solution.py:388
  27.3 0.6 %sketch_by_line.1.sketch_ref = f32[64,8,150]{2,1,0:T(8,128)S(1)} custom-call(f32[19,8,128]{2,1,0:T(8,128)S(1)} %add.15.rest_0_.refs_0_, f32[19,8,128]{2,1,0:T(8,128)S(1)} %collective-permute-done.4.rest_1_.refs_0_, f32[19,8,128]{2,1,0:T(8,128)S(1)} %collective-permute-done.5.rest_2_.refs_0_, f32[19,8,128]{2,1,0:T(8,128)S(1)} %collective-permute-done.6.rest_3_.refs_0_), custom_call_target="tpu_custom_call" | custom-call | tf_op jit(solution)/shard_map/sketch_by_line/pallas_call | solution.py:289
  27.9 2.4 %collective-permute-done.8.rest_2_ = f32[17,8,128]{2,1,0:T(8,128)S(1)} collective-permute-done((f32[17,8,128]{2,1,0:T(8,128)S(1)}, f32[17,8,128]{2,1,0:T(8,128)S(1)}, u32[]{:S(2)}, u32[]{:S(2)}) %collective-permute-start.8) | collective-permute-done | bytes 69664 | tf_op jit(solution)/shard_map/ppermute | solution.py:388
  30.3 1.0 %collective-permute-done.9.rest_3_ = f32[17,8,128]{2,1,0:T(8,128)S(1)} collective-permute-done((f32[17,8,128]{2,1,0:T(8,128)S(1)}, f32[17,8,128]{2,1,0:T(8,128)S(1)}, u32[]{:S(2)}, u32[]{:S(2)}) %collective-permute-start.9) | collective-permute-done | bytes 69664 | tf_op jit(solution)/shard_map/ppermute | solution.py:388
  31.3 1.1 %finish.1 = (f32[64,2,4,150]{3,2,1,0:T(4,128)}, bf16[128,128]{1,0:T(8,128)(2,1)}) custom-call(f32[64,8,150]{2,1,0:T(8,128)S(1)} %sketch_by_line.1.sketch_ref, f32[17,8,128]{2,1,0:T(8,128)S(1)} %get-tuple-element.26.rest_0_, f32[17,8,128]{2,1,0:T(8,128)S(1)} %collective-permute-done.7.rest_1_, f32[17,8,128]{2,1,0:T(8,128)S(1)} %collective-permute-done.8.rest_2_, ...), custom_call_target="tpu_custom_call" | custom-call | tf_op jit(solution)/shard_map/finish/pallas_call | solution.py:372
  (6 shorter events, 0.5 us)
Async XLA Ops:
  3.6 6.7 %collective-permute-start = (f32[19,8,128]{2,1,0:T(8,128)S(1)}, f32[19,8,128]{2,1,0:T(8,128)S(1)}, u32[]{:S(2)}, u32[]{:S(2)}) collective-permute-start(f32[19,8,128]{2,1,0:T(8,128)S(1)} %get-tuple-element.19), channel_id=1, source_target_pairs={{0,12},{4,8},{8,4},{12,0},{16,28},{20,24},{24,20},{28,16},{1,13},{... | collective-permute-start | bytes 233480 | tf_op jit(solution)/shard_map/ppermute | solution.py:388
  7.7 4.5 %collective-permute-start.1 = (f32[19,8,128]{2,1,0:T(8,128)S(1)}, f32[19,8,128]{2,1,0:T(8,128)S(1)}, u32[]{:S(2)}, u32[]{:S(2)}) collective-permute-start(f32[19,8,128]{2,1,0:T(8,128)S(1)} %get-tuple-element.20), channel_id=1, source_target_pairs={{0,8},{4,12},{8,0},{12,4},{16,24},{20,28},{24,16},{28,20},{1,9},{5... | collective-permute-start | bytes 233480 | tf_op jit(solution)/shard_map/ppermute | solution.py:388
  8.2 4.4 %collective-permute-start.2 = (f32[19,8,128]{2,1,0:T(8,128)S(1)}, f32[19,8,128]{2,1,0:T(8,128)S(1)}, u32[]{:S(2)}, u32[]{:S(2)}) collective-permute-start(f32[19,8,128]{2,1,0:T(8,128)S(1)} %get-tuple-element.21), channel_id=1, source_target_pairs={{0,4},{4,0},{8,12},{12,8},{16,20},{20,16},{24,28},{28,24},{1,5},{5... | collective-permute-start | bytes 233480 | tf_op jit(solution)/shard_map/ppermute | solution.py:388
  12.6 5.4 %collective-permute-start.3 = (f32[19,8,128]{2,1,0:T(8,128)S(1)}, f32[19,8,128]{2,1,0:T(8,128)S(1)}, u32[]{:S(2)}, u32[]{:S(2)}) collective-permute-start(f32[19,8,128]{2,1,0:T(8,128)S(1)} %add_add_fusion), channel_id=1, source_target_pairs={{0,16},{4,20},{8,24},{12,28},{16,0},{20,4},{24,8},{28,12},{1,17},{... | collective-permute-start | bytes 233480 | tf_op jit(solution)/shard_map/ppermute | solution.py:388
  18.0 5.5 %collective-permute-start.6 = (f32[19,8,128]{2,1,0:T(8,128)S(1)}, f32[19,8,128]{2,1,0:T(8,128)S(1)}, u32[]{:S(2)}, u32[]{:S(2)}) collective-permute-start(f32[19,8,128]{2,1,0:T(8,128)S(1)} %add.15.rest_0_.refs_0_), channel_id=1, source_target_pairs={{0,12},{4,8},{8,4},{12,0},{16,28},{20,24},{24,20},{28,16},{1,13},{... | collective-permute-start | bytes 233480 | tf_op jit(solution)/shard_map/ppermute | solution.py:388
  19.9 4.4 %collective-permute-start.5 = (f32[19,8,128]{2,1,0:T(8,128)S(1)}, f32[19,8,128]{2,1,0:T(8,128)S(1)}, u32[]{:S(2)}, u32[]{:S(2)}) collective-permute-start(f32[19,8,128]{2,1,0:T(8,128)S(1)} %add.15.rest_0_.refs_0_), channel_id=1, source_target_pairs={{0,8},{4,12},{8,0},{12,4},{16,24},{20,28},{24,16},{28,20},{1,9},{5... | collective-permute-start | bytes 233480 | tf_op jit(solution)/shard_map/ppermute | solution.py:388
  20.5 4.4 %collective-permute-start.4 = (f32[19,8,128]{2,1,0:T(8,128)S(1)}, f32[19,8,128]{2,1,0:T(8,128)S(1)}, u32[]{:S(2)}, u32[]{:S(2)}) collective-permute-start(f32[19,8,128]{2,1,0:T(8,128)S(1)} %add.15.rest_0_.refs_0_), channel_id=1, source_target_pairs={{0,4},{4,0},{8,12},{12,8},{16,20},{20,16},{24,28},{28,24},{1,5},{5... | collective-permute-start | bytes 233480 | tf_op jit(solution)/shard_map/ppermute | solution.py:388
  25.4 2.5 %collective-permute-start.7 = (f32[17,8,128]{2,1,0:T(8,128)S(1)}, f32[17,8,128]{2,1,0:T(8,128)S(1)}, u32[]{:S(2)}, u32[]{:S(2)}) collective-permute-start(f32[17,8,128]{2,1,0:T(8,128)S(1)} %get-tuple-element.27), channel_id=1, source_target_pairs={{0,1},{1,0},{2,3},{3,2},{4,5},{5,4},{6,7},{7,6},{8,9},{9,8},{10,11... | collective-permute-start | bytes 208904 | tf_op jit(solution)/shard_map/ppermute | solution.py:388
  25.4 4.8 %collective-permute-start.8 = (f32[17,8,128]{2,1,0:T(8,128)S(1)}, f32[17,8,128]{2,1,0:T(8,128)S(1)}, u32[]{:S(2)}, u32[]{:S(2)}) collective-permute-start(f32[17,8,128]{2,1,0:T(8,128)S(1)} %get-tuple-element.28), channel_id=1, source_target_pairs={{0,2},{1,3},{2,0},{3,1},{4,6},{5,7},{6,4},{7,5},{8,10},{9,11},{10,... | collective-permute-start | bytes 208904 | tf_op jit(solution)/shard_map/ppermute | solution.py:388
  26.8 4.5 %collective-permute-start.9 = (f32[17,8,128]{2,1,0:T(8,128)S(1)}, f32[17,8,128]{2,1,0:T(8,128)S(1)}, u32[]{:S(2)}, u32[]{:S(2)}) collective-permute-start(f32[17,8,128]{2,1,0:T(8,128)S(1)} %get-tuple-element.29), channel_id=1, source_target_pairs={{0,3},{1,2},{2,1},{3,0},{4,7},{5,6},{6,5},{7,4},{8,11},{9,10},{10,... | collective-permute-start | bytes 208904 | tf_op jit(solution)/shard_map/ppermute | solution.py:388
